TPU v7x, 32 devices: a whole 2x2x4 slice. The times are simulated.
32 devices in a mesh: chain: 16 (over z, x, core), dp: 2 (over y).
Axes of the slice: x: 2, y: 2, z: 4, core: 2. Of those that a mesh axis runs over, the one named last changes fastest.
Arguments:
- segments: bfloat16 [2, 16, 128, 1024], P('dp', 'chain'), may hold values from -6 to 6
- lengths: int32 [2, 16], P('dp', 'chain'), may hold values from 64 to 128, as said below
- query_weight: bfloat16 [1024, 1024], replicated, may hold values from -0.1875 to 0.1875
- key_weight: bfloat16 [1024, 256], replicated, may hold values from -0.1875 to 0.1875
- value_weight: bfloat16 [1024, 256], replicated, may hold values from -0.1875 to 0.1875
- out_weight: bfloat16 [1024, 1024], replicated, may hold values from -0.1875 to 0.1875
- norm_gain: float32 [1024], replicated, may hold values from 0.5 to 1.5
- gate_vector: float32 [1024], replicated, may hold values from -0.6 to 0.6
- gate_bias: float32 [128], replicated, may hold values from -2 to 5
- memory_init: bfloat16 [128, 1024], replicated, may hold values from -6 to 6
- cotangent: bfloat16 [2, 16, 128, 1024], P('dp', 'chain'), may hold values from -6 to 6
Outputs:
- layer_output: bfloat16 [2, 16, 128, 1024], P('dp', 'chain')
- grad_query: float32 [1024, 1024], P(('chain', 'dp'))
- grad_key: float32 [1024, 256], P(('chain', 'dp'))
- grad_value: float32 [1024, 256], P(('chain', 'dp'))
- grad_out: float32 [1024, 1024], P(('chain', 'dp'))
- grad_gain: float32 [1024], P(('chain', 'dp'))
- grad_gate: float32 [1024], P(('chain', 'dp'))
- grad_memory: float32 [128, 1024], P(None, ('chain', 'dp'))
Inputs may be any that keep to these rules, and one draw needn't show every extreme that they name: `lengths`: in every document one segment is full.
All inputs are finite; a program needn't handle non-finite values.
Results may differ from a plain program's by a relative error of at most 0.02.
Values sent between devices are 32-bit elements; how exact they have to be, the bound alone decides.
No kernel may reach another device: no remote copies, remote signals or barrier semaphores. Data moves between devices by JAX's collectives and lax.ppermute only.
A program may use at most 128 MiB of HBM per device.

v0:
```python
import functools

import jax
import jax.numpy as jnp
from jax import lax
from jax.experimental import pallas as pl
from jax.experimental.pallas import tpu as pltpu
from jax.sharding import PartitionSpec as P


HEAD = 64
LANES = 128
epsilon = 1e-05
score_scale = 0.125
F32 = jnp.float32
BF16 = jnp.bfloat16


def mm(a, b):
    return lax.dot_general(a, b, (((1,), (0,)), ((), ())), preferred_element_type=F32)


def mm_nt(a, b):
    return lax.dot_general(a, b, (((1,), (1,)), ((), ())), preferred_element_type=F32)


def inverse_rms(rows):
    return lax.rsqrt(jnp.mean(rows * rows, axis=-1, keepdims=True) + epsilon)


def low_lanes(shape):
    return lax.broadcasted_iota(jnp.int32, shape, 1) < HEAD


def padded(tile, odd):
    wide = tile.astype(F32)
    mine = low_lanes(wide.shape) != bool(odd)
    here = jnp.where(mine, wide, 0.0)
    there = pltpu.roll(here, HEAD, 1)
    low, high = (there, here) if odd else (here, there)
    return jnp.concatenate([low, high], axis=0).astype(BF16)


def unpadded(total, odd):
    rows = total.shape[0] // 2
    low_mask = low_lanes((rows, LANES))
    low = jnp.where(low_mask, total[:rows], 0.0)
    high = jnp.where(low_mask, 0.0, total[rows:])
    return high + pltpu.roll(low, HEAD, 1) if odd else low + pltpu.roll(high, HEAD, 1)


def softmax_rows(scores, allowed):
    width = scores.shape[0] // 2
    halves = []
    for part in (scores[:width], scores[width:]):
        part = jnp.where(allowed, part, -1e30)
        raised = jnp.exp(part - jnp.max(part, axis=0, keepdims=True))
        halves.append(raised / jnp.sum(raised, axis=0, keepdims=True))
    return jnp.concatenate(halves, axis=0)


def softmax_back(weights, d_weights):
    width = weights.shape[0] // 2
    halves = []
    for at in (0, width):
        w, d = weights[at : at + width], d_weights[at : at + width]
        halves.append(w * (d - jnp.sum(w * d, axis=0, keepdims=True)))
    return jnp.concatenate(halves, axis=0)


def split3(value):
    high = value.astype(BF16)
    rest = value - high.astype(F32)
    mid = rest.astype(BF16)
    return high, mid, (rest - mid.astype(F32)).astype(BF16)


def row_times(row, matrix, transposed):
    pieces = split3(row)
    stacked = jnp.concatenate(list(pieces) + [jnp.zeros_like(pieces[0])] * 13, axis=0)
    return jnp.sum((mm_nt if transposed else mm)(stacked, matrix), axis=0, keepdims=True)


def prepare_kernel(
    length, seg, wq, wk, wv, wo, gain, vector, mem0, xn_o, q_o, kv_o, sn_o, s_o, c_o, u_o
):
    count = seg.shape[0]
    kv_width = wk.shape[1]
    rows = seg[...].astype(F32)
    start = mem0[...].astype(F32)
    g = gain[...]
    xn = (rows * inverse_rms(rows) * g).astype(BF16)
    sn = (start * inverse_rms(start) * g).astype(BF16)
    xn_o[...] = xn
    sn_o[...] = sn
    both = mm(jnp.concatenate([xn, sn], axis=0), wq[...]) * score_scale
    q_o[...] = both[:count].astype(BF16)
    s_o[...] = both[count:].astype(BF16)
    kv_o[:, :kv_width] = mm(xn, wk[...]).astype(BF16)
    kv_o[:, kv_width:] = mm(xn, wv[...]).astype(BF16)
    u_o[...] = row_times(vector[...], wo[...], True)
    slots = mem0.shape[0]
    allowed = lax.broadcasted_iota(jnp.int32, (count, slots), 0) < length[0, 0]
    pairs = s_o.shape[1] // LANES
    groups = kv_width // HEAD
    for group in range(groups):
        at, odd = (group // 2) * LANES, group % 2
        keys = padded(kv_o[:, at : at + LANES], odd)
        values_t = padded(kv_o[:, kv_width + at : kv_width + at + LANES], odd).T
        for pair in range(group * pairs // groups, (group + 1) * pairs // groups):
            lanes = slice(pair * LANES, (pair + 1) * LANES)
            weights = softmax_rows(mm_nt(keys, s_o[:, lanes]), allowed).astype(BF16)
            c_o[:, lanes] = mm(values_t, weights).T.astype(BF16).astype(F32)


def owner_kernel(
    call, bias, mem_own, u, wo, wk, wv, gain, p_o, mem_o, stat_o, mn_o, mkv_o, *, chain
):
    rows = call.shape[0]
    own = rows // chain
    logits = jnp.sum(call[...] * u[...], axis=1, keepdims=True) + bias[...]
    retain = jax.nn.sigmoid(logits)
    stat_o[0] = jnp.broadcast_to(retain, (rows, LANES))
    memory = jnp.zeros((own, call.shape[1]), F32)
    keep = jnp.ones((own, LANES), F32)
    for c in range(chain):
        at = slice(c * own, (c + 1) * own)
        p_o[at, :] = memory
        stat_o[1, at, :] = keep
        ret = stat_o[0, at, :]
        memory = ret[:, :1] * memory + (1.0 - ret[:, :1]) * call[at, :]
        keep = keep * ret
    start = jnp.concatenate([mem_own[...]] * chain, axis=0)
    mem = stat_o[1][:, :1] * start + mm(p_o[...].astype(BF16), wo[...])
    mem_o[...] = mem
    inverse = inverse_rms(mem)
    stat_o[2] = jnp.broadcast_to(inverse, (rows, LANES))
    mn = (mem * inverse * gain[...]).astype(BF16)
    mn_o[...] = mn
    width = wk.shape[1]
    mkv_o[:, :width] = mm(mn, wk[...]).astype(BF16).astype(F32)
    mkv_o[:, width:] = mm(mn, wv[...]).astype(BF16).astype(F32)


def read_kernel(
    length, seg, cot, q, kv, mkv, wo, out_o, cr_o, do_o, dq_o, dkv_o, dmkv_o, dcr_s, w_s
):
    count, width = q.shape
    slots = mkv.shape[0]
    kv_width = kv.shape[1] // 2
    pairs = width // LANES
    groups = kv_width // HEAD
    valid = lax.broadcasted_iota(jnp.int32, (count, 1), 0) < length[0, 0]
    d_out = jnp.where(valid, cot[...].astype(F32), 0.0).astype(BF16)
    do_o[...] = d_out
    dcr_s[...] = mm_nt(d_out, wo[...]).astype(BF16)
    key_at = lax.broadcasted_iota(jnp.int32, (slots + count, count), 0) - slots
    query_at = lax.broadcasted_iota(jnp.int32, (slots + count, count), 1)
    allowed = (key_at < 0) | ((key_at <= query_at) & (key_at < length[0, 0]))
    d_keys = [None] * groups
    d_values = [None] * groups
    for group in range(groups):
        at, odd = (group // 2) * LANES, group % 2
        keys = padded(
            jnp.concatenate(
                [mkv[:, at : at + LANES], kv[:, at : at + LANES].astype(F32)], axis=0
            ),
            odd,
        )
        at_v = kv_width + at
        values = padded(
            jnp.concatenate(
                [mkv[:, at_v : at_v + LANES], kv[:, at_v : at_v + LANES].astype(F32)], axis=0
            ),
            odd,
        )
        keys_t, values_t = keys.T, values.T
        dk = dv = None
        for pair in range(group * pairs // groups, (group + 1) * pairs // groups):
            lanes = slice(pair * LANES, (pair + 1) * LANES)
            q_tile = q[:, lanes]
            weights = softmax_rows(mm_nt(keys, q_tile), allowed)
            rounded = weights.astype(BF16)
            cr_o[:, lanes] = mm(values_t, rounded).T.astype(BF16)
            d_tile = dcr_s[:, lanes]
            d_weights = mm_nt(values, d_tile).astype(BF16).astype(F32)
            d_scores = softmax_back(weights, d_weights).astype(BF16)
            dq = mm(keys_t, d_scores).T.astype(BF16).astype(F32)
            dq_o[:, lanes] = (dq * score_scale).astype(BF16)
            dk_here = mm(d_scores, q_tile)
            dv_here = mm(rounded, d_tile)
            dk = dk_here if dk is None else dk + dk_here
            dv = dv_here if dv is None else dv + dv_here
        d_keys[group] = unpadded(dk, odd)
        d_values[group] = unpadded(dv, odd)
    for side, parts in ((0, d_keys), (kv_width, d_values)):
        for tile in range(groups // 2):
            lanes = slice(side + tile * LANES, side + (tile + 1) * LANES)
            total = (parts[2 * tile] + parts[2 * tile + 1]).astype(BF16).astype(F32)
            dmkv_o[:, lanes] = total[:slots]
            dkv_o[:, lanes] = total[slots:]
    out_o[...] = (seg[...].astype(F32) + mm(cr_o[...], wo[...])).astype(BF16)


def owner_back_kernel(
    dmkv, mem, p, call, stat, mem_own, u, wo, wk, wv, gain, r_o, dmb_o, dc_o, g0_o, vec_o, later_s,
    *, chain,
):
    rows, width = mem.shape
    own = rows // chain
    kv_width = wk.shape[1]
    dmb = dmkv[...].astype(BF16)
    dmb_o[...] = dmb
    dmn = mm_nt(dmb[:, :kv_width], wk[...]) + mm_nt(dmb[:, kv_width:], wv[...])
    inverse = stat[2][:, :1]
    keep = stat[1][:, :1]
    retain = stat[0][:, :1]
    memory = mem[...]
    vec_o[0:1, :] = jnp.sum(dmn * memory * inverse, axis=0, keepdims=True)
    scaled = dmn * gain[...]
    inner = jnp.sum(scaled * memory, axis=1, keepdims=True) * (1.0 / width)
    r = inverse * scaled - memory * (inverse * inverse * inverse * inner)
    r_o[...] = r.astype(BF16)
    start = jnp.concatenate([mem_own[...]] * chain, axis=0)
    q = jnp.sum(r * start, axis=1, keepdims=True)
    kept = keep * r
    g0 = kept[:own]
    for c in range(1, chain):
        g0 = g0 + kept[c * own : (c + 1) * own]
    g0_o[...] = g0
    turned = mm_nt(r.astype(BF16), wo[...])
    later = jnp.zeros((own, width), F32)
    later_q = jnp.zeros((own, 1), F32)
    q_parts = [None] * chain
    for c in reversed(range(chain)):
        at = slice(c * own, (c + 1) * own)
        later_s[at, :] = later
        q_parts[c] = later_q
        later = turned[at] + retain[at] * later
        later_q = q[at] + retain[at] * later_q
    ahead = later_s[...]
    context = call[...]
    d_retain = keep * jnp.concatenate(q_parts, axis=0) + jnp.sum(
        ahead * (p[...] - context), axis=1, keepdims=True
    )
    dz = d_retain * retain * (1.0 - retain)
    dc_o[...] = (1.0 - retain) * ahead + dz * u[...]
    v = jnp.sum(dz * context, axis=0, keepdims=True)
    vec_o[1:2, :] = v
    vec_o[2:3, :] = row_times(v, wo[...], False)


def finish_kernel(
    place, length, seg, xn, sn, s, kv, dc, dq, dkv_r, mem0, g0, wq, wk, wv, gain, vec,
    dkv_o, dqs_o, mem_o, vec_o,
):
    count, width = seg.shape
    slots = mem0.shape[0]
    kv_width = wk.shape[1]
    pairs = width // LANES
    groups = kv_width // HEAD
    allowed = lax.broadcasted_iota(jnp.int32, (count, slots), 0) < length[0, 0]
    d_keys = [None] * groups
    d_values = [None] * groups
    for group in range(groups):
        at, odd = (group // 2) * LANES, group % 2
        keys = padded(kv[:, at : at + LANES], odd)
        values = padded(kv[:, kv_width + at : kv_width + at + LANES], odd)
        keys_t = keys.T
        dk = dv = None
        for pair in range(group * pairs // groups, (group + 1) * pairs // groups):
            lanes = slice(pair * LANES, (pair + 1) * LANES)
            s_tile = s[:, lanes]
            weights = softmax_rows(mm_nt(keys, s_tile), allowed)
            d_tile = dc[:, lanes].astype(BF16)
            d_weights = mm_nt(values, d_tile).astype(BF16).astype(F32)
            d_scores = softmax_back(weights, d_weights).astype(BF16)
            dqs = mm(keys_t, d_scores).T.astype(BF16).astype(F32)
            dqs_o[:, lanes] = (dqs * score_scale).astype(BF16)
            dk_here = mm(d_scores, s_tile)
            dv_here = mm(weights.astype(BF16), d_tile)
            dk = dk_here if dk is None else dk + dk_here
            dv = dv_here if dv is None else dv + dv_here
        d_keys[group] = unpadded(dk, odd)
        d_values[group] = unpadded(dv, odd)
    for side, parts in ((0, d_keys), (kv_width, d_values)):
        for tile in range(groups // 2):
            lanes = slice(side + tile * LANES, side + (tile + 1) * LANES)
            total = (parts[2 * tile] + parts[2 * tile + 1]).astype(BF16).astype(F32)
            dkv_o[:, lanes] = (total + dkv_r[:, lanes]).astype(BF16)
    d_both = mm_nt(jnp.concatenate([dq[...], dqs_o[...]], axis=0), wq[...])
    dxn = d_both[:count] + mm_nt(dkv_o[:, :kv_width], wk[...]) + mm_nt(dkv_o[:, kv_width:], wv[...])
    dsn = d_both[count:]
    rows = seg[...].astype(F32)
    start = mem0[...].astype(F32)
    inverse = inverse_rms(start)
    gain_here = jnp.sum(dxn * (rows * inverse_rms(rows)), axis=0, keepdims=True) + jnp.sum(
        dsn * (start * inverse), axis=0, keepdims=True
    )
    vec_o[...] = jnp.zeros(vec_o.shape, F32)
    vec_o[0:1, :] = vec[0:1, :] + gain_here
    vec_o[1:3, :] = vec[1:3, :]
    scaled = dsn * gain[...]
    inner = jnp.sum(scaled * start, axis=1, keepdims=True) * (1.0 / width)
    d_start = inverse * scaled - start * (inverse * inverse * inverse * inner)
    own = g0.shape[0]
    held = jnp.concatenate([g0[...]] * (slots // own), axis=0)
    at = lax.broadcasted_iota(jnp.int32, (slots, 1), 0)
    first = place[0, 0] * own
    mem_o[...] = d_start + jnp.where((at >= first) & (at < first + own), held, 0.0)


def arranged(source, scratch, lined, me, table):
    blocks, height, _ = scratch.shape
    tall = source.shape[1]
    for b in range(blocks):
        scratch[b, :, :tall] = source[b * height : (b + 1) * height]
    for b in range(blocks):
        lined[b * height : (b + 1) * height, :tall] = scratch[me ^ table[b], :, :tall]


def product_kernel(me, *refs, plan):
    ins = refs[: plan["ins"]]
    outs = refs[plan["ins"] : plan["ins"] + 2 * len(plan["groups"])]
    scratch, lined = refs[-2:]
    half = lined.shape[0] // 2
    for index, (columns, lefts, rights, passed, table) in enumerate(plan["groups"]):
        sources = [ins[i][...].astype(F32) for i in (*lefts, *passed)]
        tokens = sum(ins[i].shape[0] for i in lefts)
        tall = sum(part.shape[0] for part in sources)
        arranged(jnp.concatenate(sources, axis=0).T, scratch, lined, me[0, 0], table)
        right = jnp.concatenate([ins[i][:, columns[0] : columns[1]] for i in rights], axis=0)
        for side, out in ((0, outs[2 * index]), (half, outs[2 * index + 1])):
            left = lined[side : side + half, :tokens].astype(BF16)
            out[:, : right.shape[1]] = mm(left, right)
            if passed:
                out[:, right.shape[1] :] = lined[side : side + half, tokens:tall]


SMEM = pl.BlockSpec(memory_space=pltpu.SMEM)
VMEM = pl.BlockSpec(memory_space=pltpu.VMEM)


def call(kernel, scalars, arrays, outs, scratch=()):
    return pl.pallas_call(
        kernel,
        out_shape=tuple(jax.ShapeDtypeStruct(shape, kind) for shape, kind in outs),
        in_specs=[SMEM] * len(scalars) + [VMEM] * len(arrays),
        out_specs=tuple([VMEM] * len(outs)),
        scratch_shapes=[pltpu.VMEM(shape, kind) for shape, kind in scratch],
    )(*scalars, *arrays)


def per_device(
    chain,
    docs,
    segments,
    lengths,
    query_weight,
    key_weight,
    value_weight,
    out_weight,
    norm_gain,
    gate_vector,
    gate_bias,
    memory_init,
    cotangent,
):
    segment, cot = segments[0, 0], cotangent[0, 0]
    count, width = segment.shape
    slots = memory_init.shape[0]
    kv2 = 2 * key_weight.shape[1]
    own = slots // chain
    devices = chain * docs
    place = lax.axis_index("chain")
    me = (place * docs + lax.axis_index("dp")).reshape(1, 1)
    gain, vector = norm_gain[None, :], gate_vector[None, :]
    bias = jnp.tile(lax.dynamic_slice(gate_bias, (place * own,), (own,)), chain)[:, None]
    mem_own = lax.dynamic_slice(memory_init, (place * own, 0), (own, width)).astype(F32)

    bits = devices.bit_length() - 1
    low = docs.bit_length() - 1
    others = list(range(low + 1, bits))
    within = list(range(low))
    order_a = [low] + within + others
    order_b = [low] + others[:1] + within + others[1:]
    order_c = [low] + others[1:] + others[:1] + within
    meet = low + 2
    cut = width * 5 // 8 // LANES * LANES
    height = width // devices

    def table_of(order):
        table = []
        for b in range(devices):
            table.append(sum(((b >> (bits - 1 - k)) & 1) << pos for k, pos in enumerate(order)))
        return tuple(table)

    def products(arrays, groups):
        outs, most, plan = [], 0, []
        for columns, lefts, rights, passed, order in groups:
            extra = sum(arrays[i].shape[0] for i in passed)
            shape = (width // 2, columns[1] - columns[0] + extra)
            outs += [(shape, F32), (shape, F32)]
            most = max(most, extra + sum(arrays[i].shape[0] for i in lefts))
            plan.append((columns, lefts, rights, passed, table_of(order)))
        return call(
            functools.partial(product_kernel, plan={"ins": len(arrays), "groups": plan}),
            [me],
            arrays,
            outs,
            [((devices, height, most), F32), ((width, most), F32)],
        )

    def swap(rows, pos):
        return lax.ppermute(rows, ("chain", "dp"), [(i, i ^ (1 << pos)) for i in range(devices)])

    def halved(total, order):
        for pos in order:
            half = total.shape[0] // 2
            total = total[:half] + swap(total[half:], pos)
        return total

    def scattered(kept, sent, order):
        return halved(kept + swap(sent, order[0]), order[1:])

    def trade(blocks):
        return lax.all_to_all(blocks, "chain", 0, 0, tiled=True)

    xn, q, kv, sn, s, c, u = call(
        prepare_kernel,
        [lengths],
        [segment, query_weight, key_weight, value_weight, out_weight, gain, vector, memory_init],
        [
            ((count, width), BF16),
            ((count, width), BF16),
            ((count, kv2), BF16),
            ((slots, width), BF16),
            ((slots, width), BF16),
            ((slots, width), F32),
            ((1, width), F32),
        ],
    )
    c_all = trade(c)
    p, mem, stat, mn, mkv = call(
        functools.partial(owner_kernel, chain=chain),
        [],
        [c_all, bias, mem_own, u, out_weight, key_weight, value_weight, gain],
        [
            ((slots, width), F32),
            ((slots, width), F32),
            ((3, slots, LANES), F32),
            ((slots, width), BF16),
            ((slots, kv2), F32),
        ],
    )
    mkv_here = trade(mkv)
    out, cr, d_out, dq, dkv_r, dmkv = call(
        read_kernel,
        [lengths],
        [segment, cot, q, kv, mkv_here, out_weight],
        [
            ((count, width), BF16),
            ((count, width), BF16),
            ((count, width), BF16),
            ((count, width), BF16),
            ((count, kv2), F32),
            ((slots, kv2), F32),
        ],
        [((count, width), BF16), ((8, LANES), F32)],
    )
    dmkv_all = trade(dmkv)
    early_a, sent_a, early_b, sent_b = products(
        [xn, dq], [((0, cut), (0,), (1,), (), order_a), ((cut, width), (0,), (1,), (), order_b)]
    )
    early_a = scattered(early_a, sent_a, order_a[:meet])
    early_b = scattered(early_b, sent_b, order_b[:meet])
    r, dmb, dc, g0, vec = call(
        functools.partial(owner_back_kernel, chain=chain),
        [],
        [dmkv_all, mem, p, c_all, stat, mem_own, u, out_weight, key_weight, value_weight, gain],
        [
            ((slots, width), BF16),
            ((slots, kv2), BF16),
            ((slots, width), F32),
            ((own, width), F32),
            ((3, width), F32),
        ],
        [((slots, width), F32)],
    )
    dc_here = trade(dc)
    out_a, sent_a, out_b, sent_b = products(
        [cr, p, d_out, r],
        [
            ((0, width // 2), (0, 1), (2, 3), (), order_a),
            ((width // 2, width), (0, 1), (2, 3), (), order_b),
        ],
    )
    out_a = scattered(out_a, sent_a, order_a[:meet])
    out_b = scattered(out_b, sent_b, order_b[:meet])
    dkv, dqs, d_mem, vec = call(
        finish_kernel,
        [place.reshape(1, 1), lengths],
        [
            segment, xn, sn, s, kv, dc_here, dq, dkv_r, memory_init, g0,
            query_weight, key_weight, value_weight, gain, vec,
        ],
        [
            ((count, kv2), BF16),
            ((slots, width), BF16),
            ((slots, width), F32),
            ((LANES, width), F32),
        ],
    )
    late_a, sent_a, late_b, sent_b, late_c, sent_c = products(
        [sn, dqs, xn, mn, dkv, dmb, d_mem, vec],
        [
            ((0, cut), (0,), (1,), (), order_a),
            ((cut, width), (0,), (1,), (6, 7), order_b),
            ((0, kv2), (2, 3), (4, 5), (), order_c),
        ],
    )
    late_a = scattered(late_a, sent_a, order_a[:meet])
    late_b = scattered(late_b, sent_b, order_b[:meet])
    g_kv = scattered(late_c, sent_c, order_c)
    right = width - cut
    joined = jnp.concatenate(
        [late_a + early_a, late_b[:, :right] + early_b, late_b[:, right:], out_a, out_b], axis=1
    )
    joined = halved(joined, order_a[meet:])
    extra = joined[:, width : width + slots + LANES]
    g_out = joined[:, width + slots + LANES :] + extra[:, slots + 1 : slots + 2] * vector
    return (
        out[None, None],
        joined[:, :width],
        g_kv[:, : kv2 // 2],
        g_kv[:, kv2 // 2 :],
        g_out,
        extra[:, slots],
        extra[:, slots + 2],
        extra[:, :slots].T,
    )


def solution(mesh):
    in_specs = (
        P("dp", "chain", None, None),
        P("dp", "chain"),
        P(),
        P(),
        P(),
        P(),
        P(),
        P(),
        P(),
        P(),
        P("dp", "chain", None, None),
    )
    out_specs = (
        P("dp", "chain", None, None),
        P(("chain", "dp"), None),
        P(("chain", "dp"), None),
        P(("chain", "dp"), None),
        P(("chain", "dp"), None),
        P(("chain", "dp")),
        P(("chain", "dp")),
        P(None, ("chain", "dp")),
    )

    def step(*args):
        return per_device(mesh.shape["chain"], mesh.shape["dp"], *args)

    return jax.shard_map(
        step, mesh=mesh, in_specs=in_specs, out_specs=out_specs, check_vma=False
    )
```

profile of v0, /device:TPU:0, one launch (start us, length us, event | category | flops | bytes accessed | tf_op | source)
XLA Modules:
  0.0 201.7 jit_solution(17907141720519875878)
XLA Ops:
  1.3 5.8 %shard_map.170 = (bf16[128,1024]{1,0:T(8,128)(2,1)}, bf16[128,1024]{1,0:T(8,128)(2,1)}, bf16[128,512]{1,0:T(8,128)(2,1)}, bf16[128,1024]{1,0:T(8,128)(2,1)}, bf1...) custom-call(s32[1,1]{1,0:T(1,128)S(6)} %copy.25.length, bf16[128,1024]{1,0:T(8,128)(2,1)} %bitcast.19, ...), custom_call_target="tpu_custom_call" | custom-call | tf_op jit(solution)/shard_map/pallas_call | solution.py:345
  7.1 7.4 %all-to-all-start = ((f32[16,8,1024]{2,1,0:T(8,128)}), f32[16,8,1024]{2,1,0:T(8,128)S(1)}, u32[]{:S(2)}, u32[]{:S(2)}) async-start(f32[16,8,1024]{2,1,0:T(8,128)} %bitcast.25), calls=%async_computation | async-start | bytes 1048576 | tf_op jit(solution)/shard_map/all_to_all | solution.py:427
  14.6 0.7 broadcast_in_dim_tile.4.bias
  15.3 1.3 dynamic-slice_convert_fusion.mem_own
  16.6 12.1 %all-to-all-done = f32[16,8,1024]{2,1,0:T(8,128)S(1)} async-done(((f32[16,8,1024]{2,1,0:T(8,128)}), f32[16,8,1024]{2,1,0:T(8,128)S(1)}, u32[]{:S(2)}, u32[]{:S(2)}) %all-to-all-start) | async-done | bytes 524320 | tf_op jit(solution)/shard_map/all_to_all | solution.py:427
  28.8 0.8 copy-done
  29.6 3.8 %shard_map.171 = (f32[128,1024]{1,0:T(8,128)}, f32[128,1024]{1,0:T(8,128)}, f32[3,128,128]{2,1,0:T(8,128)}, bf16[128,1024]{1,0:T(8,128)(2,1)}, f32[128,512]{1,0:T(8,128)}) custom-call(f32[128,1024]{1,0:T(8,128)} %bitcast.17, f32[128,1]{1,0:T(8,128)} %broadcast_in_dim_tile.4.bias, f32[8,1024]{1,0:T(8,128)} %dynamic-slice_convert_fusion.mem_own, ...), custom_call_target="tpu_custom_call" | custom-call | tf_op jit(solution)/shard_map/pallas_call | solution.py:345
  33.3 14.3 %all_to_all.44 = f32[16,8,512]{2,1,0:T(8,128)} all-to-all(f32[16,8,512]{2,1,0:T(8,128)} %bitcast.28), channel_id=1, replica_groups=mesh['chain'=16,'dp'=2] {'chain'}, dimensions={0} | all-to-all | bytes 524288 | tf_op jit(solution)/shard_map/all_to_all | solution.py:427
  47.6 6.3 %shard_map.172 = (bf16[128,1024]{1,0:T(8,128)(2,1)}, bf16[128,1024]{1,0:T(8,128)(2,1)}, bf16[128,1024]{1,0:T(8,128)(2,1)}, bf16[128,1024]{1,0:T(8,128)(2,1)}, f32[128,512]{1,0:T(8,128)}, /*index=5*/f32[128,512]{1,0:T(8,128)}) custom-call(s32[1,1]{1,0:T(1,128)S(6)} %copy.25.length, bf16[128,1024]{1,0:T(8,128)(2,1)} %bitcast.20, bf16[128,1024]{1,0:T(8,128)(2,1)} %bitcast.29, ...), custom_call_target="tpu_custom_call" | custom-call | tf_op jit(solution)/shard_map/pallas_call | solution.py:345
  53.9 3.5 %all-to-all-start.2 = ((f32[16,8,512]{2,1,0:T(8,128)}), f32[16,8,512]{2,1,0:T(8,128)S(1)}, u32[]{:S(2)}, u32[]{:S(2)}) async-start(f32[16,8,512]{2,1,0:T(8,128)} %bitcast.27), calls=%async_computation.2 | async-start | bytes 524288 | tf_op jit(solution)/shard_map/all_to_all | solution.py:427
  57.5 3.6 %shard_map.176 = (f32[512,640]{1,0:T(8,128)}, f32[512,640]{1,0:T(8,128)}, f32[512,384]{1,0:T(8,128)}, f32[512,384]{1,0:T(8,128)}) custom-call(s32[1,1]{1,0:T(1,128)} %bitcast.9.me, bf16[128,1024]{1,0:T(8,128)(2,1)} %get-tuple-element.56.xn.refs_2_.refs_0_, bf16[128,1024]{1,0:T(8,128)(2,1)} %get-tuple-element.63.dq.refs_1_), custom_call_target="tpu_custom_call" | custom-call | tf_op jit(solution)/shard_map/pallas_call | solution.py:345
  61.3 6.1 %all-to-all-done.2 = f32[16,8,512]{2,1,0:T(8,128)S(1)} async-done(((f32[16,8,512]{2,1,0:T(8,128)}), f32[16,8,512]{2,1,0:T(8,128)S(1)}, u32[]{:S(2)}, u32[]{:S(2)}) %all-to-all-start.2) | async-done | bytes 262176 | tf_op jit(solution)/shard_map/all_to_all | solution.py:427
  67.4 0.7 copy-done.8
  68.1 5.2 %shard_map.173 = (bf16[128,1024]{1,0:T(8,128)(2,1)}, bf16[128,512]{1,0:T(8,128)(2,1)}, f32[128,1024]{1,0:T(8,128)}, f32[8,1024]{1,0:T(8,128)}, f32[3,1024]{1,0:T(4,128)}) custom-call(f32[128,512]{1,0:T(8,128)} %bitcast.23, f32[128,1024]{1,0:T(8,128)} %get-tuple-element.59.mem, f32[128,1024]{1,0:T(8,128)} %get-tuple-element.60.p.refs_1_, ...), custom_call_target="tpu_custom_call" | custom-call | tf_op jit(solution)/shard_map/pallas_call | solution.py:345
  73.4 3.8 %all-to-all-start.3 = ((f32[16,8,1024]{2,1,0:T(8,128)}), f32[16,8,1024]{2,1,0:T(8,128)S(1)}, u32[]{:S(2)}, u32[]{:S(2)}) async-start(f32[16,8,1024]{2,1,0:T(8,128)} %bitcast.26), calls=%async_computation.3 | async-start | bytes 1048576 | tf_op jit(solution)/shard_map/all_to_all | solution.py:427
  77.1 4.0 %shard_map.177 = (f32[512,512]{1,0:T(8,128)}, f32[512,512]{1,0:T(8,128)}, f32[512,512]{1,0:T(8,128)}, f32[512,512]{1,0:T(8,128)}) custom-call(s32[1,1]{1,0:T(1,128)} %bitcast.9.me, bf16[128,1024]{1,0:T(8,128)(2,1)} %get-tuple-element.81.refs_0_, f32[128,1024]{1,0:T(8,128)} %get-tuple-element.60.p.refs_1_, bf16[128,1024]{1,0:T(8,128)(2,1)} %get-tuple-element.82.refs_2_, ...), custom_call_target="tpu_custom_call" | custom-call | tf_op jit(solution)/shard_map/pallas_call | solution.py:345
  81.7 9.5 %all-to-all-done.3 = f32[16,8,1024]{2,1,0:T(8,128)S(1)} async-done(((f32[16,8,1024]{2,1,0:T(8,128)}), f32[16,8,1024]{2,1,0:T(8,128)S(1)}, u32[]{:S(2)}, u32[]{:S(2)}) %all-to-all-start.3) | async-done | bytes 524320 | tf_op jit(solution)/shard_map/all_to_all | solution.py:427
  91.2 0.8 copy-done.1
  92.0 6.8 %shard_map.174 = (bf16[128,512]{1,0:T(8,128)(2,1)}, bf16[128,1024]{1,0:T(8,128)(2,1)}, f32[128,1024]{1,0:T(8,128)}, f32[128,1024]{1,0:T(8,128)}) custom-call(s32[1,1]{1,0:T(1,128)} %bitcast.10.place, s32[1,1]{1,0:T(1,128)S(6)} %copy.25.length, bf16[128,1024]{1,0:T(8,128)(2,1)} %bitcast.21, bf16[128,1024]{1,0:T(8,128)(2,1)} %get-tuple-element.56.xn.refs_2_.refs_0_, ...), custom_call_target="tpu_custom_call" | custom-call | tf_op jit(solution)/shard_map/pallas_call | solution.py:345
  98.8 5.6 %shard_map.175 = (f32[512,640]{1,0:T(8,128)}, f32[512,640]{1,0:T(8,128)}, f32[512,640]{1,0:T(8,128)}, f32[512,640]{1,0:T(8,128)}, f32[512,512]{1,0:T(8,128)}, /*index=5*/f32[512,512]{1,0:T(8,128)}) custom-call(s32[1,1]{1,0:T(1,128)} %bitcast.9.me, bf16[128,1024]{1,0:T(8,128)(2,1)} %get-tuple-element.55.sn.refs_0_, ...), custom_call_target="tpu_custom_call" | custom-call | tf_op jit(solution)/shard_map/pallas_call | solution.py:345
  105.2 1.6 collective-permute-start.4
  106.9 1.3 collective-permute-start.10
  108.3 1.5 add.110
  109.9 8.3 %collective-permute-done.10 = f32[256,384]{1,0:T(8,128)S(1)} collective-permute-done((f32[256,384]{1,0:T(8,128)S(1)}, f32[256,384]{1,0:T(8,128)S(1)}, u32[]{:S(2)}, u32[]{:S(2)}) %collective-permute-start.10) | collective-permute-done | bytes 393248 | tf_op jit(solution)/shard_map/ppermute | solution.py:415
  118.2 0.9 collective-permute-start.16
  119.5 1.3 collective-permute-start.13
  121.0 1.3 collective-permute-done.4
  122.3 1.8 collective-permute-start.1
  124.7 7.8 %collective-permute-done.16 = f32[256,512]{1,0:T(8,128)S(1)} collective-permute-done((f32[256,512]{1,0:T(8,128)S(1)}, f32[256,512]{1,0:T(8,128)S(1)}, u32[]{:S(2)}, u32[]{:S(2)}) %collective-permute-start.16) | collective-permute-done | bytes 524320 | tf_op jit(solution)/shard_map/ppermute | solution.py:415
  132.5 0.9 collective-permute-start.7
  133.5 0.8 collective-permute-done.13
  134.3 1.1 collective-permute-start.5
  135.6 1.3 collective-permute-start.17
  137.2 11.2 %collective-permute-done.1 = f32[256,640]{1,0:T(8,128)S(1)} collective-permute-done((f32[256,640]{1,0:T(8,128)S(1)}, f32[256,640]{1,0:T(8,128)S(1)}, u32[]{:S(2)}, u32[]{:S(2)}) %collective-permute-start.1) | collective-permute-done | bytes 655392 | tf_op jit(solution)/shard_map/ppermute | solution.py:415
  148.4 1.5 collective-permute-start.21
  150.1 1.0 collective-permute-start.2
  151.2 9.6 %collective-permute-done.21 = f32[256,512]{1,0:T(8,128)S(1)} collective-permute-done((f32[256,512]{1,0:T(8,128)S(1)}, f32[256,512]{1,0:T(8,128)S(1)}, u32[]{:S(2)}, u32[]{:S(2)}) %collective-permute-start.21) | collective-permute-done | bytes 524320 | tf_op jit(solution)/shard_map/ppermute | solution.py:415
  160.8 1.8 collective-permute-start.8
  163.3 2.3 %collective-permute-start.22 = (f32[128,512]{1,0:T(8,128)S(1)}, f32[128,512]{1,0:T(8,128)S(1)}, u32[]{:S(2)}, u32[]{:S(2)}) collective-permute-start(f32[128,512]{1,0:T(8,128)S(1)} %slice.223), channel_id=1, source_target_pairs={{0,16},{1,17},{2,18},{3,19},{4,20},{5,21},{6,22},{7,23},{8,24},{9,... | collective-permute-start | bytes 786440 | tf_op jit(solution)/shard_map/ppermute | solution.py:415
  165.8 2.8 %collective-permute-done.8 = f32[128,640]{1,0:T(8,128)S(1)} collective-permute-done((f32[128,640]{1,0:T(8,128)S(1)}, f32[128,640]{1,0:T(8,128)S(1)}, u32[]{:S(2)}, u32[]{:S(2)}) %collective-permute-start.8) | collective-permute-done | bytes 327712 | tf_op jit(solution)/shard_map/ppermute | solution.py:415
  169.2 1.3 collective-permute-start.18
  170.5 5.8 %collective-permute-done.22 = f32[128,512]{1,0:T(8,128)S(1)} collective-permute-done((f32[128,512]{1,0:T(8,128)S(1)}, f32[128,512]{1,0:T(8,128)S(1)}, u32[]{:S(2)}, u32[]{:S(2)}) %collective-permute-start.22) | collective-permute-done | bytes 262176 | tf_op jit(solution)/shard_map/ppermute | solution.py:415
  176.4 1.0 collective-permute-start.23
  177.3 4.1 %collective-permute-done.23 = f32[64,512]{1,0:T(8,128)S(1)} collective-permute-done((f32[64,512]{1,0:T(8,128)S(1)}, f32[64,512]{1,0:T(8,128)S(1)}, u32[]{:S(2)}, u32[]{:S(2)}) %collective-permute-start.23) | collective-permute-done | bytes 131104 | tf_op jit(solution)/shard_map/ppermute | solution.py:415
  181.4 1.3 collective-permute-start.24
  182.8 3.3 %collective-permute-done.18 = f32[64,2304]{1,0:T(8,128)S(1)} collective-permute-done((f32[64,2304]{1,0:T(8,128)S(1)}, f32[64,2304]{1,0:T(8,128)S(1)}, u32[]{:S(2)}, u32[]{:S(2)}) %collective-permute-start.18) | collective-permute-done | bytes 589856 | tf_op jit(solution)/shard_map/ppermute | solution.py:415
  186.9 12.7 %collective-permute-done.19 = f32[32,2304]{1,0:T(8,128)S(1)} collective-permute-done((f32[32,2304]{1,0:T(8,128)S(1)}, f32[32,2304]{1,0:T(8,128)S(1)}, u32[]{:S(2)}, u32[]{:S(2)}) %collective-permute-start.19) | collective-permute-done | bytes 294944 | tf_op jit(solution)/shard_map/ppermute | solution.py:415
  201.0 0.7 slice_add_fusion.16
  (94 shorter events, 7.4 us)
Async XLA Ops:
  1.3 13.2 %copy-start.12 = (f32[128]{0:T(128)S(1)}, f32[128]{0:T(128)}, u32[]{:S(2)}) copy-start(f32[128]{0:T(128)} %param.19) | copy-start | bytes 1540
  7.1 21.7 %all-to-all-start = ((f32[16,8,1024]{2,1,0:T(8,128)}), f32[16,8,1024]{2,1,0:T(8,128)S(1)}, u32[]{:S(2)}, u32[]{:S(2)}) async-start(f32[16,8,1024]{2,1,0:T(8,128)} %bitcast.25), calls=%async_computation | async-start | bytes 1048576 | tf_op jit(solution)/shard_map/all_to_all | solution.py:427
  28.8 0.8 copy-start
  53.9 13.5 %all-to-all-start.2 = ((f32[16,8,512]{2,1,0:T(8,128)}), f32[16,8,512]{2,1,0:T(8,128)S(1)}, u32[]{:S(2)}, u32[]{:S(2)}) async-start(f32[16,8,512]{2,1,0:T(8,128)} %bitcast.27), calls=%async_computation.2 | async-start | bytes 524288 | tf_op jit(solution)/shard_map/all_to_all | solution.py:427
  61.1 43.8 %collective-permute-start.3 = (f32[512,640]{1,0:T(8,128)}, f32[512,640]{1,0:T(8,128)S(1)}, u32[]{:S(2)}, u32[]{:S(2)}) collective-permute-start(f32[512,640]{1,0:T(8,128)} %get-tuple-element.76), channel_id=1, source_target_pairs={{0,2},{1,3},{2,0},{3,1},{4,6},{5,7},{6,4},{7,5},{8,10},{9,11},{10,... | collective-permute-start | bytes 3932168 | tf_op jit(solution)/shard_map/ppermute | solution.py:415
  67.4 0.7 copy-start.8
  73.4 17.8 %all-to-all-start.3 = ((f32[16,8,1024]{2,1,0:T(8,128)}), f32[16,8,1024]{2,1,0:T(8,128)S(1)}, u32[]{:S(2)}, u32[]{:S(2)}) async-start(f32[16,8,1024]{2,1,0:T(8,128)} %bitcast.26), calls=%async_computation.3 | async-start | bytes 1048576 | tf_op jit(solution)/shard_map/all_to_all | solution.py:427
  81.2 25.8 %collective-permute-start.15 = (f32[512,512]{1,0:T(8,128)}, f32[512,512]{1,0:T(8,128)}, u32[]{:S(2)}, u32[]{:S(2)}) collective-permute-start(f32[512,512]{1,0:T(8,128)} %get-tuple-element.87), channel_id=1, source_target_pairs={{0,2},{1,3},{2,0},{3,1},{4,6},{5,7},{6,4},{7,5},{8,10},{9,11},{10,... | collective-permute-start | bytes 3145736 | tf_op jit(solution)/shard_map/ppermute | solution.py:415
  81.3 24.0 %collective-permute-start.9 = (f32[512,384]{1,0:T(8,128)}, f32[512,384]{1,0:T(8,128)S(1)}, u32[]{:S(2)}, u32[]{:S(2)}) collective-permute-start(f32[512,384]{1,0:T(8,128)} %get-tuple-element.80), channel_id=1, source_target_pairs={{0,2},{1,3},{2,0},{3,1},{4,6},{5,7},{6,4},{7,5},{8,10},{9,11},{10,... | collective-permute-start | bytes 2359304 | tf_op jit(solution)/shard_map/ppermute | solution.py:415
  91.2 0.8 copy-start.1
  98.8 6.2 %copy-start.3 = (f32[512,640]{1,0:T(8,128)S(1)}, f32[512,640]{1,0:T(8,128)}, u32[]{:S(2)}) copy-start(f32[512,640]{1,0:T(8,128)} %get-tuple-element.75) | copy-start | bytes 3932164
  104.4 15.1 %collective-permute-start = (f32[512,640]{1,0:T(8,128)}, f32[512,640]{1,0:T(8,128)S(1)}, u32[]{:S(2)}, u32[]{:S(2)}) collective-permute-start(f32[512,640]{1,0:T(8,128)} %get-tuple-element.74), channel_id=1, source_target_pairs={{0,2},{1,3},{2,0},{3,1},{4,6},{5,7},{6,4},{7,5},{8,10},{9,11},{10,... | collective-permute-start | bytes 3932168 | tf_op jit(solution)/shard_map/ppermute | solution.py:415
  104.5 13.7 %collective-permute-start.12 = (f32[512,512]{1,0:T(8,128)}, f32[512,512]{1,0:T(8,128)S(1)}, u32[]{:S(2)}, u32[]{:S(2)}) collective-permute-start(f32[512,512]{1,0:T(8,128)} %get-tuple-element.85), channel_id=1, source_target_pairs={{0,2},{1,3},{2,0},{3,1},{4,6},{5,7},{6,4},{7,5},{8,10},{9,11},{10,... | collective-permute-start | bytes 3145736 | tf_op jit(solution)/shard_map/ppermute | solution.py:415
  104.9 19.3 %collective-permute-start.6 = (f32[512,640]{1,0:T(8,128)}, f32[512,640]{1,0:T(8,128)S(1)}, u32[]{:S(2)}, u32[]{:S(2)}) collective-permute-start(f32[512,640]{1,0:T(8,128)} %get-tuple-element.78), channel_id=1, source_target_pairs={{0,2},{1,3},{2,0},{3,1},{4,6},{5,7},{6,4},{7,5},{8,10},{9,11},{10,... | collective-permute-start | bytes 3932168 | tf_op jit(solution)/shard_map/ppermute | solution.py:415
  105.2 1.7 copy-start.9
  105.2 17.1 %collective-permute-start.4 = (f32[256,640]{1,0:T(8,128)S(1)}, f32[256,640]{1,0:T(8,128)S(1)}, u32[]{:S(2)}, u32[]{:S(2)}) collective-permute-start(f32[256,640]{1,0:T(8,128)S(1)} %slice.194), channel_id=1, source_target_pairs={{0,1},{1,0},{2,3},{3,2},{4,5},{5,4},{6,7},{7,6},{8,9},{9,8},{10,11... | collective-permute-start | bytes 1966088 | tf_op jit(solution)/shard_map/ppermute | solution.py:415
  106.8 1.5 copy-start.7
  106.9 11.2 %collective-permute-start.10 = (f32[256,384]{1,0:T(8,128)S(1)}, f32[256,384]{1,0:T(8,128)S(1)}, u32[]{:S(2)}, u32[]{:S(2)}) collective-permute-start(f32[256,384]{1,0:T(8,128)S(1)} %slice.203), channel_id=1, source_target_pairs={{0,4},{1,5},{2,6},{3,7},{4,0},{5,1},{6,2},{7,3},{8,12},{9,13},{10,... | collective-permute-start | bytes 1179656 | tf_op jit(solution)/shard_map/ppermute | solution.py:415
  108.3 9.9 %copy-start.11 = (f32[512,512]{1,0:T(8,128)S(1)}, f32[512,512]{1,0:T(8,128)}, u32[]{:S(2)}) copy-start(f32[512,512]{1,0:T(8,128)} %get-tuple-element.89) | copy-start | bytes 3145732
  109.8 9.4 %copy-start.6 = (f32[512,512]{1,0:T(8,128)S(1)}, f32[512,512]{1,0:T(8,128)}, u32[]{:S(2)}) copy-start(f32[512,512]{1,0:T(8,128)} %get-tuple-element.84) | copy-start | bytes 3145732
  118.1 17.4 %collective-permute-start.20 = (f32[512,512]{1,0:T(8,128)S(1)}, f32[512,512]{1,0:T(8,128)S(1)}, u32[]{:S(2)}, u32[]{:S(2)}) collective-permute-start(f32[512,512]{1,0:T(8,128)S(1)} %copy-done.11), channel_id=1, source_target_pairs={{0,2},{1,3},{2,0},{3,1},{4,6},{5,7},{6,4},{7,5},{8,10},{9,11},{10,... | collective-permute-start | bytes 3145736 | tf_op jit(solution)/shard_map/ppermute | solution.py:415
  118.2 14.3 %collective-permute-start.16 = (f32[256,512]{1,0:T(8,128)S(1)}, f32[256,512]{1,0:T(8,128)S(1)}, u32[]{:S(2)}, u32[]{:S(2)}) collective-permute-start(f32[256,512]{1,0:T(8,128)S(1)} %slice.212), channel_id=1, source_target_pairs={{0,4},{1,5},{2,6},{3,7},{4,0},{5,1},{6,2},{7,3},{8,12},{9,13},{10,... | collective-permute-start | bytes 1572872 | tf_op jit(solution)/shard_map/ppermute | solution.py:415
  119.2 1.6 copy-start.4
  119.5 14.9 %collective-permute-start.13 = (f32[256,512]{1,0:T(8,128)S(1)}, f32[256,512]{1,0:T(8,128)S(1)}, u32[]{:S(2)}, u32[]{:S(2)}) collective-permute-start(f32[256,512]{1,0:T(8,128)S(1)} %slice.208), channel_id=1, source_target_pairs={{0,1},{1,0},{2,3},{3,2},{4,5},{5,4},{6,7},{7,6},{8,9},{9,8},{10,11... | collective-permute-start | bytes 1572872 | tf_op jit(solution)/shard_map/ppermute | solution.py:415
  121.0 3.5 %copy-start.2 = (f32[512,640]{1,0:T(8,128)S(1)}, f32[512,640]{1,0:T(8,128)}, u32[]{:S(2)}) copy-start(f32[512,640]{1,0:T(8,128)} %get-tuple-element.77) | copy-start | bytes 3932164
  122.3 26.0 %collective-permute-start.1 = (f32[256,640]{1,0:T(8,128)S(1)}, f32[256,640]{1,0:T(8,128)S(1)}, u32[]{:S(2)}, u32[]{:S(2)}) collective-permute-start(f32[256,640]{1,0:T(8,128)S(1)} %slice.190), channel_id=1, source_target_pairs={{0,1},{1,0},{2,3},{3,2},{4,5},{5,4},{6,7},{7,6},{8,9},{9,8},{10,11... | collective-permute-start | bytes 1966088 | tf_op jit(solution)/shard_map/ppermute | solution.py:415
  124.2 44.4 %collective-permute-start.11 = (f32[128,384]{1,0:T(8,128)S(1)}, f32[128,384]{1,0:T(8,128)S(1)}, u32[]{:S(2)}, u32[]{:S(2)}) collective-permute-start(f32[128,384]{1,0:T(8,128)S(1)} %slice.205), channel_id=1, source_target_pairs={{0,1},{1,0},{2,3},{3,2},{4,5},{5,4},{6,7},{7,6},{8,9},{9,8},{10,11... | collective-permute-start | bytes 589832 | tf_op jit(solution)/shard_map/ppermute | solution.py:415
  132.5 17.6 %collective-permute-start.7 = (f32[256,640]{1,0:T(8,128)S(1)}, f32[256,640]{1,0:T(8,128)S(1)}, u32[]{:S(2)}, u32[]{:S(2)}) collective-permute-start(f32[256,640]{1,0:T(8,128)S(1)} %slice.198), channel_id=1, source_target_pairs={{0,4},{1,5},{2,6},{3,7},{4,0},{5,1},{6,2},{7,3},{8,12},{9,13},{10,... | collective-permute-start | bytes 1966088 | tf_op jit(solution)/shard_map/ppermute | solution.py:415
  133.5 3.5 %copy-start.5 = (f32[512,512]{1,0:T(8,128)S(1)}, f32[512,512]{1,0:T(8,128)}, u32[]{:S(2)}) copy-start(f32[512,512]{1,0:T(8,128)} %get-tuple-element.88) | copy-start | bytes 3145732
  134.3 28.3 %collective-permute-start.5 = (f32[128,640]{1,0:T(8,128)S(1)}, f32[128,640]{1,0:T(8,128)S(1)}, u32[]{:S(2)}, u32[]{:S(2)}) collective-permute-start(f32[128,640]{1,0:T(8,128)S(1)} %slice.196), channel_id=1, source_target_pairs={{0,4},{1,5},{2,6},{3,7},{4,0},{5,1},{6,2},{7,3},{8,12},{9,13},{10,... | collective-permute-start | bytes 983048 | tf_op jit(solution)/shard_map/ppermute | solution.py:415
  135.6 33.5 %collective-permute-start.17 = (f32[128,512]{1,0:T(8,128)S(1)}, f32[128,512]{1,0:T(8,128)S(1)}, u32[]{:S(2)}, u32[]{:S(2)}) collective-permute-start(f32[128,512]{1,0:T(8,128)S(1)} %slice.214), channel_id=1, source_target_pairs={{0,1},{1,0},{2,3},{3,2},{4,5},{5,4},{6,7},{7,6},{8,9},{9,8},{10,11... | collective-permute-start | bytes 786440 | tf_op jit(solution)/shard_map/ppermute | solution.py:415
  148.4 12.4 %collective-permute-start.21 = (f32[256,512]{1,0:T(8,128)S(1)}, f32[256,512]{1,0:T(8,128)S(1)}, u32[]{:S(2)}, u32[]{:S(2)}) collective-permute-start(f32[256,512]{1,0:T(8,128)S(1)} %slice.221), channel_id=1, source_target_pairs={{0,8},{1,9},{2,10},{3,11},{4,12},{5,13},{6,14},{7,15},{8,0},{9,1},... | collective-permute-start | bytes 1572872 | tf_op jit(solution)/shard_map/ppermute | solution.py:415
  150.1 13.2 %collective-permute-start.2 = (f32[128,640]{1,0:T(8,128)S(1)}, f32[128,640]{1,0:T(8,128)S(1)}, u32[]{:S(2)}, u32[]{:S(2)}) collective-permute-start(f32[128,640]{1,0:T(8,128)S(1)} %slice.192), channel_id=1, source_target_pairs={{0,4},{1,5},{2,6},{3,7},{4,0},{5,1},{6,2},{7,3},{8,12},{9,13},{10,... | collective-permute-start | bytes 983048 | tf_op jit(solution)/shard_map/ppermute | solution.py:415
  160.8 7.8 %collective-permute-start.8 = (f32[128,640]{1,0:T(8,128)S(1)}, f32[128,640]{1,0:T(8,128)S(1)}, u32[]{:S(2)}, u32[]{:S(2)}) collective-permute-start(f32[128,640]{1,0:T(8,128)S(1)} %slice.200), channel_id=1, source_target_pairs={{0,1},{1,0},{2,3},{3,2},{4,5},{5,4},{6,7},{7,6},{8,9},{9,8},{10,11... | collective-permute-start | bytes 983048 | tf_op jit(solution)/shard_map/ppermute | solution.py:415
  162.6 6.4 %collective-permute-start.14 = (f32[128,512]{1,0:T(8,128)S(1)}, f32[128,512]{1,0:T(8,128)S(1)}, u32[]{:S(2)}, u32[]{:S(2)}) collective-permute-start(f32[128,512]{1,0:T(8,128)S(1)} %slice.210), channel_id=1, source_target_pairs={{0,4},{1,5},{2,6},{3,7},{4,0},{5,1},{6,2},{7,3},{8,12},{9,13},{10,... | collective-permute-start | bytes 786440 | tf_op jit(solution)/shard_map/ppermute | solution.py:415
  163.3 13.0 %collective-permute-start.22 = (f32[128,512]{1,0:T(8,128)S(1)}, f32[128,512]{1,0:T(8,128)S(1)}, u32[]{:S(2)}, u32[]{:S(2)}) collective-permute-start(f32[128,512]{1,0:T(8,128)S(1)} %slice.223), channel_id=1, source_target_pairs={{0,16},{1,17},{2,18},{3,19},{4,20},{5,21},{6,22},{7,23},{8,24},{9,... | collective-permute-start | bytes 786440 | tf_op jit(solution)/shard_map/ppermute | solution.py:415
  169.2 16.9 %collective-permute-start.18 = (f32[64,2304]{1,0:T(8,128)S(1)}, f32[64,2304]{1,0:T(8,128)S(1)}, u32[]{:S(2)}, u32[]{:S(2)}) collective-permute-start(f32[64,2304]{1,0:T(8,128)S(1)} %slice.216), channel_id=1, source_target_pairs={{0,8},{1,9},{2,10},{3,11},{4,12},{5,13},{6,14},{7,15},{8,0},{9,1},... | collective-permute-start | bytes 1769480 | tf_op jit(solution)/shard_map/ppermute | solution.py:415
  176.4 5.0 %collective-permute-start.23 = (f32[64,512]{1,0:T(8,128)S(1)}, f32[64,512]{1,0:T(8,128)S(1)}, u32[]{:S(2)}, u32[]{:S(2)}) collective-permute-start(f32[64,512]{1,0:T(8,128)S(1)} %slice.225), channel_id=1, source_target_pairs={{0,4},{1,5},{2,6},{3,7},{4,0},{5,1},{6,2},{7,3},{8,12},{9,13},{10,... | collective-permute-start | bytes 393224 | tf_op jit(solution)/shard_map/ppermute | solution.py:415
  181.4 4.8 %collective-permute-start.24 = (f32[32,512]{1,0:T(8,128)S(1)}, f32[32,512]{1,0:T(8,128)S(1)}, u32[]{:S(2)}, u32[]{:S(2)}) collective-permute-start(f32[32,512]{1,0:T(8,128)S(1)} %slice.227), channel_id=1, source_target_pairs={{0,1},{1,0},{2,3},{3,2},{4,5},{5,4},{6,7},{7,6},{8,9},{9,8},{10,11... | collective-permute-start | bytes 196616 | tf_op jit(solution)/shard_map/ppermute | solution.py:415
  186.1 14.8 %copy-start.10 = (f32[1024]{0:T(1024)S(1)}, f32[1024]{0:T(1024)}, u32[]{:S(2)}) copy-start(f32[1024]{0:T(1024)} %param.18) | copy-start | bytes 12292
  186.2 13.4 %collective-permute-start.19 = (f32[32,2304]{1,0:T(8,128)S(1)}, f32[32,2304]{1,0:T(8,128)S(1)}, u32[]{:S(2)}, u32[]{:S(2)}) collective-permute-start(f32[32,2304]{1,0:T(8,128)S(1)} %slice.218), channel_id=1, source_target_pairs={{0,16},{1,17},{2,18},{3,19},{4,20},{5,21},{6,22},{7,23},{8,24},{9,... | collective-permute-start | bytes 884744 | tf_op jit(solution)/shard_map/ppermute | solution.py:415
where the time goes:
time: 202 us
  waiting for transfers between devices  95.9 us (47%)
  Pallas kernels  41.1 us (20%)
  starting transfers between devices  37.7 us (19%)
  blocking collectives  14.3 us (7%)
  local copies, waits for them, and re-layouts  5.61 us (3%)
  other arithmetic  5.41 us (3%)
    ppermute x25, waiting for transfers between devices, swap(): lax.ppermute(rows, ('chain', 'dp'), [(i, i ^ 1 << pos) for i in range(dev...  68.2 us
    pallas_call x8, Pallas kernels, call(): pl.pallas_call(kernel, out_shape=tuple((jax.ShapeDtypeStruct(shape, kind)...  41.1 us
    all_to_all x3, waiting for transfers between devices, trade(): return lax.all_to_all(blocks, 'chain', 0, 0, tiled=True)  27.7 us
    ppermute x25, starting transfers between devices, swap(): lax.ppermute(rows, ('chain', 'dp'), [(i, i ^ 1 << pos) for i in range(dev...  23 us
    all_to_all x3, starting transfers between devices, trade(): return lax.all_to_all(blocks, 'chain', 0, 0, tiled=True)  14.7 us
    all_to_all x1, blocking collectives, trade(): return lax.all_to_all(blocks, 'chain', 0, 0, tiled=True)  14.3 us
  transfers between devices with their start and end apart: 28, of which 16 were waited for; matrix products, arithmetic and copies ran while one was open for 3% of the time, Pallas kernels for 13%

commit v1 on v0

v1 whole, which is shorter than its diff:
```python
import functools

import jax
import jax.numpy as jnp
from jax import lax
from jax.experimental import pallas as pl
from jax.experimental.pallas import tpu as pltpu
from jax.sharding import PartitionSpec as P


HEAD = 64
LANES = 128
epsilon = 1e-05
score_scale = 0.125
F32 = jnp.float32
BF16 = jnp.bfloat16


def mm(a, b):
    return lax.dot_general(a, b, (((1,), (0,)), ((), ())), preferred_element_type=F32)


def mm_nt(a, b):
    return lax.dot_general(a, b, (((1,), (1,)), ((), ())), preferred_element_type=F32)


def inverse_rms(rows):
    return lax.rsqrt(jnp.mean(rows * rows, axis=-1, keepdims=True) + epsilon)


def low_lanes(shape):
    return lax.broadcasted_iota(jnp.int32, shape, 1) < HEAD


def padded(tile, odd):
    wide = tile.astype(F32)
    mine = low_lanes(wide.shape) != bool(odd)
    here = jnp.where(mine, wide, 0.0)
    there = pltpu.roll(here, HEAD, 1)
    low, high = (there, here) if odd else (here, there)
    return jnp.concatenate([low, high], axis=0).astype(BF16)


def unpadded(total, odd):
    rows = total.shape[0] // 2
    low_mask = low_lanes((rows, LANES))
    low = jnp.where(low_mask, total[:rows], 0.0)
    high = jnp.where(low_mask, 0.0, total[rows:])
    return high + pltpu.roll(low, HEAD, 1) if odd else low + pltpu.roll(high, HEAD, 1)


def softmax_rows(scores, allowed):
    width = scores.shape[0] // 2
    halves = []
    for part in (scores[:width], scores[width:]):
        part = jnp.where(allowed, part, -1e30)
        raised = jnp.exp(part - jnp.max(part, axis=0, keepdims=True))
        halves.append(raised / jnp.sum(raised, axis=0, keepdims=True))
    return jnp.concatenate(halves, axis=0)


def softmax_back(weights, d_weights):
    width = weights.shape[0] // 2
    halves = []
    for at in (0, width):
        w, d = weights[at : at + width], d_weights[at : at + width]
        halves.append(w * (d - jnp.sum(w * d, axis=0, keepdims=True)))
    return jnp.concatenate(halves, axis=0)


def split3(value):
    high = value.astype(BF16)
    rest = value - high.astype(F32)
    mid = rest.astype(BF16)
    return high, mid, (rest - mid.astype(F32)).astype(BF16)


def row_times(row, matrix, transposed):
    pieces = split3(row)
    stacked = jnp.concatenate(list(pieces) + [jnp.zeros_like(pieces[0])] * 13, axis=0)
    return jnp.sum((mm_nt if transposed else mm)(stacked, matrix), axis=0, keepdims=True)


def prepare_kernel(
    length, seg, cot, wq, wk, wv, wo, gain, vector, mem0,
    q_o, kv_o, sn_o, s_o, c_o, u_o, both_o,
):
    count = seg.shape[0]
    kv_width = wk.shape[1]
    rows = seg[...].astype(F32)
    start = mem0[...].astype(F32)
    g = gain[...]
    xn = (rows * inverse_rms(rows) * g).astype(BF16)
    sn = (start * inverse_rms(start) * g).astype(BF16)
    sn_o[...] = sn
    both = mm(jnp.concatenate([xn, sn], axis=0), wq[...]) * score_scale
    q_o[...] = both[:count].astype(BF16)
    s_o[...] = both[count:].astype(BF16)
    kv_o[:, :kv_width] = mm(xn, wk[...]).astype(BF16)
    kv_o[:, kv_width:] = mm(xn, wv[...]).astype(BF16)
    u_o[...] = row_times(vector[...], wo[...], True)
    slots = mem0.shape[0]
    allowed = lax.broadcasted_iota(jnp.int32, (count, slots), 0) < length[0, 0]
    pairs = s_o.shape[1] // LANES
    groups = kv_width // HEAD
    for group in range(groups):
        at, odd = (group // 2) * LANES, group % 2
        keys = padded(kv_o[:, at : at + LANES], odd)
        values_t = padded(kv_o[:, kv_width + at : kv_width + at + LANES], odd).T
        for pair in range(group * pairs // groups, (group + 1) * pairs // groups):
            lanes = slice(pair * LANES, (pair + 1) * LANES)
            weights = softmax_rows(mm_nt(keys, s_o[:, lanes]), allowed).astype(BF16)
            c_o[:, lanes] = mm(values_t, weights).T.astype(BF16).astype(F32)
    valid = lax.broadcasted_iota(jnp.int32, (count, 1), 0) < length[0, 0]
    both_o[:count] = xn.astype(F32)
    both_o[count:] = jnp.where(valid, cot[...].astype(F32), 0.0)


def tiled(rows, times):
    return jnp.concatenate([rows] * times, axis=0)


def owner_scan_kernel(call, bias, u, p_o, stat_o, end_o, *, count):
    rows, width = call.shape
    own = rows // count
    logits = jnp.sum(call[...] * u[...], axis=1, keepdims=True) + tiled(bias[...], count)
    stat_o[0] = jnp.broadcast_to(jax.nn.sigmoid(logits), (rows, LANES))
    memory = jnp.zeros((own, width), F32)
    keep = jnp.ones((own, LANES), F32)
    for c in range(count):
        at = slice(c * own, (c + 1) * own)
        p_o[at, :] = memory
        stat_o[1, at, :] = keep
        ret = stat_o[0, at, :]
        memory = ret[:, :1] * memory + (1.0 - ret[:, :1]) * call[at, :]
        keep = keep * ret
    end_o[:, :width] = memory
    end_o[:, width:] = 1.0 - keep


def owner_kernel(
    p_in, stat, handed, mem_own, wo, wk, wv, gain, both_o, mem_o, stat_o, mkv_o, *, count
):
    rows, width = p_in.shape
    keep_here = stat[1]
    p = p_in[...] + keep_here[:, :1] * tiled(handed[:, :width], count)
    keep = keep_here * tiled(1.0 - handed[:, width:], count)
    both_o[rows:] = p
    mem = keep[:, :1] * tiled(mem_own[...], count) + mm(p.astype(BF16), wo[...])
    mem_o[...] = mem
    inverse = inverse_rms(mem)
    stat_o[0] = keep
    stat_o[1] = jnp.broadcast_to(inverse, (rows, LANES))
    mn = (mem * inverse * gain[...]).astype(BF16)
    both_o[:rows] = mn.astype(F32)
    kv_width = wk.shape[1]
    mkv_o[:, :kv_width] = mm(mn, wk[...]).astype(BF16).astype(F32)
    mkv_o[:, kv_width:] = mm(mn, wv[...]).astype(BF16).astype(F32)


def read_kernel(
    length, seg, cot, q, kv, mkv, wo, out_o, cr_o, dq_o, dkv_o, dmkv_o, dcr_s, cr_s
):
    count, width = q.shape
    slots = mkv.shape[0]
    kv_width = kv.shape[1] // 2
    pairs = width // LANES
    groups = kv_width // HEAD
    valid = lax.broadcasted_iota(jnp.int32, (count, 1), 0) < length[0, 0]
    d_out = jnp.where(valid, cot[...].astype(F32), 0.0).astype(BF16)
    dcr_s[...] = mm_nt(d_out, wo[...]).astype(BF16)
    key_at = lax.broadcasted_iota(jnp.int32, (slots + count, count), 0) - slots
    query_at = lax.broadcasted_iota(jnp.int32, (slots + count, count), 1)
    allowed = (key_at < 0) | ((key_at <= query_at) & (key_at < length[0, 0]))
    d_keys = [None] * groups
    d_values = [None] * groups
    for group in range(groups):
        at, odd = (group // 2) * LANES, group % 2
        keys = padded(
            jnp.concatenate(
                [mkv[:, at : at + LANES], kv[:, at : at + LANES].astype(F32)], axis=0
            ),
            odd,
        )
        at_v = kv_width + at
        values = padded(
            jnp.concatenate(
                [mkv[:, at_v : at_v + LANES], kv[:, at_v : at_v + LANES].astype(F32)], axis=0
            ),
            odd,
        )
        keys_t, values_t = keys.T, values.T
        dk = dv = None
        for pair in range(group * pairs // groups, (group + 1) * pairs // groups):
            lanes = slice(pair * LANES, (pair + 1) * LANES)
            q_tile = q[:, lanes]
            weights = softmax_rows(mm_nt(keys, q_tile), allowed)
            rounded = weights.astype(BF16)
            context = mm(values_t, rounded).T.astype(BF16)
            cr_s[:, lanes] = context
            cr_o[:, lanes] = context.astype(F32)
            d_tile = dcr_s[:, lanes]
            d_weights = mm_nt(values, d_tile).astype(BF16).astype(F32)
            d_scores = softmax_back(weights, d_weights).astype(BF16)
            dq = mm(keys_t, d_scores).T.astype(BF16).astype(F32)
            dq_o[:, lanes] = dq * score_scale
            dk_here = mm(d_scores, q_tile)
            dv_here = mm(rounded, d_tile)
            dk = dk_here if dk is None else dk + dk_here
            dv = dv_here if dv is None else dv + dv_here
        d_keys[group] = unpadded(dk, odd)
        d_values[group] = unpadded(dv, odd)
    for side, parts in ((0, d_keys), (kv_width, d_values)):
        for tile in range(groups // 2):
            lanes = slice(side + tile * LANES, side + (tile + 1) * LANES)
            total = (parts[2 * tile] + parts[2 * tile + 1]).astype(BF16).astype(F32)
            dmkv_o[:, lanes] = total[:slots]
            dkv_o[:, lanes] = total[slots:]
    out_o[...] = (seg[...].astype(F32) + mm(cr_s[...], wo[...])).astype(BF16)


def back_scan_kernel(
    place, dmkv, mem, ret, stat, mem_own, wo, wk, wv, gain,
    r_o, later_o, stat_o, end_o, g0_o, gain_o, *, count,
):
    rows, width = mem.shape
    own = rows // count
    kv_width = wk.shape[1]
    dmb = dmkv[...].astype(BF16)
    dmn = mm_nt(dmb[:, :kv_width], wk[...]) + mm_nt(dmb[:, kv_width:], wv[...])
    inverse = stat[1][:, :1]
    keep = stat[0][:, :1]
    memory = mem[...]
    gain_o[...] = jnp.sum(dmn * memory * inverse, axis=0, keepdims=True)
    scaled = dmn * gain[...]
    inner = jnp.sum(scaled * memory, axis=1, keepdims=True) * (1.0 / width)
    r = inverse * scaled - memory * (inverse * inverse * inverse * inner)
    rounded = r.astype(BF16)
    r_o[...] = rounded.astype(F32)
    q = jnp.sum(r * tiled(mem_own[...], count), axis=1, keepdims=True)
    kept = keep * r
    g0 = kept[:own]
    for c in range(1, count):
        g0 = g0 + kept[c * own : (c + 1) * own]
    at = lax.broadcasted_iota(jnp.int32, (rows, 1), 0)
    first = place[0, 0] * own
    g0_o[...] = jnp.where((at >= first) & (at < first + own), tiled(g0, count), 0.0)
    turned = mm_nt(rounded, wo[...])
    q = jnp.broadcast_to(q, (rows, LANES))
    later = jnp.zeros((own, width), F32)
    later_q = jnp.zeros((own, LANES), F32)
    passed = jnp.ones((own, LANES), F32)
    for c in reversed(range(count)):
        at = slice(c * own, (c + 1) * own)
        retain = ret[0, at, :]
        later_o[at, :] = later
        stat_o[0, at, :] = later_q
        stat_o[1, at, :] = passed
        later = turned[at] + retain[:, :1] * later
        later_q = q[at] + retain * later_q
        passed = passed * retain
    end_o[:, :width] = later
    end_o[:, width:] = later_q


def back_kernel(later, stat_b, handed, both, call, ret, stat, u, wo, gain_g, dc_o, vec_o, *, count):
    rows, width = later.shape
    passed = stat_b[1][:, :1]
    ahead = later[...] + passed * tiled(handed[:, :width], count)
    ahead_q = stat_b[0][:, :1] + passed * tiled(handed[:, width : width + 1], count)
    context = call[...]
    retain = ret[0][:, :1]
    d_retain = stat[0][:, :1] * ahead_q + jnp.sum(
        ahead * (both[rows:] - context), axis=1, keepdims=True
    )
    dz = d_retain * retain * (1.0 - retain)
    dc_o[...] = (1.0 - retain) * ahead + dz * u[...]
    v = jnp.sum(dz * context, axis=0, keepdims=True)
    vec_o[0:1, :] = gain_g[...]
    vec_o[1:2, :] = v
    vec_o[2:3, :] = row_times(v, wo[...], False)


def finish_kernel(
    key, length, seg, s, kv, dc, dq, dkv_r, wq, wk, wv, vec,
    dkv_o, keep_o, send_o, dqs_s, dkv_s,
):
    count, width = seg.shape
    slots = s.shape[0]
    pieces, piece, _ = dqs_s.shape
    kv_width = wk.shape[1]
    pairs = width // LANES
    groups = kv_width // HEAD
    allowed = lax.broadcasted_iota(jnp.int32, (count, slots), 0) < length[0, 0]
    d_keys = [None] * groups
    d_values = [None] * groups
    for group in range(groups):
        at, odd = (group // 2) * LANES, group % 2
        keys = padded(kv[:, at : at + LANES], odd)
        values = padded(kv[:, kv_width + at : kv_width + at + LANES], odd)
        keys_t = keys.T
        dk = dv = None
        for pair in range(group * pairs // groups, (group + 1) * pairs // groups):
            lanes = slice(pair * LANES, (pair + 1) * LANES)
            s_tile = s[:, lanes]
            weights = softmax_rows(mm_nt(keys, s_tile), allowed)
            d_tile = dc[:, lanes].astype(BF16)
            d_weights = mm_nt(values, d_tile).astype(BF16).astype(F32)
            d_scores = softmax_back(weights, d_weights).astype(BF16)
            dqs = mm(keys_t, d_scores).T.astype(BF16).astype(F32)
            dqs = dqs * score_scale
            for t in range(pieces):
                dqs_s[t, :, lanes] = dqs[t * piece : (t + 1) * piece]
            dk_here = mm(d_scores, s_tile)
            dv_here = mm(weights.astype(BF16), d_tile)
            dk = dk_here if dk is None else dk + dk_here
            dv = dv_here if dv is None else dv + dv_here
        d_keys[group] = unpadded(dk, odd)
        d_values[group] = unpadded(dv, odd)
    for side, parts in ((0, d_keys), (kv_width, d_values)):
        for tile in range(groups // 2):
            lanes = slice(side + tile * LANES, side + (tile + 1) * LANES)
            total = (parts[2 * tile] + parts[2 * tile + 1]).astype(BF16).astype(F32)
            total = (total + dkv_r[:, lanes]).astype(BF16)
            dkv_s[:, lanes] = total
            dkv_o[:, lanes] = total.astype(F32)
    dxn = mm_nt(dq[...].astype(BF16), wq[...])
    dxn = dxn + mm_nt(dkv_s[:, :kv_width], wk[...]) + mm_nt(dkv_s[:, kv_width:], wv[...])
    rows = seg[...].astype(F32)
    gain_here = jnp.sum(dxn * (rows * inverse_rms(rows)), axis=0, keepdims=True)
    half = slots // 2
    for t in range(pieces // 2):
        at = slice(t * piece, (t + 1) * piece)
        keep_o[at, :] = dqs_s[key[0, 0] ^ t]
        send_o[at, :] = dqs_s[key[0, 0] ^ (t + pieces // 2)]
    sums = jnp.concatenate(
        [vec[0:1, :] + gain_here, vec[1:3, :], jnp.zeros((5, width), F32)], axis=0
    )
    keep_o[half:] = sums
    send_o[half:] = sums


def last_kernel(
    key, me, near, far, total, sn, wq, mem0, gain, vector, kept, got, kept_out, got_out,
    query_o, out_o, small_o, mem_o, dqs_s, turn_s,
):
    slots, width = sn.shape
    pieces, piece, _ = dqs_s.shape
    height = kept.shape[0]
    for t in range(pieces // 2):
        at = slice(t * piece, (t + 1) * piece)
        dqs_s[key[0, 0] ^ t] = near[at]
        dqs_s[key[0, 0] ^ (t + pieces // 2)] = far[at]
    d_slots = jnp.concatenate([dqs_s[t] for t in range(pieces)], axis=0).astype(BF16)
    turned = sn[...].astype(F32).T
    for b in range(width // height):
        turn_s[b, :, :slots] = turned[b * height : (b + 1) * height]
    rows = turn_s[me[0, 0], :, :slots].astype(BF16)
    query_o[...] = kept[...] + got[...] + mm(rows, d_slots)
    dsn = mm_nt(d_slots, wq[...])
    start = mem0[...].astype(F32)
    inverse = inverse_rms(start)
    gain_row = jnp.sum(dsn * (start * inverse), axis=0, keepdims=True)
    scaled = dsn * gain[...]
    inner = jnp.sum(scaled * start, axis=1, keepdims=True) * (1.0 / width)
    d_start = inverse * scaled - start * (inverse * inverse * inverse * inner)
    sums = total[total.shape[0] - 8 :]
    small = jnp.concatenate(
        [sums, sums[0:1] + gain_row, jnp.zeros((slots - 9, width), F32)], axis=0
    )
    columns = jnp.concatenate([d_start, small], axis=0).T
    for b in range(width // height):
        turn_s[b] = columns[b * height : (b + 1) * height]
    mine = turn_s[me[0, 0]]
    held = kept_out[:, width:] + got_out[:, width:]
    mem_o[...] = (mine[:, :slots] + held).T
    small_o[...] = mine[:, slots:].T[:16]
    out_o[...] = (
        kept_out[:, :width]
        + got_out[:, :width]
        + mine[:, slots + 1 : slots + 2] * vector[...]
    )


def line_kernel(me, *refs, table, ranges):
    ins, out, turned = refs[:-2], refs[-2], refs[-1]
    blocks, height, _ = turned.shape
    lane = 0
    for i, first, last in ranges:
        across = slice(lane, lane + last - first)
        tall = ins[i][first:last].T
        for b in range(blocks):
            turned[b, :, across] = tall[b * height : (b + 1) * height]
        lane += last - first
    for b in range(blocks // 2):
        out[b * height : (b + 1) * height, :] = turned[me[0, 0] ^ table[b]].astype(BF16)


def product_kernel(me, *refs, plan):
    ins = refs[: plan["ins"]]
    outs = refs[plan["ins"] : plan["ins"] + 2 * len(plan["groups"])]
    turned, lined = refs[-2:]
    blocks, height, _ = turned.shape
    kind = turned.dtype
    places, lane = {}, 0
    for _, items in plan["groups"]:
        for lefts, _, _ in items:
            for left in lefts:
                if left in places:
                    continue
                if left[0] == "line":
                    places[left] = (ins[left[1]], slice(left[2], left[3]))
                    continue
                i, first, last = left
                rows = ins[i][first:last].astype(kind)
                across = slice(lane, lane + last - first)
                places[left] = (lined, across)
                tall = rows.T
                for b in range(blocks):
                    turned[b, :, across] = tall[b * height : (b + 1) * height]
                lane += last - first
    base = plan["groups"][0][0]
    for b in range(blocks // 2 if lane else 0):
        lined[b * height : (b + 1) * height, :lane] = turned[me[0, 0] ^ base[b], :, :lane]
    where = {dest: b for b, dest in enumerate(base)}
    for index, (table, items) in enumerate(plan["groups"]):
        runs = []
        for dest in table:
            b = where[dest]
            if runs and runs[-1][1] == b:
                runs[-1][1] = b + 1
            else:
                runs.append([b, b + 1])
        offset = 0
        cuts = []
        for lo, hi in runs:
            while lo < hi:
                take = min(hi - lo, blocks // 4 - offset % (blocks // 4))
                cuts.append((offset, lo, lo + take))
                offset += take
                lo += take
        at = 0
        for lefts, rights, columns in items:
            if rights:
                right = jnp.concatenate(
                    [
                        ins[i][first:last, columns[0] : columns[1]].astype(BF16)
                        for i, first, last in rights
                    ],
                    axis=0,
                )
            for offset, lo, hi in cuts:
                out = outs[2 * index + offset // (blocks // 4)]
                first = offset % (blocks // 4) * height
                to = slice(first, first + (hi - lo) * height)
                left = [
                    places[part][0][lo * height : hi * height, places[part][1]] for part in lefts
                ]
                if rights:
                    left = jnp.concatenate([part.astype(BF16) for part in left], axis=1)
                    out[to, at : at + right.shape[1]] = mm(left, right)
                else:
                    out[to, at : at + left[0].shape[1]] = sum(left[1:], left[0])
            at += columns[1] - columns[0]


SMEM = pl.BlockSpec(memory_space=pltpu.SMEM)
VMEM = pl.BlockSpec(memory_space=pltpu.VMEM)


def call(kernel, scalars, arrays, outs, scratch=()):
    return pl.pallas_call(
        kernel,
        out_shape=tuple(jax.ShapeDtypeStruct(shape, kind) for shape, kind in outs),
        in_specs=[SMEM] * len(scalars) + [VMEM] * len(arrays),
        out_specs=tuple([VMEM] * len(outs)),
        scratch_shapes=[pltpu.VMEM(shape, kind) for shape, kind in scratch],
    )(*scalars, *arrays)


def per_device(
    chain,
    docs,
    segments,
    lengths,
    query_weight,
    key_weight,
    value_weight,
    out_weight,
    norm_gain,
    gate_vector,
    gate_bias,
    memory_init,
    cotangent,
):
    segment, cot = segments[0, 0], cotangent[0, 0]
    count, width = segment.shape
    slots = memory_init.shape[0]
    kv2 = 2 * key_weight.shape[1]
    count_half = chain // 2
    own = slots // count_half
    devices = chain * docs
    place = lax.axis_index("chain")
    me = (place * docs + lax.axis_index("dp")).reshape(1, 1)
    mine = place % count_half
    gain, vector = norm_gain[None, :], gate_vector[None, :]
    bias = lax.dynamic_slice(gate_bias, (mine * own,), (own,))[:, None]
    mem_own = lax.dynamic_slice(memory_init, (mine * own, 0), (own, width)).astype(F32)

    bits = devices.bit_length() - 1
    low = docs.bit_length() - 1
    others = list(range(low + 1, bits))
    within = list(range(low))
    order_a = within + others
    order_b = others[:1] + within + others[1:]
    meet = low + 1
    cut = width // 2
    height = width // devices

    def table_of(order):
        table = []
        for b in range(devices // 2):
            table.append(sum(((b >> (bits - 2 - k)) & 1) << pos for k, pos in enumerate(order)))
        return tuple(table)

    def products(arrays, groups):
        outs, plan, ranges = [], [], {}
        for order, items in groups:
            lanes = sum(columns[1] - columns[0] for _, _, columns in items)
            outs += [((width // 4, lanes), F32)] * 2
            for lefts, _, _ in items:
                ranges.update({left: left[2] - left[1] for left in lefts if left[0] != "line"})
            plan.append((table_of(order), items))
        tall = max(LANES, sum(ranges.values()))
        return call(
            functools.partial(product_kernel, plan={"ins": len(arrays), "groups": plan}),
            [me],
            arrays,
            outs,
            [((devices, height, tall), F32), ((width // 2, tall), F32)],
        )

    def line(arrays, ranges):
        tall = sum(last - first for _, first, last in ranges)
        return call(
            functools.partial(line_kernel, table=table_of(order_a), ranges=ranges),
            [me],
            arrays,
            [((width // 2, tall), BF16)],
            [((devices, height, tall), F32)],
        )[0]

    def swap(rows, pos):
        return lax.ppermute(rows, ("chain", "dp"), [(i, i ^ (1 << pos)) for i in range(devices)])

    def fold(kept, got):
        half = kept.shape[0] // 2
        return kept[:half] + got[:half], kept[half:] + got[half:]

    def halved(kept, sent, order):
        for pos in order[:-1]:
            kept, sent = fold(kept, swap(sent, pos))
        return kept, swap(sent, order[-1])

    def joined(pairs):
        halves = [fold(*pair) for pair in pairs]
        return tuple(jnp.concatenate([half[i] for half in halves], axis=1) for i in (0, 1))

    halves = [list(range(count_half)), list(range(count_half, chain))]

    def trade(blocks):
        return lax.all_to_all(
            blocks, "chain", 0, 0, axis_index_groups=halves, tiled=True
        )

    def handed(rows, back):
        pairs = [(c, c + count_half) for c in range(count_half)]
        return lax.ppermute(rows, "chain", [(b, a) if back else (a, b) for a, b in pairs])

    q, kv, sn, s, c, u, pack0 = call(
        prepare_kernel,
        [lengths],
        [
            segment, cot, query_weight, key_weight, value_weight, out_weight, gain, vector,
            memory_init,
        ],
        [
            ((count, width), BF16),
            ((count, kv2), BF16),
            ((slots, width), BF16),
            ((slots, width), BF16),
            ((slots, width), F32),
            ((1, width), F32),
            ((2 * count, width), F32),
        ],
    )
    c_all = trade(c)
    pack0_far = swap(pack0, low)
    p_here, ret, end = call(
        functools.partial(owner_scan_kernel, count=count_half),
        [],
        [c_all, bias, u],
        [
            ((slots, width), F32),
            ((2, slots, LANES), F32),
            ((own, width + LANES), F32),
        ],
    )
    entering = handed(end, False)
    pack1, mem, stat, mkv = call(
        functools.partial(owner_kernel, count=count_half),
        [],
        [p_here, ret, entering, mem_own, out_weight, key_weight, value_weight, gain],
        [
            ((2 * slots, width), F32),
            ((slots, width), F32),
            ((2, slots, LANES), F32),
            ((slots, kv2), F32),
        ],
    )
    mkv_here = trade(mkv)
    pack1_far = swap(pack1, low)
    out, cr, dq, dkv_r, dmkv = call(
        read_kernel,
        [lengths],
        [segment, cot, q, kv, mkv_here, out_weight],
        [
            ((count, width), BF16),
            ((count, width), F32),
            ((count, width), F32),
            ((count, kv2), F32),
            ((slots, kv2), F32),
        ],
        [((count, width), BF16), ((count, width), BF16)],
    )
    dq_far = swap(dq, low)
    cr_far = swap(cr, low)
    dmkv_all = trade(dmkv)

    def rows_of(i, first, size):
        return (i, first, first + size)

    lined0 = line([pack0, pack0_far], [rows_of(0, 0, count), rows_of(1, 0, count)])
    lined1 = line(
        [pack1, pack1_far],
        [
            rows_of(0, 0, slots), rows_of(1, 0, slots),
            rows_of(0, slots, slots), rows_of(1, slots, slots),
        ],
    )
    early_items = (
        (("line", 0, 0, 2 * count),),
        (rows_of(1, 0, count), rows_of(2, 0, count)),
    )

    def split(items, *more):
        lefts, rights = items
        return [
            (order_a, [(lefts, rights, (0, cut))]),
            (order_b, [(lefts, rights, (cut, width)), *more]),
        ]

    early_a, sent_a, early_b, sent_b = products([lined0, dq, dq_far], split(early_items))
    early_a = halved(early_a, sent_a, order_a[:meet])
    early_b = halved(early_b, sent_b, order_b[:meet])
    r, later, stat_b, end, g0, gain_g = call(
        functools.partial(back_scan_kernel, count=count_half),
        [mine.reshape(1, 1)],
        [dmkv_all, mem, ret, stat, mem_own, out_weight, key_weight, value_weight, gain],
        [
            ((slots, width), F32),
            ((slots, width), F32),
            ((2, slots, LANES), F32),
            ((own, width + LANES), F32),
            ((slots, width), F32),
            ((1, width), F32),
        ],
    )
    r_far = swap(r, low)
    entering = handed(end, True)
    dmkv_far = swap(dmkv_all, low)
    g0_far = swap(g0, low)
    out_lefts = (
        rows_of(0, 0, count), rows_of(1, 0, count), ("line", 2, 2 * slots, 4 * slots),
    )
    out_rights = (
        rows_of(3, count, count), rows_of(4, count, count), rows_of(5, 0, slots), rows_of(6, 0, slots),
    )
    out_a, sent_a, out_b, sent_b = products(
        [cr, cr_far, lined1, pack0, pack0_far, r, r_far, g0, g0_far],
        split(
            (out_lefts, out_rights),
            ((rows_of(7, 0, slots), rows_of(8, 0, slots)), (), (0, slots)),
        ),
    )
    out_a = halved(out_a, sent_a, order_a[:meet])
    out_b = halved(out_b, sent_b, order_b[:meet])
    early_kept, early_got = halved(*joined([early_a, early_b]), order_a[meet:])
    out_kept, out_got = halved(*joined([out_a, out_b]), order_a[meet:])
    dc, vec = call(
        functools.partial(back_kernel, count=count_half),
        [],
        [later, stat_b, entering, pack1, c_all, ret, stat, u, out_weight, gain_g],
        [((slots, width), F32), ((3, width), F32)],
    )
    dc_here = trade(dc)
    slot_bits = [low] + order_a[:meet]
    parts = 1 << len(slot_bits)
    flat = me[0, 0]
    key = sum(
        ((flat >> pos) & 1) << (len(slot_bits) - 1 - k) for k, pos in enumerate(slot_bits)
    ).reshape(1, 1)
    dkv, kept_s, sent_s = call(
        finish_kernel,
        [key, lengths],
        [segment, s, kv, dc_here, dq, dkv_r, query_weight, key_weight, value_weight, vec],
        [((count, kv2), F32)] + [((slots // 2 + 8, width), F32)] * 2,
        [((parts, slots // parts, width), F32), ((count, kv2), BF16)],
    )
    got_s = swap(sent_s, low)
    dkv_far = swap(dkv, low)
    kv_left = (("line", 0, 0, 2 * count), ("line", 1, 0, 2 * slots))
    kv_right = (
        rows_of(2, 0, count), rows_of(3, 0, count), rows_of(4, 0, slots), rows_of(5, 0, slots),
    )
    late_a, sent_a, late_b, sent_b = products(
        [lined0, lined1, dkv, dkv_far, dmkv_all, dmkv_far],
        [
            (order_a, [(kv_left, kv_right, (0, kv2 // 2))]),
            (order_b, [(kv_left, kv_right, (kv2 // 2, kv2))]),
        ],
    )
    for pos in slot_bits[1:]:
        half = (kept_s.shape[0] - 8) // 2
        shared = kept_s[2 * half :] + got_s[2 * half :]
        sent_s = jnp.concatenate([kept_s[half : 2 * half] + got_s[half : 2 * half], shared], axis=0)
        kept_s = jnp.concatenate([kept_s[:half] + got_s[:half], shared], axis=0)
        got_s = swap(sent_s, pos)
    total = kept_s + got_s
    for pos in order_a[meet:]:
        total = total + swap(total, pos)
    slot_rows = total[:-8]
    for pos in reversed(slot_bits):
        slot_far = swap(slot_rows, pos)
        if pos != low:
            slot_rows = jnp.concatenate([slot_rows, slot_far], axis=0)
    late_a = halved(late_a, sent_a, order_a[:meet])
    late_b = halved(late_b, sent_b, order_b[:meet])
    late, got = halved(*joined([late_a, late_b]), order_a[meet:])
    g_kv = late + got
    g_query, g_out, g_small, g_mem = call(
        last_kernel,
        [key, me],
        [
            slot_rows, slot_far, total, sn, query_weight, memory_init, gain, vector,
            early_kept, early_got, out_kept, out_got,
        ],
        [((height, width), F32), ((height, width), F32), ((16, height), F32), ((slots, height), F32)],
        [((parts, slots // parts, width), F32), ((devices, height, 2 * slots), F32)],
    )
    return (
        out[None, None],
        g_query,
        g_kv[:, : kv2 // 2],
        g_kv[:, kv2 // 2 :],
        g_out,
        g_small[8],
        g_small[2],
        g_mem,
    )


def solution(mesh):
    in_specs = (
        P("dp", "chain", None, None),
        P("dp", "chain"),
        P(),
        P(),
        P(),
        P(),
        P(),
        P(),
        P(),
        P(),
        P("dp", "chain", None, None),
    )
    out_specs = (
        P("dp", "chain", None, None),
        P(("chain", "dp"), None),
        P(("chain", "dp"), None),
        P(("chain", "dp"), None),
        P(("chain", "dp"), None),
        P(("chain", "dp")),
        P(("chain", "dp")),
        P(None, ("chain", "dp")),
    )

    def step(*args):
        return per_device(mesh.shape["chain"], mesh.shape["dp"], *args)

    return jax.shard_map(
        step, mesh=mesh, in_specs=in_specs, out_specs=out_specs, check_vma=False
    )
```

time: 202 us -> 181 us (0.90)
  waiting for transfers between devices: 95.9 us -> 40.4 us
  starting transfers between devices: 37.7 us -> 53.4 us
  Pallas kernels: 41.1 us -> 54.4 us
  local copies, waits for them, and re-layouts: 5.61 us -> 10.3 us
  other arithmetic: 5.41 us -> 9.66 us
  blocking collectives: 14.3 us -> 10.3 us
    ppermute x25 -> x34, waiting for transfers between devices: 68.2 us -> 24.9 us  [swap(): lax.ppermute(rows, ('chain', 'dp'), [(i, i ^ 1 << pos) for i in range(dev...]
    all_to_all x3, waiting for transfers between devices: 27.7 us -> 7.59 us  [trade(): lax.all_to_all(blocks, 'chain', 0, 0, axis_index_groups=halves, tiled=True)]
    pallas_call x8 -> x13, Pallas kernels: 41.1 us -> 54.4 us  [call(): pl.pallas_call(kernel, out_shape=tuple((jax.ShapeDtypeStruct(shape, kind)...]
    ppermute x25 -> x34, starting transfers between devices: 23 us -> 35.1 us  [swap(): lax.ppermute(rows, ('chain', 'dp'), [(i, i ^ 1 << pos) for i in range(dev...]
    ppermute x0 -> x2, waiting for transfers between devices: none -> 7.95 us  [handed(): lax.ppermute(rows, 'chain', [(b, a) if back else (a, b) for a, b in pairs])]
    ppermute x0 -> x2, starting transfers between devices: none -> 5.77 us  [handed(): lax.ppermute(rows, 'chain', [(b, a) if back else (a, b) for a, b in pairs])]
    unnamed x27 -> x45, local copies, waits for them, and re-layouts: 2.39 us -> 7.68 us
    all_to_all x1, blocking collectives: 14.3 us -> 10.3 us  [trade(): lax.all_to_all(blocks, 'chain', 0, 0, axis_index_groups=halves, tiled=True)]
  transfers between devices with their start and end apart: 28 -> 39, of which waited for: 16 -> 14; matrix products, arithmetic and copies ran while one was open for 3% -> 6% of each run, Pallas kernels for 13% -> 24%
where the time goes in v1:
time: 181 us; the launch traced here: 180 us
  Pallas kernels  54.4 us (30%)
  starting transfers between devices  53.4 us (30%)
  waiting for transfers between devices  40.4 us (22%)
  local copies, waits for them, and re-layouts  10.3 us (6%)
  blocking collectives  10.3 us (6%)
  other arithmetic  9.66 us (5%)
    pallas_call x13, Pallas kernels, call(): pl.pallas_call(kernel, out_shape=tuple((jax.ShapeDtypeStruct(shape, kind)...  54.4 us
    ppermute x34, starting transfers between devices, swap(): lax.ppermute(rows, ('chain', 'dp'), [(i, i ^ 1 << pos) for i in range(dev...  35.1 us
    ppermute x34, waiting for transfers between devices, swap(): lax.ppermute(rows, ('chain', 'dp'), [(i, i ^ 1 << pos) for i in range(dev...  24.9 us
    all_to_all x3, starting transfers between devices, trade(): lax.all_to_all(blocks, 'chain', 0, 0, axis_index_groups=halves, tiled=True)  12.5 us
    all_to_all x1, blocking collectives, trade(): lax.all_to_all(blocks, 'chain', 0, 0, axis_index_groups=halves, tiled=True)  10.3 us
    ppermute x2, waiting for transfers between devices, handed(): lax.ppermute(rows, 'chain', [(b, a) if back else (a, b) for a, b in pairs])  7.95 us
    unnamed x45, local copies, waits for them, and re-layouts  7.68 us
    all_to_all x3, waiting for transfers between devices, trade(): lax.all_to_all(blocks, 'chain', 0, 0, axis_index_groups=halves, tiled=True)  7.59 us
  transfers between devices with their start and end apart: 39, of which 14 were waited for; matrix products, arithmetic and copies ran while one was open for 6% of the time, Pallas kernels for 24%

profile of v1, /device:TPU:0, one launch (start us, length us, event | category | flops | bytes accessed | tf_op | source)
XLA Modules:
  0.0 180.1 jit_solution(106466449472094475)
XLA Ops:
  1.3 6.2 %shard_map.170 = (bf16[128,1024]{1,0:T(8,128)(2,1)}, bf16[128,512]{1,0:T(8,128)(2,1)}, bf16[128,1024]{1,0:T(8,128)(2,1)}, bf16[128,1024]{1,0:T(8,128)(2,1)}, f32...) custom-call(s32[1,1]{1,0:T(1,128)S(6)} %copy.21.length, bf16[128,1024]{1,0:T(8,128)(2,1)} %bitcast.24, ...), custom_call_target="tpu_custom_call" | custom-call | tf_op jit(solution)/shard_map/pallas_call | solution.py:472
  7.5 5.3 %all-to-all-start = ((f32[8,16,1024]{2,1,0:T(8,128)}), f32[8,16,1024]{2,1,0:T(8,128)S(1)}, u32[]{:S(2)}, u32[]{:S(2)}) async-start(f32[8,16,1024]{2,1,0:T(8,128)} %bitcast.35), calls=%async_computation | async-start | bytes 1048576 | tf_op jit(solution)/shard_map/all_to_all | solution.py:572
  14.0 7.6 %all-to-all-done = f32[8,16,1024]{2,1,0:T(8,128)S(1)} async-done(((f32[8,16,1024]{2,1,0:T(8,128)}), f32[8,16,1024]{2,1,0:T(8,128)S(1)}, u32[]{:S(2)}, u32[]{:S(2)}) %all-to-all-start) | async-done | bytes 524320 | tf_op jit(solution)/shard_map/all_to_all | solution.py:572
  22.4 2.2 %shard_map.171 = (f32[128,1024]{1,0:T(8,128)}, f32[2,128,128]{2,1,0:T(8,128)}, f32[16,1152]{1,0:T(8,128)}) custom-call(f32[128,1024]{1,0:T(8,128)} %bitcast.22, f32[16,1]{1,0:T(8,128)} %copy.19.bias, f32[1,1024]{1,0:T(1,128)} %get-tuple-element.57.u), custom_call_target="tpu_custom_call" | custom-call | tf_op jit(solution)/shard_map/pallas_call | solution.py:472
  24.6 4.5 %collective-permute-start = (f32[16,1152]{1,0:T(8,128)}, f32[16,1152]{1,0:T(8,128)S(1)}, u32[]{:S(2)}, u32[]{:S(2)}) collective-permute-start(f32[16,1152]{1,0:T(8,128)} %get-tuple-element.60), channel_id=1, source_target_pairs={{0,16},{2,18},{4,20},{6,22},{8,24},{10,26},{12,28},{14,30},{1,17},... | collective-permute-start | bytes 221192 | tf_op jit(solution)/shard_map/ppermute | solution.py:578
  29.1 1.4 dynamic-slice_convert_fusion.mem_own
  32.0 3.9 %shard_map.172 = (f32[256,1024]{1,0:T(8,128)}, f32[128,1024]{1,0:T(8,128)}, f32[2,128,128]{2,1,0:T(8,128)}, f32[128,512]{1,0:T(8,128)}) custom-call(f32[128,1024]{1,0:T(8,128)} %get-tuple-element.58.p_in, f32[2,128,128]{2,1,0:T(8,128)} %get-tuple-element.59.stat.ret, f32[16,1152]{1,0:T(8,128)} %copy-done.21, f32[16,1024]{1,0:T(8,128)} %dynamic-slice_convert_fusion.mem_own, ...), custom_call_target="tpu_custom_call" | custom-call | tf_op jit(solution)/shard_map/pallas_call | solution.py:472
  35.9 10.3 %all_to_all.44 = f32[8,16,512]{2,1,0:T(8,128)} all-to-all(f32[8,16,512]{2,1,0:T(8,128)} %bitcast.37), channel_id=1, replica_groups={{0,2,4,6,8,10,12,14},{16,18,20,22,24,26,28,30},{1,3,5,7,9,11,13,15},{17..., dimensions={0} | all-to-all | bytes 524288 | tf_op jit(solution)/shard_map/all_to_all | solution.py:572
  46.2 6.4 %shard_map.173 = (bf16[128,1024]{1,0:T(8,128)(2,1)}, f32[128,1024]{1,0:T(8,128)}, f32[128,1024]{1,0:T(8,128)}, f32[128,512]{1,0:T(8,128)}, f32[128,512]{1,0:T(8,128)}) custom-call(s32[1,1]{1,0:T(1,128)S(6)} %copy.21.length, bf16[128,1024]{1,0:T(8,128)(2,1)} %bitcast.25, bf16[128,1024]{1,0:T(8,128)(2,1)} %bitcast.32, bf16[128,1024]{1,0:T(8,128)(2,1)} %get-tuple-element.54.q, ...), custom_call_target="tpu_custom_call" | custom-call | tf_op jit(solution)/shard_map/pallas_call | solution.py:472
  53.1 3.4 %all-to-all-start.2 = ((f32[8,16,512]{2,1,0:T(8,128)}), f32[8,16,512]{2,1,0:T(8,128)S(1)}, u32[]{:S(2)}, u32[]{:S(2)}) async-start(f32[8,16,512]{2,1,0:T(8,128)} %bitcast.36), calls=%async_computation.2 | async-start | bytes 524288 | tf_op jit(solution)/shard_map/all_to_all | solution.py:572
  57.5 2.6 %shard_map.177.refs_0_ = bf16[512,256]{1,0:T(8,128)(2,1)} custom-call(s32[1,1]{1,0:T(1,128)} %bitcast.11.me, f32[256,1024]{1,0:T(8,128)} %get-tuple-element.79.refs_0_.refs_3_, f32[256,1024]{1,0:T(8,128)} %copy-done.2), custom_call_target="tpu_custom_call" | custom-call | tf_op jit(solution)/shard_map/pallas_call | solution.py:472
  60.9 2.8 %shard_map.178 = (f32[256,512]{1,0:T(8,128)}, f32[256,512]{1,0:T(8,128)}, f32[256,512]{1,0:T(8,128)}, f32[256,512]{1,0:T(8,128)}) custom-call(s32[1,1]{1,0:T(1,128)} %bitcast.11.me, bf16[512,256]{1,0:T(8,128)(2,1)} %shard_map.177.refs_0_, f32[128,1024]{1,0:T(8,128)} %get-tuple-element.73.dq.refs_1_, f32[128,1024]{1,0:T(8,128)} %copy-done.13), custom_call_target="tpu_custom_call" | custom-call | tf_op jit(solution)/shard_map/pallas_call | solution.py:472
  63.7 1.5 collective-permute-start.12
  65.2 1.9 %collective-permute-start.14 = (f32[256,512]{1,0:T(8,128)}, f32[256,512]{1,0:T(8,128)}, u32[]{:S(2)}, u32[]{:S(2)}) collective-permute-start(f32[256,512]{1,0:T(8,128)} %get-tuple-element.83), channel_id=1, source_target_pairs={{0,4},{1,5},{2,6},{3,7},{4,0},{5,1},{6,2},{7,3},{8,12},{9,13},{10,... | collective-permute-start | bytes 1572872 | tf_op jit(solution)/shard_map/ppermute | solution.py:554
  67.9 4.9 %shard_map.174 = (f32[128,1024]{1,0:T(8,128)}, f32[128,1024]{1,0:T(8,128)}, f32[2,128,128]{2,1,0:T(8,128)}, f32[16,1152]{1,0:T(8,128)}, f32[128,1024]{1,0:T(8,128)}, /*index=5*/f32[1,1024]{1,0:T(1,128)}) custom-call(s32[1,1]{1,0:T(1,128)} %bitcast.12.place, f32[128,512]{1,0:T(8,128)} %bitcast.27, f32[128,1024]{1,0:T(8,128)} %get-tuple-element.65.mem, ...), custom_call_target="tpu_custom_call" | custom-call | tf_op jit(solution)/shard_map/pallas_call | solution.py:472
  72.8 1.3 collective-permute-start.1
  74.1 7.1 %collective-permute-done.1.handed = f32[16,1152]{1,0:T(8,128)S(1)} collective-permute-done((f32[16,1152]{1,0:T(8,128)}, f32[16,1152]{1,0:T(8,128)S(1)}, u32[]{:S(2)}, u32[]{:S(2)}) %collective-permute-start.1) | collective-permute-done | bytes 73760 | tf_op jit(solution)/shard_map/ppermute | solution.py:578
  81.8 3.8 %shard_map.175 = (f32[128,1024]{1,0:T(8,128)}, f32[3,1024]{1,0:T(4,128)}) custom-call(f32[128,1024]{1,0:T(8,128)} %get-tuple-element.67.later, f32[2,128,128]{2,1,0:T(8,128)} %get-tuple-element.68.stat_b, f32[16,1152]{1,0:T(8,128)} %copy-done.20, f32[256,1024]{1,0:T(8,128)} %get-tuple-element.70.both.refs_0_, f32[128,1024]{1,0:T(8,128)} %bitcast.23, ...), custom_call_target="tpu_custom_call" | custom-call | tf_op jit(solution)/shard_map/pallas_call | solution.py:472
  85.6 3.8 %all-to-all-start.3 = ((f32[8,16,1024]{2,1,0:T(8,128)}), f32[8,16,1024]{2,1,0:T(8,128)S(1)}, u32[]{:S(2)}, u32[]{:S(2)}) async-start(f32[8,16,1024]{2,1,0:T(8,128)} %bitcast.34), calls=%async_computation.3 | async-start | bytes 1048576 | tf_op jit(solution)/shard_map/all_to_all | solution.py:572
  89.7 2.0 %slice_add_fusion.7 = (f32[128,512]{1,0:T(8,128)S(1)}, f32[128,512]{1,0:T(8,128)}) fusion(f32[256,512]{1,0:T(8,128)} %collective-permute-done.12, f32[256,512]{1,0:T(8,128)} %get-tuple-element.80), kind=kLoop, calls=%fused_computation.10 | loop fusion | flops 131072 | bytes 1572864 | tf_op jit(solution)/shard_map/add | solution.py:558
  91.6 1.6 collective-permute-start.13
  93.3 1.9 %slice_add_fusion.5 = (f32[128,512]{1,0:T(8,128)S(1)}, f32[128,512]{1,0:T(8,128)}) fusion(f32[256,512]{1,0:T(8,128)} %collective-permute-done.14, f32[256,512]{1,0:T(8,128)S(1)} %copy-done.12), kind=kLoop, calls=%fused_computation.8 | loop fusion | flops 131072 | bytes 1572864 | tf_op jit(solution)/shard_map/add | solution.py:558
  95.6 3.0 %shard_map.179.refs_2_.refs_1_ = bf16[512,512]{1,0:T(8,128)(2,1)} custom-call(s32[1,1]{1,0:T(1,128)} %bitcast.11.me, f32[256,1024]{1,0:T(8,128)} %get-tuple-element.70.both.refs_0_, f32[256,1024]{1,0:T(8,128)} %collective-permute-done.19.refs_1_), custom_call_target="tpu_custom_call" | custom-call | tf_op jit(solution)/shard_map/pallas_call | solution.py:472
  98.7 5.0 %shard_map.180 = (f32[256,512]{1,0:T(8,128)}, f32[256,512]{1,0:T(8,128)}, f32[256,640]{1,0:T(8,128)}, f32[256,640]{1,0:T(8,128)}) custom-call(s32[1,1]{1,0:T(1,128)} %bitcast.11.me, f32[128,1024]{1,0:T(8,128)} %get-tuple-element.84.refs_0_, f32[128,1024]{1,0:T(8,128)} %collective-permute-done.18.refs_1_, bf16[512,512]{1,0:T(8,128)(2,1)} %shard_map.179.refs_2_.refs_1_, ...), custom_call_target="tpu_custom_call" | custom-call | tf_op jit(solution)/shard_map/pallas_call | solution.py:472
  103.6 1.5 collective-permute-start.22
  106.3 1.7 collective-permute-start.16
  108.8 6.8 %shard_map.176 = (f32[128,512]{1,0:T(8,128)}, f32[72,1024]{1,0:T(8,128)}, f32[72,1024]{1,0:T(8,128)}) custom-call(s32[1,1]{1,0:T(1,128)} %bitcast.10.key, s32[1,1]{1,0:T(1,128)S(6)} %copy.21.length, bf16[128,1024]{1,0:T(8,128)(2,1)} %bitcast.26, bf16[128,1024]{1,0:T(8,128)(2,1)} %get-tuple-element.63.s, bf16[128,512]{1,0:T(8,128)(2,1)} %get-tuple-element.55.kv, ...), custom_call_target="tpu_custom_call" | custom-call | tf_op jit(solution)/shard_map/pallas_call | solution.py:472
  116.1 1.4 collective-permute-done.22
  119.4 2.2 %collective-permute-done.24 = f32[256,640]{1,0:T(8,128)S(1)} collective-permute-done((f32[256,640]{1,0:T(8,128)}, f32[256,640]{1,0:T(8,128)S(1)}, u32[]{:S(2)}, u32[]{:S(2)}) %collective-permute-start.24) | collective-permute-done | bytes 655392 | tf_op jit(solution)/shard_map/ppermute | solution.py:554
  122.2 2.7 %shard_map.182 = (f32[256,256]{1,0:T(8,128)}, f32[256,256]{1,0:T(8,128)}, f32[256,256]{1,0:T(8,128)}, f32[256,256]{1,0:T(8,128)}) custom-call(s32[1,1]{1,0:T(1,128)} %bitcast.11.me, bf16[512,256]{1,0:T(8,128)(2,1)} %shard_map.177.refs_0_, bf16[512,512]{1,0:T(8,128)(2,1)} %shard_map.179.refs_2_.refs_1_, f32[128,512]{1,0:T(8,128)} %get-tuple-element.92.refs_2_, ...), custom_call_target="tpu_custom_call" | custom-call | tf_op jit(solution)/shard_map/pallas_call | solution.py:472
  124.9 1.5 collective-permute-start.30
  127.3 2.0 %collective-permute-start.3 = (f32[40,1024]{1,0:T(8,128)S(1)}, f32[40,1024]{1,0:T(8,128)S(1)}, u32[]{:S(2)}, u32[]{:S(2)}) collective-permute-start(f32[40,1024]{1,0:T(8,128)S(1)} %pad_maximum_fusion.3), channel_id=1, source_target_pairs={{0,1},{1,0},{2,3},{3,2},{4,5},{5,4},{6,7},{7,6},{8,9},{9,8},{10,11... | collective-permute-start | bytes 491528 | tf_op jit(solution)/shard_map/ppermute | solution.py:554
  130.3 8.8 %collective-permute-done.3 = f32[40,1024]{1,0:T(8,128)S(1)} collective-permute-done((f32[40,1024]{1,0:T(8,128)S(1)}, f32[40,1024]{1,0:T(8,128)S(1)}, u32[]{:S(2)}, u32[]{:S(2)}) %collective-permute-start.3) | collective-permute-done | bytes 163872 | tf_op jit(solution)/shard_map/ppermute | solution.py:554
  142.5 1.4 collective-permute-done.4
  143.9 1.5 collective-permute-start.5
  146.6 1.5 collective-permute-start.34
  148.1 1.8 %collective-permute-done.5 = f32[24,1024]{1,0:T(8,128)S(1)} collective-permute-done((f32[24,1024]{1,0:T(8,128)S(1)}, f32[24,1024]{1,0:T(8,128)S(1)}, u32[]{:S(2)}, u32[]{:S(2)}) %collective-permute-start.5) | collective-permute-done | bytes 98336 | tf_op jit(solution)/shard_map/ppermute | solution.py:554
  149.9 2.4 %collective-permute-start.6 = (f32[24,1024]{1,0:T(8,128)S(1)}, f32[24,1024]{1,0:T(8,128)S(1)}, u32[]{:S(2)}, u32[]{:S(2)}) collective-permute-start(f32[24,1024]{1,0:T(8,128)S(1)} %add.149), channel_id=1, source_target_pairs={{0,16},{1,17},{2,18},{3,19},{4,20},{5,21},{6,22},{7,23},{8,24},{9,... | collective-permute-start | bytes 294920 | tf_op jit(solution)/shard_map/ppermute | solution.py:554
  152.4 2.6 %collective-permute-start.26 = (f32[64,1152]{1,0:T(8,128)S(1)}, f32[64,1152]{1,0:T(8,128)S(1)}, u32[]{:S(2)}, u32[]{:S(2)}) collective-permute-start(f32[64,1152]{1,0:T(8,128)S(1)} %pad_maximum_fusion), channel_id=1, source_target_pairs={{0,8},{1,9},{2,10},{3,11},{4,12},{5,13},{6,14},{7,15},{8,0},{9,1},... | collective-permute-start | bytes 884744 | tf_op jit(solution)/shard_map/ppermute | solution.py:554
  155.0 1.5 collective-permute-done.6
  156.6 1.7 collective-permute-start.7
  158.2 2.0 %collective-permute-start.35 = (f32[32,512]{1,0:T(8,128)S(1)}, f32[32,512]{1,0:T(8,128)S(1)}, u32[]{:S(2)}, u32[]{:S(2)}) collective-permute-start(f32[32,512]{1,0:T(8,128)S(1)} %slice_add_fusion.24), channel_id=1, source_target_pairs={{0,16},{1,17},{2,18},{3,19},{4,20},{5,21},{6,22},{7,23},{8,24},{9,... | collective-permute-start | bytes 196616 | tf_op jit(solution)/shard_map/ppermute | solution.py:554
  160.9 3.2 %collective-permute-start.8 = (f32[32,1024]{1,0:T(8,128)S(1)}, f32[32,1024]{1,0:T(8,128)S(1)}, u32[]{:S(2)}, u32[]{:S(2)}) collective-permute-start(f32[32,1024]{1,0:T(8,128)S(1)} %pad_maximum_fusion.6), channel_id=1, source_target_pairs={{0,1},{1,0},{2,3},{3,2},{4,5},{5,4},{6,7},{7,6},{8,9},{9,8},{10,11... | collective-permute-start | bytes 393224 | tf_op jit(solution)/shard_map/ppermute | solution.py:554
  164.8 1.3 collective-permute-start.27
  167.8 4.6 %collective-permute-done.27.got_out = f32[32,1152]{1,0:T(8,128)S(1)} collective-permute-done((f32[32,1152]{1,0:T(8,128)S(1)}, f32[32,1152]{1,0:T(8,128)S(1)}, u32[]{:S(2)}, u32[]{:S(2)}) %collective-permute-start.27) | collective-permute-done | bytes 147488 | tf_op jit(solution)/shard_map/ppermute | solution.py:554
  173.1 4.2 %shard_map.181 = (f32[32,1024]{1,0:T(8,128)}, f32[32,1024]{1,0:T(8,128)}, f32[16,32]{1,0:T(8,128)}, f32[128,32]{1,0:T(8,128)}) custom-call(s32[1,1]{1,0:T(1,128)} %bitcast.10.key, s32[1,1]{1,0:T(1,128)} %bitcast.11.me, f32[64,1024]{1,0:T(8,128)} %copy-done.7, f32[64,1024]{1,0:T(8,128)} %copy-done.17, f32[24,1024]{1,0:T(8,128)} %copy-done.8, ...), custom_call_target="tpu_custom_call" | custom-call | tf_op jit(solution)/shard_map/pallas_call | solution.py:472
  177.3 1.5 copy.20
  178.9 1.2 slice_bitcast_fusion
  (125 shorter events, 23.1 us)
Async XLA Ops:
  0.6 12.6 %copy-start = (f32[128]{0:T(128)S(1)}, f32[128]{0:T(128)}, u32[]{:S(2)}) copy-start(f32[128]{0:T(128)} %param.19) | copy-start | bytes 1540
  7.5 14.1 %all-to-all-start = ((f32[8,16,1024]{2,1,0:T(8,128)}), f32[8,16,1024]{2,1,0:T(8,128)S(1)}, u32[]{:S(2)}, u32[]{:S(2)}) async-start(f32[8,16,1024]{2,1,0:T(8,128)} %bitcast.35), calls=%async_computation | async-start | bytes 1048576 | tf_op jit(solution)/shard_map/all_to_all | solution.py:572
  12.7 43.8 %collective-permute-start.10 = (f32[256,1024]{1,0:T(8,128)}, f32[256,1024]{1,0:T(8,128)S(1)}, u32[]{:S(2)}, u32[]{:S(2)}) collective-permute-start(f32[256,1024]{1,0:T(8,128)} %get-tuple-element.79.refs_0_.refs_3_), channel_id=1, source_target_pairs={{0,2},{1,3},{2,0},{3,1},{4,6},{5,7},{6,4},{7,5},{8,10},{9,11},{10,... | collective-permute-start | bytes 3145736 | tf_op jit(solution)/shard_map/ppermute | solution.py:554
  24.6 6.8 %collective-permute-start = (f32[16,1152]{1,0:T(8,128)}, f32[16,1152]{1,0:T(8,128)S(1)}, u32[]{:S(2)}, u32[]{:S(2)}) collective-permute-start(f32[16,1152]{1,0:T(8,128)} %get-tuple-element.60), channel_id=1, source_target_pairs={{0,16},{2,18},{4,20},{6,22},{8,24},{10,26},{12,28},{14,30},{1,17},... | collective-permute-start | bytes 221192 | tf_op jit(solution)/shard_map/ppermute | solution.py:578
  35.9 16.7 %copy-start.3 = (f32[256,1024]{1,0:T(8,128)S(1)}, f32[256,1024]{1,0:T(8,128)}, u32[]{:S(2)}) copy-start(f32[256,1024]{1,0:T(8,128)} %get-tuple-element.70.both.refs_0_) | copy-start | bytes 3145732
  52.6 7.5 %collective-permute-start.11 = (f32[128,1024]{1,0:T(8,128)}, f32[128,1024]{1,0:T(8,128)S(1)}, u32[]{:S(2)}, u32[]{:S(2)}) collective-permute-start(f32[128,1024]{1,0:T(8,128)} %get-tuple-element.73.dq.refs_1_), channel_id=1, source_target_pairs={{0,2},{1,3},{2,0},{3,1},{4,6},{5,7},{6,4},{7,5},{8,10},{9,11},{10,... | collective-permute-start | bytes 1572872 | tf_op jit(solution)/shard_map/ppermute | solution.py:554
  52.6 42.6 %collective-permute-start.19 = (f32[256,1024]{1,0:T(8,128)S(1)}, f32[256,1024]{1,0:T(8,128)}, u32[]{:S(2)}, u32[]{:S(2)}) collective-permute-start(f32[256,1024]{1,0:T(8,128)S(1)} %copy-done.3), channel_id=1, source_target_pairs={{0,2},{1,3},{2,0},{3,1},{4,6},{5,7},{6,4},{7,5},{8,10},{9,11},{10,... | collective-permute-start | bytes 3145736 | tf_op jit(solution)/shard_map/ppermute | solution.py:554
  53.1 14.1 %all-to-all-start.2 = ((f32[8,16,512]{2,1,0:T(8,128)}), f32[8,16,512]{2,1,0:T(8,128)S(1)}, u32[]{:S(2)}, u32[]{:S(2)}) async-start(f32[8,16,512]{2,1,0:T(8,128)} %bitcast.36), calls=%async_computation.2 | async-start | bytes 524288 | tf_op jit(solution)/shard_map/all_to_all | solution.py:572
  63.7 25.7 %collective-permute-start.12 = (f32[256,512]{1,0:T(8,128)}, f32[256,512]{1,0:T(8,128)}, u32[]{:S(2)}, u32[]{:S(2)}) collective-permute-start(f32[256,512]{1,0:T(8,128)} %get-tuple-element.81), channel_id=1, source_target_pairs={{0,1},{1,0},{2,3},{3,2},{4,5},{5,4},{6,7},{7,6},{8,9},{9,8},{10,11... | collective-permute-start | bytes 1572872 | tf_op jit(solution)/shard_map/ppermute | solution.py:554
  65.2 26.4 %collective-permute-start.14 = (f32[256,512]{1,0:T(8,128)}, f32[256,512]{1,0:T(8,128)}, u32[]{:S(2)}, u32[]{:S(2)}) collective-permute-start(f32[256,512]{1,0:T(8,128)} %get-tuple-element.83), channel_id=1, source_target_pairs={{0,4},{1,5},{2,6},{3,7},{4,0},{5,1},{6,2},{7,3},{8,12},{9,13},{10,... | collective-permute-start | bytes 1572872 | tf_op jit(solution)/shard_map/ppermute | solution.py:554
  67.9 6.2 %copy-start.10 = (f32[128,1024]{1,0:T(8,128)S(1)}, f32[128,1024]{1,0:T(8,128)}, u32[]{:S(2)}) copy-start(f32[128,1024]{1,0:T(8,128)} %get-tuple-element.84.refs_0_) | copy-start | bytes 1572868
  72.8 8.5 %collective-permute-start.1 = (f32[16,1152]{1,0:T(8,128)}, f32[16,1152]{1,0:T(8,128)S(1)}, u32[]{:S(2)}, u32[]{:S(2)}) collective-permute-start(f32[16,1152]{1,0:T(8,128)} %get-tuple-element.69), channel_id=1, source_target_pairs={{16,0},{18,2},{20,4},{22,6},{24,8},{26,10},{28,12},{30,14},{17,1},... | collective-permute-start | bytes 221192 | tf_op jit(solution)/shard_map/ppermute | solution.py:578
  74.1 24.6 %collective-permute-start.18 = (f32[128,1024]{1,0:T(8,128)S(1)}, f32[128,1024]{1,0:T(8,128)}, u32[]{:S(2)}, u32[]{:S(2)}) collective-permute-start(f32[128,1024]{1,0:T(8,128)S(1)} %copy-done.10), channel_id=1, source_target_pairs={{0,2},{1,3},{2,0},{3,1},{4,6},{5,7},{6,4},{7,5},{8,10},{9,11},{10,... | collective-permute-start | bytes 1572872 | tf_op jit(solution)/shard_map/ppermute | solution.py:554
  81.2 17.5 %collective-permute-start.20 = (f32[128,1024]{1,0:T(8,128)}, f32[128,1024]{1,0:T(8,128)}, u32[]{:S(2)}, u32[]{:S(2)}) collective-permute-start(f32[128,1024]{1,0:T(8,128)} %get-tuple-element.85.refs_5_), channel_id=1, source_target_pairs={{0,2},{1,3},{2,0},{3,1},{4,6},{5,7},{6,4},{7,5},{8,10},{9,11},{10,... | collective-permute-start | bytes 1572872 | tf_op jit(solution)/shard_map/ppermute | solution.py:554
  85.6 7.7 %copy-start.12 = (f32[256,512]{1,0:T(8,128)S(1)}, f32[256,512]{1,0:T(8,128)}, u32[]{:S(2)}) copy-start(f32[256,512]{1,0:T(8,128)} %get-tuple-element.82) | copy-start | bytes 1572868
  85.6 22.4 %all-to-all-start.3 = ((f32[8,16,1024]{2,1,0:T(8,128)}), f32[8,16,1024]{2,1,0:T(8,128)S(1)}, u32[]{:S(2)}, u32[]{:S(2)}) async-start(f32[8,16,1024]{2,1,0:T(8,128)} %bitcast.34), calls=%async_computation.3 | async-start | bytes 1048576 | tf_op jit(solution)/shard_map/all_to_all | solution.py:572
  89.4 9.2 %collective-permute-start.21 = (f32[128,1024]{1,0:T(8,128)}, f32[128,1024]{1,0:T(8,128)}, u32[]{:S(2)}, u32[]{:S(2)}) collective-permute-start(f32[128,1024]{1,0:T(8,128)} %get-tuple-element.86.refs_7_), channel_id=1, source_target_pairs={{0,2},{1,3},{2,0},{3,1},{4,6},{5,7},{6,4},{7,5},{8,10},{9,11},{10,... | collective-permute-start | bytes 1572872 | tf_op jit(solution)/shard_map/ppermute | solution.py:554
  91.6 13.9 %collective-permute-start.13 = (f32[128,512]{1,0:T(8,128)}, f32[128,512]{1,0:T(8,128)S(1)}, u32[]{:S(2)}, u32[]{:S(2)}) collective-permute-start(f32[128,512]{1,0:T(8,128)} %get-tuple-element.115), channel_id=1, source_target_pairs={{0,4},{1,5},{2,6},{3,7},{4,0},{5,1},{6,2},{7,3},{8,12},{9,13},{10,... | collective-permute-start | bytes 786440 | tf_op jit(solution)/shard_map/ppermute | solution.py:554
  95.1 10.4 %collective-permute-start.15 = (f32[128,512]{1,0:T(8,128)}, f32[128,512]{1,0:T(8,128)S(1)}, u32[]{:S(2)}, u32[]{:S(2)}) collective-permute-start(f32[128,512]{1,0:T(8,128)} %get-tuple-element.113), channel_id=1, source_target_pairs={{0,1},{1,0},{2,3},{3,2},{4,5},{5,4},{6,7},{7,6},{8,9},{9,8},{10,11... | collective-permute-start | bytes 786440 | tf_op jit(solution)/shard_map/ppermute | solution.py:554
  103.6 13.9 %collective-permute-start.22 = (f32[256,512]{1,0:T(8,128)}, f32[256,512]{1,0:T(8,128)S(1)}, u32[]{:S(2)}, u32[]{:S(2)}) collective-permute-start(f32[256,512]{1,0:T(8,128)} %get-tuple-element.88), channel_id=1, source_target_pairs={{0,1},{1,0},{2,3},{3,2},{4,5},{5,4},{6,7},{7,6},{8,9},{9,8},{10,11... | collective-permute-start | bytes 1572872 | tf_op jit(solution)/shard_map/ppermute | solution.py:554
  105.2 16.4 %collective-permute-start.24 = (f32[256,640]{1,0:T(8,128)}, f32[256,640]{1,0:T(8,128)S(1)}, u32[]{:S(2)}, u32[]{:S(2)}) collective-permute-start(f32[256,640]{1,0:T(8,128)} %get-tuple-element.90), channel_id=1, source_target_pairs={{0,4},{1,5},{2,6},{3,7},{4,0},{5,1},{6,2},{7,3},{8,12},{9,13},{10,... | collective-permute-start | bytes 1966088 | tf_op jit(solution)/shard_map/ppermute | solution.py:554
  106.3 11.9 %collective-permute-start.16 = (f32[64,1024]{1,0:T(8,128)}, f32[64,1024]{1,0:T(8,128)S(1)}, u32[]{:S(2)}, u32[]{:S(2)}) collective-permute-start(f32[64,1024]{1,0:T(8,128)} %pad_maximum_fusion.2), channel_id=1, source_target_pairs={{0,8},{1,9},{2,10},{3,11},{4,12},{5,13},{6,14},{7,15},{8,0},{9,1},... | collective-permute-start | bytes 786440 | tf_op jit(solution)/shard_map/ppermute | solution.py:554
  108.0 13.6 %collective-permute-start.29 = (f32[128,512]{1,0:T(8,128)S(1)}, f32[128,512]{1,0:T(8,128)}, u32[]{:S(2)}, u32[]{:S(2)}) collective-permute-start(f32[128,512]{1,0:T(8,128)S(1)} %bitcast.29), channel_id=1, source_target_pairs={{0,2},{1,3},{2,0},{3,1},{4,6},{5,7},{6,4},{7,5},{8,10},{9,11},{10,... | collective-permute-start | bytes 786440 | tf_op jit(solution)/shard_map/ppermute | solution.py:554
  108.8 8.7 %copy-start.11 = (f32[256,512]{1,0:T(8,128)S(1)}, f32[256,512]{1,0:T(8,128)}, u32[]{:S(2)}) copy-start(f32[256,512]{1,0:T(8,128)} %get-tuple-element.87) | copy-start | bytes 1572868
  115.7 6.6 %collective-permute-start.28 = (f32[128,512]{1,0:T(8,128)}, f32[128,512]{1,0:T(8,128)}, u32[]{:S(2)}, u32[]{:S(2)}) collective-permute-start(f32[128,512]{1,0:T(8,128)} %get-tuple-element.92.refs_2_), channel_id=1, source_target_pairs={{0,2},{1,3},{2,0},{3,1},{4,6},{5,7},{6,4},{7,5},{8,10},{9,11},{10,... | collective-permute-start | bytes 786440 | tf_op jit(solution)/shard_map/ppermute | solution.py:554
  117.5 8.9 %collective-permute-start.2 = (f32[72,1024]{1,0:T(8,128)}, f32[72,1024]{1,0:T(8,128)S(1)}, u32[]{:S(2)}, u32[]{:S(2)}) collective-permute-start(f32[72,1024]{1,0:T(8,128)} %get-tuple-element.77), channel_id=1, source_target_pairs={{0,2},{1,3},{2,0},{3,1},{4,6},{5,7},{6,4},{7,5},{8,10},{9,11},{10,... | collective-permute-start | bytes 884744 | tf_op jit(solution)/shard_map/ppermute | solution.py:554
  118.3 9.0 %collective-permute-start.23 = (f32[128,512]{1,0:T(8,128)}, f32[128,512]{1,0:T(8,128)}, u32[]{:S(2)}, u32[]{:S(2)}) collective-permute-start(f32[128,512]{1,0:T(8,128)} %get-tuple-element.111), channel_id=1, source_target_pairs={{0,4},{1,5},{2,6},{3,7},{4,0},{5,1},{6,2},{7,3},{8,12},{9,13},{10,... | collective-permute-start | bytes 786440 | tf_op jit(solution)/shard_map/ppermute | solution.py:554
  119.4 7.4 %copy-start.14 = (f32[72,1024]{1,0:T(8,128)S(1)}, f32[72,1024]{1,0:T(8,128)}, u32[]{:S(2)}) copy-start(f32[72,1024]{1,0:T(8,128)} %get-tuple-element.76) | copy-start | bytes 884740
  121.6 46.2 %collective-permute-start.17 = (f32[32,1024]{1,0:T(8,128)}, f32[32,1024]{1,0:T(8,128)S(1)}, u32[]{:S(2)}, u32[]{:S(2)}) collective-permute-start(f32[32,1024]{1,0:T(8,128)} %get-tuple-element.128), channel_id=1, source_target_pairs={{0,16},{1,17},{2,18},{3,19},{4,20},{5,21},{6,22},{7,23},{8,24},{9,... | collective-permute-start | bytes 393224 | tf_op jit(solution)/shard_map/ppermute | solution.py:554
  121.6 18.7 %collective-permute-start.25 = (f32[128,640]{1,0:T(8,128)S(1)}, f32[128,640]{1,0:T(8,128)S(1)}, u32[]{:S(2)}, u32[]{:S(2)}) collective-permute-start(f32[128,640]{1,0:T(8,128)S(1)} %get-tuple-element.109), channel_id=1, source_target_pairs={{0,1},{1,0},{2,3},{3,2},{4,5},{5,4},{6,7},{7,6},{8,9},{9,8},{10,11... | collective-permute-start | bytes 983048 | tf_op jit(solution)/shard_map/ppermute | solution.py:554
  124.9 15.4 %copy-start.16 = (f32[256,256]{1,0:T(8,128)S(1)}, f32[256,256]{1,0:T(8,128)}, u32[]{:S(2)}) copy-start(f32[256,256]{1,0:T(8,128)} %get-tuple-element.93) | copy-start | bytes 786436
  124.9 15.4 %collective-permute-start.30 = (f32[256,256]{1,0:T(8,128)}, f32[256,256]{1,0:T(8,128)S(1)}, u32[]{:S(2)}, u32[]{:S(2)}) collective-permute-start(f32[256,256]{1,0:T(8,128)} %get-tuple-element.94), channel_id=1, source_target_pairs={{0,1},{1,0},{2,3},{3,2},{4,5},{5,4},{6,7},{7,6},{8,9},{9,8},{10,11... | collective-permute-start | bytes 786440 | tf_op jit(solution)/shard_map/ppermute | solution.py:554
  126.4 15.0 %collective-permute-start.32 = (f32[256,256]{1,0:T(8,128)}, f32[256,256]{1,0:T(8,128)S(1)}, u32[]{:S(2)}, u32[]{:S(2)}) collective-permute-start(f32[256,256]{1,0:T(8,128)} %get-tuple-element.96), channel_id=1, source_target_pairs={{0,4},{1,5},{2,6},{3,7},{4,0},{5,1},{6,2},{7,3},{8,12},{9,13},{10,... | collective-permute-start | bytes 786440 | tf_op jit(solution)/shard_map/ppermute | solution.py:554
  126.8 14.7 %copy-start.15 = (f32[256,256]{1,0:T(8,128)S(1)}, f32[256,256]{1,0:T(8,128)}, u32[]{:S(2)}) copy-start(f32[256,256]{1,0:T(8,128)} %get-tuple-element.95) | copy-start | bytes 786436
  127.3 11.8 %collective-permute-start.3 = (f32[40,1024]{1,0:T(8,128)S(1)}, f32[40,1024]{1,0:T(8,128)S(1)}, u32[]{:S(2)}, u32[]{:S(2)}) collective-permute-start(f32[40,1024]{1,0:T(8,128)S(1)} %pad_maximum_fusion.3), channel_id=1, source_target_pairs={{0,1},{1,0},{2,3},{3,2},{4,5},{5,4},{6,7},{7,6},{8,9},{9,8},{10,11... | collective-permute-start | bytes 491528 | tf_op jit(solution)/shard_map/ppermute | solution.py:554
  139.2 4.7 %collective-permute-start.4 = (f32[24,1024]{1,0:T(8,128)S(1)}, f32[24,1024]{1,0:T(8,128)S(1)}, u32[]{:S(2)}, u32[]{:S(2)}) collective-permute-start(f32[24,1024]{1,0:T(8,128)S(1)} %pad_maximum_fusion.8), channel_id=1, source_target_pairs={{0,4},{1,5},{2,6},{3,7},{4,0},{5,1},{6,2},{7,3},{8,12},{9,13},{10,... | collective-permute-start | bytes 294920 | tf_op jit(solution)/shard_map/ppermute | solution.py:554
  140.4 5.0 %collective-permute-start.31 = (f32[128,256]{1,0:T(8,128)S(1)}, f32[128,256]{1,0:T(8,128)S(1)}, u32[]{:S(2)}, u32[]{:S(2)}) collective-permute-start(f32[128,256]{1,0:T(8,128)S(1)} %get-tuple-element.123), channel_id=1, source_target_pairs={{0,4},{1,5},{2,6},{3,7},{4,0},{5,1},{6,2},{7,3},{8,12},{9,13},{10,... | collective-permute-start | bytes 393224 | tf_op jit(solution)/shard_map/ppermute | solution.py:554
  141.5 5.0 %collective-permute-start.33 = (f32[128,256]{1,0:T(8,128)S(1)}, f32[128,256]{1,0:T(8,128)S(1)}, u32[]{:S(2)}, u32[]{:S(2)}) collective-permute-start(f32[128,256]{1,0:T(8,128)S(1)} %get-tuple-element.125), channel_id=1, source_target_pairs={{0,1},{1,0},{2,3},{3,2},{4,5},{5,4},{6,7},{7,6},{8,9},{9,8},{10,11... | collective-permute-start | bytes 393224 | tf_op jit(solution)/shard_map/ppermute | solution.py:554
  143.9 6.0 %collective-permute-start.5 = (f32[24,1024]{1,0:T(8,128)S(1)}, f32[24,1024]{1,0:T(8,128)S(1)}, u32[]{:S(2)}, u32[]{:S(2)}) collective-permute-start(f32[24,1024]{1,0:T(8,128)S(1)} %fusion.4), channel_id=1, source_target_pairs={{0,8},{1,9},{2,10},{3,11},{4,12},{5,13},{6,14},{7,15},{8,0},{9,1},... | collective-permute-start | bytes 294920 | tf_op jit(solution)/shard_map/ppermute | solution.py:554
  146.6 11.6 %collective-permute-start.34 = (f32[64,512]{1,0:T(8,128)S(1)}, f32[64,512]{1,0:T(8,128)S(1)}, u32[]{:S(2)}, u32[]{:S(2)}) collective-permute-start(f32[64,512]{1,0:T(8,128)S(1)} %pad_maximum_fusion.7), channel_id=1, source_target_pairs={{0,8},{1,9},{2,10},{3,11},{4,12},{5,13},{6,14},{7,15},{8,0},{9,1},... | collective-permute-start | bytes 393224 | tf_op jit(solution)/shard_map/ppermute | solution.py:554
  149.9 6.6 %collective-permute-start.6 = (f32[24,1024]{1,0:T(8,128)S(1)}, f32[24,1024]{1,0:T(8,128)S(1)}, u32[]{:S(2)}, u32[]{:S(2)}) collective-permute-start(f32[24,1024]{1,0:T(8,128)S(1)} %add.149), channel_id=1, source_target_pairs={{0,16},{1,17},{2,18},{3,19},{4,20},{5,21},{6,22},{7,23},{8,24},{9,... | collective-permute-start | bytes 294920 | tf_op jit(solution)/shard_map/ppermute | solution.py:554
  152.4 11.7 %collective-permute-start.26 = (f32[64,1152]{1,0:T(8,128)S(1)}, f32[64,1152]{1,0:T(8,128)S(1)}, u32[]{:S(2)}, u32[]{:S(2)}) collective-permute-start(f32[64,1152]{1,0:T(8,128)S(1)} %pad_maximum_fusion), channel_id=1, source_target_pairs={{0,8},{1,9},{2,10},{3,11},{4,12},{5,13},{6,14},{7,15},{8,0},{9,1},... | collective-permute-start | bytes 884744 | tf_op jit(solution)/shard_map/ppermute | solution.py:554
  156.5 15.9 %copy-start.8 = (f32[24,1024]{1,0:T(8,128)}, f32[24,1024]{1,0:T(8,128)S(1)}, u32[]{:S(2)}) copy-start(f32[24,1024]{1,0:T(8,128)S(1)} %add.150.total) | copy-start | bytes 294916
  156.6 4.3 %collective-permute-start.7 = (f32[16,1024]{1,0:T(8,128)S(1)}, f32[16,1024]{1,0:T(8,128)S(1)}, u32[]{:S(2)}, u32[]{:S(2)}) collective-permute-start(f32[16,1024]{1,0:T(8,128)S(1)} %slice.312), channel_id=1, source_target_pairs={{0,4},{1,5},{2,6},{3,7},{4,0},{5,1},{6,2},{7,3},{8,12},{9,13},{10,... | collective-permute-start | bytes 196616 | tf_op jit(solution)/shard_map/ppermute | solution.py:554
  158.2 8.9 %collective-permute-start.35 = (f32[32,512]{1,0:T(8,128)S(1)}, f32[32,512]{1,0:T(8,128)S(1)}, u32[]{:S(2)}, u32[]{:S(2)}) collective-permute-start(f32[32,512]{1,0:T(8,128)S(1)} %slice_add_fusion.24), channel_id=1, source_target_pairs={{0,16},{1,17},{2,18},{3,19},{4,20},{5,21},{6,22},{7,23},{8,24},{9,... | collective-permute-start | bytes 196616 | tf_op jit(solution)/shard_map/ppermute | solution.py:554
  160.9 6.1 %collective-permute-start.8 = (f32[32,1024]{1,0:T(8,128)S(1)}, f32[32,1024]{1,0:T(8,128)S(1)}, u32[]{:S(2)}, u32[]{:S(2)}) collective-permute-start(f32[32,1024]{1,0:T(8,128)S(1)} %pad_maximum_fusion.6), channel_id=1, source_target_pairs={{0,1},{1,0},{2,3},{3,2},{4,5},{5,4},{6,7},{7,6},{8,9},{9,8},{10,11... | collective-permute-start | bytes 393224 | tf_op jit(solution)/shard_map/ppermute | solution.py:554
  164.8 7.6 %collective-permute-start.27 = (f32[32,1152]{1,0:T(8,128)S(1)}, f32[32,1152]{1,0:T(8,128)S(1)}, u32[]{:S(2)}, u32[]{:S(2)}) collective-permute-start(f32[32,1152]{1,0:T(8,128)S(1)} %get-tuple-element.118), channel_id=1, source_target_pairs={{0,16},{1,17},{2,18},{3,19},{4,20},{5,21},{6,22},{7,23},{8,24},{9,... | collective-permute-start | bytes 442376 | tf_op jit(solution)/shard_map/ppermute | solution.py:554
  167.0 5.3 %collective-permute-start.9 = (f32[64,1024]{1,0:T(8,128)S(1)}, f32[64,1024]{1,0:T(8,128)S(1)}, u32[]{:S(2)}, u32[]{:S(2)}) collective-permute-start(f32[64,1024]{1,0:T(8,128)S(1)} %pad_maximum_fusion.1.near), channel_id=1, source_target_pairs={{0,2},{1,3},{2,0},{3,1},{4,6},{5,7},{6,4},{7,5},{8,10},{9,11},{10,... | collective-permute-start | bytes 786440 | tf_op jit(solution)/shard_map/ppermute | solution.py:554
  (13 other events, 27.1 us)

commit v2 on v1

--- a/solution.py
+++ b/solution.py
@@ -82,8 +82,7 @@
 
 
 def prepare_kernel(
-    length, seg, cot, wq, wk, wv, wo, gain, vector, mem0,
-    q_o, kv_o, sn_o, s_o, c_o, u_o, both_o,
+    length, seg, wq, wk, wv, gain, mem0, q_o, kv_o, sn_o, s_o, c_o
 ):
     count = seg.shape[0]
     kv_width = wk.shape[1]
@@ -98,7 +97,6 @@
     s_o[...] = both[count:].astype(BF16)
     kv_o[:, :kv_width] = mm(xn, wk[...]).astype(BF16)
     kv_o[:, kv_width:] = mm(xn, wv[...]).astype(BF16)
-    u_o[...] = row_times(vector[...], wo[...], True)
     slots = mem0.shape[0]
     allowed = lax.broadcasted_iota(jnp.int32, (count, slots), 0) < length[0, 0]
     pairs = s_o.shape[1] // LANES
@@ -111,9 +109,15 @@
             lanes = slice(pair * LANES, (pair + 1) * LANES)
             weights = softmax_rows(mm_nt(keys, s_o[:, lanes]), allowed).astype(BF16)
             c_o[:, lanes] = mm(values_t, weights).T.astype(BF16).astype(F32)
+
+
+def rows_kernel(length, seg, cot, wo, gain, vector, both_o, u_o):
+    count = seg.shape[0]
+    rows = seg[...].astype(F32)
+    both_o[:count] = (rows * inverse_rms(rows) * gain[...]).astype(BF16).astype(F32)
     valid = lax.broadcasted_iota(jnp.int32, (count, 1), 0) < length[0, 0]
-    both_o[:count] = xn.astype(F32)
     both_o[count:] = jnp.where(valid, cot[...].astype(F32), 0.0)
+    u_o[...] = row_times(vector[...], wo[...], True)
 
 
 def tiled(rows, times):
@@ -328,27 +332,27 @@
     dxn = dxn + mm_nt(dkv_s[:, :kv_width], wk[...]) + mm_nt(dkv_s[:, kv_width:], wv[...])
     rows = seg[...].astype(F32)
     gain_here = jnp.sum(dxn * (rows * inverse_rms(rows)), axis=0, keepdims=True)
-    half = slots // 2
+    step = piece + 8
+    sums = jnp.concatenate(
+        [vec[0:1, :] + gain_here, vec[1:3, :], jnp.zeros((5, width), F32)], axis=0
+    )
     for t in range(pieces // 2):
-        at = slice(t * piece, (t + 1) * piece)
+        at = slice(t * step, t * step + piece)
         keep_o[at, :] = dqs_s[key[0, 0] ^ t]
         send_o[at, :] = dqs_s[key[0, 0] ^ (t + pieces // 2)]
-    sums = jnp.concatenate(
-        [vec[0:1, :] + gain_here, vec[1:3, :], jnp.zeros((5, width), F32)], axis=0
-    )
-    keep_o[half:] = sums
-    send_o[half:] = sums
+        keep_o[t * step + piece : (t + 1) * step] = sums
+        send_o[t * step + piece : (t + 1) * step] = sums
 
 
 def last_kernel(
-    key, me, near, far, total, sn, wq, mem0, gain, vector, kept, got, kept_out, got_out,
-    query_o, out_o, small_o, mem_o, dqs_s, turn_s,
+    key, me, near, far, sn, wq, mem0, gain, vector, kept, got, kept_out, got_out,
+    query_o, out_o, gain_o, gate_o, mem_o, dqs_s, turn_s,
 ):
     slots, width = sn.shape
     pieces, piece, _ = dqs_s.shape
     height = kept.shape[0]
     for t in range(pieces // 2):
-        at = slice(t * piece, (t + 1) * piece)
+        at = slice(t * (piece + 8), t * (piece + 8) + piece)
         dqs_s[key[0, 0] ^ t] = near[at]
         dqs_s[key[0, 0] ^ (t + pieces // 2)] = far[at]
     d_slots = jnp.concatenate([dqs_s[t] for t in range(pieces)], axis=0).astype(BF16)
@@ -364,7 +368,7 @@
     scaled = dsn * gain[...]
     inner = jnp.sum(scaled * start, axis=1, keepdims=True) * (1.0 / width)
     d_start = inverse * scaled - start * (inverse * inverse * inverse * inner)
-    sums = total[total.shape[0] - 8 :]
+    sums = near[piece : piece + 8]
     small = jnp.concatenate(
         [sums, sums[0:1] + gain_row, jnp.zeros((slots - 9, width), F32)], axis=0
     )
@@ -373,8 +377,10 @@
         turn_s[b] = columns[b * height : (b + 1) * height]
     mine = turn_s[me[0, 0]]
     held = kept_out[:, width:] + got_out[:, width:]
-    mem_o[...] = (mine[:, :slots] + held).T
-    small_o[...] = mine[:, slots:].T[:16]
+    mem_o[...] = mine[:, :slots] + held
+    across = mine[:, slots:].T
+    gain_o[...] = across[8:9]
+    gate_o[...] = across[2:3]
     out_o[...] = (
         kept_out[:, :width]
         + got_out[:, :width]
@@ -398,12 +404,12 @@
 
 def product_kernel(me, *refs, plan):
     ins = refs[: plan["ins"]]
-    outs = refs[plan["ins"] : plan["ins"] + 2 * len(plan["groups"])]
+    outs = list(refs[plan["ins"] : -2])
     turned, lined = refs[-2:]
     blocks, height, _ = turned.shape
     kind = turned.dtype
     places, lane = {}, 0
-    for _, items in plan["groups"]:
+    for _, _, items in plan["groups"]:
         for lefts, _, _ in items:
             for left in lefts:
                 if left in places:
@@ -423,7 +429,8 @@
     for b in range(blocks // 2 if lane else 0):
         lined[b * height : (b + 1) * height, :lane] = turned[me[0, 0] ^ base[b], :, :lane]
     where = {dest: b for b, dest in enumerate(base)}
-    for index, (table, items) in enumerate(plan["groups"]):
+    for table, pieces, items in plan["groups"]:
+        size = blocks // 2 // pieces
         runs = []
         for dest in table:
             b = where[dest]
@@ -435,7 +442,7 @@
         cuts = []
         for lo, hi in runs:
             while lo < hi:
-                take = min(hi - lo, blocks // 4 - offset % (blocks // 4))
+                take = min(hi - lo, size - offset % size)
                 cuts.append((offset, lo, lo + take))
                 offset += take
                 lo += take
@@ -450,8 +457,8 @@
                     axis=0,
                 )
             for offset, lo, hi in cuts:
-                out = outs[2 * index + offset // (blocks // 4)]
-                first = offset % (blocks // 4) * height
+                out = outs[offset // size]
+                first = offset % size * height
                 to = slice(first, first + (hi - lo) * height)
                 left = [
                     places[part][0][lo * height : hi * height, places[part][1]] for part in lefts
@@ -462,6 +469,7 @@
                 else:
                     out[to, at : at + left[0].shape[1]] = sum(left[1:], left[0])
             at += columns[1] - columns[0]
+        outs = outs[pieces:]
 
 
 SMEM = pl.BlockSpec(memory_space=pltpu.SMEM)
@@ -525,12 +533,12 @@
 
     def products(arrays, groups):
         outs, plan, ranges = [], [], {}
-        for order, items in groups:
+        for order, pieces, items in groups:
             lanes = sum(columns[1] - columns[0] for _, _, columns in items)
-            outs += [((width // 4, lanes), F32)] * 2
+            outs += [((width // 2 // pieces, lanes), F32)] * pieces
             for lefts, _, _ in items:
                 ranges.update({left: left[2] - left[1] for left in lefts if left[0] != "line"})
-            plan.append((table_of(order), items))
+            plan.append((table_of(order), pieces, items))
         tall = max(LANES, sum(ranges.values()))
         return call(
             functools.partial(product_kernel, plan={"ins": len(arrays), "groups": plan}),
@@ -553,6 +561,27 @@
     def swap(rows, pos):
         return lax.ppermute(rows, ("chain", "dp"), [(i, i ^ (1 << pos)) for i in range(devices)])
 
+    spread = 1 << meet
+    masks = [
+        sum(((t >> (meet - 1 - k)) & 1) << pos for k, pos in enumerate(order_a[:meet]))
+        for t in range(spread)
+    ]
+
+    def direct(sent):
+        got = []
+        for t, part in enumerate(sent):
+            mask = masks[t + 1]
+            got.append(
+                lax.ppermute(
+                    part, ("chain", "dp"), [(i, i ^ mask) for i in range(devices)]
+                )
+            )
+        return got
+
+    def split_sum(parts):
+        half = parts[0].shape[0] // 2
+        return sum(part[:half] for part in parts), sum(part[half:] for part in parts)
+
     def fold(kept, got):
         half = kept.shape[0] // 2
         return kept[:half] + got[:half], kept[half:] + got[half:]
@@ -577,24 +606,25 @@
         pairs = [(c, c + count_half) for c in range(count_half)]
         return lax.ppermute(rows, "chain", [(b, a) if back else (a, b) for a, b in pairs])
 
-    q, kv, sn, s, c, u, pack0 = call(
+    q, kv, sn, s, c = call(
         prepare_kernel,
         [lengths],
-        [
-            segment, cot, query_weight, key_weight, value_weight, out_weight, gain, vector,
-            memory_init,
-        ],
+        [segment, query_weight, key_weight, value_weight, gain, memory_init],
         [
             ((count, width), BF16),
             ((count, kv2), BF16),
             ((slots, width), BF16),
             ((slots, width), BF16),
             ((slots, width), F32),
-            ((1, width), F32),
-            ((2 * count, width), F32),
         ],
     )
     c_all = trade(c)
+    pack0, u = call(
+        rows_kernel,
+        [lengths],
+        [segment, cot, out_weight, gain, vector],
+        [((2 * count, width), F32), ((1, width), F32)],
+    )
     pack0_far = swap(pack0, low)
     p_here, ret, end = call(
         functools.partial(owner_scan_kernel, count=count_half),
@@ -656,13 +686,13 @@
     def split(items, *more):
         lefts, rights = items
         return [
-            (order_a, [(lefts, rights, (0, cut))]),
-            (order_b, [(lefts, rights, (cut, width)), *more]),
+            (order_a, 2, [(lefts, rights, (0, cut))]),
+            (order_b, 2, [(lefts, rights, (cut, width)), *more]),
         ]
 
-    early_a, sent_a, early_b, sent_b = products([lined0, dq, dq_far], split(early_items))
-    early_a = halved(early_a, sent_a, order_a[:meet])
-    early_b = halved(early_b, sent_b, order_b[:meet])
+    early, *sent = products([lined0, dq, dq_far], [(order_a, spread, [(*early_items, (0, width))])])
+    early_far = direct(sent)
+    early = split_sum([early, *early_far])
     r, later, stat_b, end, g0, gain_g = call(
         functools.partial(back_scan_kernel, count=count_half),
         [mine.reshape(1, 1)],
@@ -695,7 +725,7 @@
     )
     out_a = halved(out_a, sent_a, order_a[:meet])
     out_b = halved(out_b, sent_b, order_b[:meet])
-    early_kept, early_got = halved(*joined([early_a, early_b]), order_a[meet:])
+    early_kept, early_got = halved(*early, order_a[meet:])
     out_kept, out_got = halved(*joined([out_a, out_b]), order_a[meet:])
     dc, vec = call(
         functools.partial(back_kernel, count=count_half),
@@ -710,11 +740,12 @@
     key = sum(
         ((flat >> pos) & 1) << (len(slot_bits) - 1 - k) for k, pos in enumerate(slot_bits)
     ).reshape(1, 1)
+    step = slots // parts + 8
     dkv, kept_s, sent_s = call(
         finish_kernel,
         [key, lengths],
         [segment, s, kv, dc_here, dq, dkv_r, query_weight, key_weight, value_weight, vec],
-        [((count, kv2), F32)] + [((slots // 2 + 8, width), F32)] * 2,
+        [((count, kv2), F32)] + [((spread * step, width), F32)] * 2,
         [((parts, slots // parts, width), F32), ((count, kv2), BF16)],
     )
     got_s = swap(sent_s, low)
@@ -723,39 +754,29 @@
     kv_right = (
         rows_of(2, 0, count), rows_of(3, 0, count), rows_of(4, 0, slots), rows_of(5, 0, slots),
     )
-    late_a, sent_a, late_b, sent_b = products(
+    late, *sent = products(
         [lined0, lined1, dkv, dkv_far, dmkv_all, dmkv_far],
-        [
-            (order_a, [(kv_left, kv_right, (0, kv2 // 2))]),
-            (order_b, [(kv_left, kv_right, (kv2 // 2, kv2))]),
-        ],
-    )
-    for pos in slot_bits[1:]:
-        half = (kept_s.shape[0] - 8) // 2
-        shared = kept_s[2 * half :] + got_s[2 * half :]
-        sent_s = jnp.concatenate([kept_s[half : 2 * half] + got_s[half : 2 * half], shared], axis=0)
-        kept_s = jnp.concatenate([kept_s[:half] + got_s[:half], shared], axis=0)
-        got_s = swap(sent_s, pos)
-    total = kept_s + got_s
+        [(order_a, spread, [(kv_left, kv_right, (0, kv2))])],
+    )
+    mine_s, *sent_s = [
+        kept_s[t * step : (t + 1) * step] + got_s[t * step : (t + 1) * step]
+        for t in range(spread)
+    ]
+    total = sum(direct(sent_s), mine_s)
     for pos in order_a[meet:]:
         total = total + swap(total, pos)
-    slot_rows = total[:-8]
-    for pos in reversed(slot_bits):
-        slot_far = swap(slot_rows, pos)
-        if pos != low:
-            slot_rows = jnp.concatenate([slot_rows, slot_far], axis=0)
-    late_a = halved(late_a, sent_a, order_a[:meet])
-    late_b = halved(late_b, sent_b, order_b[:meet])
-    late, got = halved(*joined([late_a, late_b]), order_a[meet:])
+    near = jnp.concatenate([total, *direct([total] * (spread - 1))], axis=0)
+    far = swap(near, low)
+    late, got = halved(*split_sum([late, *direct(sent)]), order_a[meet:])
     g_kv = late + got
-    g_query, g_out, g_small, g_mem = call(
+    g_query, g_out, g_gain, g_gate, g_mem = call(
         last_kernel,
         [key, me],
         [
-            slot_rows, slot_far, total, sn, query_weight, memory_init, gain, vector,
+            near, far, sn, query_weight, memory_init, gain, vector,
             early_kept, early_got, out_kept, out_got,
         ],
-        [((height, width), F32), ((height, width), F32), ((16, height), F32), ((slots, height), F32)],
+        [((height, width), F32)] * 2 + [((1, height), F32)] * 2 + [((height, slots), F32)],
         [((parts, slots // parts, width), F32), ((devices, height, 2 * slots), F32)],
     )
     return (
@@ -764,9 +785,9 @@
         g_kv[:, : kv2 // 2],
         g_kv[:, kv2 // 2 :],
         g_out,
-        g_small[8],
-        g_small[2],
-        g_mem,
+        g_gain[0],
+        g_gate[0],
+        g_mem.T,
     )
 
 

time: 181 us -> 189 us (1.044)
  waiting for transfers between devices: 40.4 us -> 53.6 us
  local copies, waits for them, and re-layouts: 10.3 us -> 6.82 us
  starting transfers between devices: 53.4 us -> 50.7 us
    ppermute x0 -> x12, waiting for transfers between devices: none -> 26.7 us  [direct(): lax.ppermute(part, ('chain', 'dp'), [(i, i ^ mask) for i in range(devices)])]
    ppermute x34 -> x22, starting transfers between devices: 35.1 us -> 19 us  [swap(): lax.ppermute(rows, ('chain', 'dp'), [(i, i ^ 1 << pos) for i in range(dev...]
    ppermute x0 -> x12, starting transfers between devices: none -> 13.6 us  [direct(): lax.ppermute(part, ('chain', 'dp'), [(i, i ^ mask) for i in range(devices)])]
    ppermute x34 -> x22, waiting for transfers between devices: 24.9 us -> 16.5 us  [swap(): lax.ppermute(rows, ('chain', 'dp'), [(i, i ^ 1 << pos) for i in range(dev...]
    ppermute x2, waiting for transfers between devices: 7.95 us -> 0.89 us  [handed(): lax.ppermute(rows, 'chain', [(b, a) if back else (a, b) for a, b in pairs])]
    add x5 -> x4, other arithmetic: 0.08 us -> 4.02 us  [the longest x2 3.3 us: split_sum(): sum((part[:half] for part in parts))]
    add x15 -> x7, other arithmetic: 7.33 us -> 3.42 us  [fold(): return (kept[:half] + got[:half], kept[half:] + got[half:])]
    unnamed x45 -> x40, local copies, waits for them, and re-layouts: 7.68 us -> 5.43 us
  transfers between devices with their start and end apart: 39 -> 39, of which waited for: 14 -> 13; matrix products, arithmetic and copies ran while one was open for 6% -> 5% of each run, Pallas kernels for 24% -> 25%
where the time goes in v2:
time: 189 us; the launch traced here: 188 us
  Pallas kernels  56.1 us (30%)
  waiting for transfers between devices  53.6 us (28%)
  starting transfers between devices  50.7 us (27%)
  blocking collectives  10.5 us (6%)
  other arithmetic  8.93 us (5%)
  local copies, waits for them, and re-layouts  6.82 us (4%)
    pallas_call x14, Pallas kernels, call(): pl.pallas_call(kernel, out_shape=tuple((jax.ShapeDtypeStruct(shape, kind)...  56.1 us
    ppermute x12, waiting for transfers between devices, direct(): lax.ppermute(part, ('chain', 'dp'), [(i, i ^ mask) for i in range(devices)])  26.7 us
    ppermute x22, starting transfers between devices, swap(): lax.ppermute(rows, ('chain', 'dp'), [(i, i ^ 1 << pos) for i in range(dev...  19 us
    ppermute x22, waiting for transfers between devices, swap(): lax.ppermute(rows, ('chain', 'dp'), [(i, i ^ 1 << pos) for i in range(dev...  16.5 us
    ppermute x12, starting transfers between devices, direct(): lax.ppermute(part, ('chain', 'dp'), [(i, i ^ mask) for i in range(devices)])  13.6 us
    all_to_all x3, starting transfers between devices, trade(): lax.all_to_all(blocks, 'chain', 0, 0, axis_index_groups=halves, tiled=True)  12.4 us
    all_to_all x1, blocking collectives, trade(): lax.all_to_all(blocks, 'chain', 0, 0, axis_index_groups=halves, tiled=True)  10.5 us
    all_to_all x3, waiting for transfers between devices, trade(): lax.all_to_all(blocks, 'chain', 0, 0, axis_index_groups=halves, tiled=True)  9.61 us
  transfers between devices with their start and end apart: 39, of which 13 were waited for; matrix products, arithmetic and copies ran while one was open for 5% of the time, Pallas kernels for 25%

profile of v2, /device:TPU:0, one launch (start us, length us, event | category | flops | bytes accessed | tf_op | source)
XLA Modules:
  0.0 188.3 jit_solution(17865365189466941852)
XLA Ops:
  1.3 4.6 %shard_map.170 = (bf16[128,1024]{1,0:T(8,128)(2,1)}, bf16[128,512]{1,0:T(8,128)(2,1)}, bf16[128,1024]{1,0:T(8,128)(2,1)}, bf16[128,1024]{1,0:T(8,128)(2,1)}, f32[128,1024]{1,0:T(8,128)}) custom-call(s32[1,1]{1,0:T(1,128)S(6)} %copy.20.length, bf16[128,1024]{1,0:T(8,128)(2,1)} %bitcast.23, bf16[1024,1024]{1,0:T(8,128)(2,1)} %wq.5, bf16[1024,256]{1,0:T(8,128)(2,1)} %wk.7, ...), custom_call_target="tpu_custom_call" | custom-call | tf_op jit(solution)/shard_map/pallas_call | solution.py:480
  5.9 5.3 %all-to-all-start = ((f32[8,16,1024]{2,1,0:T(8,128)}), f32[8,16,1024]{2,1,0:T(8,128)S(1)}, u32[]{:S(2)}, u32[]{:S(2)}) async-start(f32[8,16,1024]{2,1,0:T(8,128)} %bitcast.35), calls=%async_computation | async-start | bytes 1048576 | tf_op jit(solution)/shard_map/all_to_all | solution.py:601
  11.1 3.5 %shard_map.171 = (f32[256,1024]{1,0:T(8,128)}, f32[1,1024]{1,0:T(1,128)}) custom-call(s32[1,1]{1,0:T(1,128)S(6)} %copy.20.length, bf16[128,1024]{1,0:T(8,128)(2,1)} %bitcast.24, bf16[128,1024]{1,0:T(8,128)(2,1)} %bitcast.31, bf16[1024,1024]{1,0:T(8,128)(2,1)} %wo.9, f32[1,1024]{1,0:T(1,128)} %bitcast.39, f32[1,1024]{1,0:T(1,128)} %bitcast.43), custom_call_target="tpu_custom_call" | custom-call | tf_op jit(solution)/shard_map/pallas_call | solution.py:480
  15.8 4.1 %all-to-all-done = f32[8,16,1024]{2,1,0:T(8,128)S(1)} async-done(((f32[8,16,1024]{2,1,0:T(8,128)}), f32[8,16,1024]{2,1,0:T(8,128)S(1)}, u32[]{:S(2)}, u32[]{:S(2)}) %all-to-all-start) | async-done | bytes 524320 | tf_op jit(solution)/shard_map/all_to_all | solution.py:601
  20.8 2.2 %shard_map.172 = (f32[128,1024]{1,0:T(8,128)}, f32[2,128,128]{2,1,0:T(8,128)}, f32[16,1152]{1,0:T(8,128)}) custom-call(f32[128,1024]{1,0:T(8,128)} %bitcast.21, f32[16,1]{1,0:T(8,128)} %copy.19.bias, f32[1,1024]{1,0:T(1,128)} %get-tuple-element.58.u), custom_call_target="tpu_custom_call" | custom-call | tf_op jit(solution)/shard_map/pallas_call | solution.py:480
  23.0 4.5 %collective-permute-start = (f32[16,1152]{1,0:T(8,128)}, f32[16,1152]{1,0:T(8,128)S(1)}, u32[]{:S(2)}, u32[]{:S(2)}) collective-permute-start(f32[16,1152]{1,0:T(8,128)} %get-tuple-element.61), channel_id=1, source_target_pairs={{0,16},{2,18},{4,20},{6,22},{8,24},{10,26},{12,28},{14,30},{1,17},... | collective-permute-start | bytes 221192 | tf_op jit(solution)/shard_map/ppermute | solution.py:607
  27.5 1.4 dynamic-slice_convert_fusion.mem_own
  30.4 3.9 %shard_map.173 = (f32[256,1024]{1,0:T(8,128)}, f32[128,1024]{1,0:T(8,128)}, f32[2,128,128]{2,1,0:T(8,128)}, f32[128,512]{1,0:T(8,128)}) custom-call(f32[128,1024]{1,0:T(8,128)} %get-tuple-element.59.p_in, f32[2,128,128]{2,1,0:T(8,128)} %get-tuple-element.60.stat.ret, f32[16,1152]{1,0:T(8,128)} %copy-done.19, f32[16,1024]{1,0:T(8,128)} %dynamic-slice_convert_fusion.mem_own, ...), custom_call_target="tpu_custom_call" | custom-call | tf_op jit(solution)/shard_map/pallas_call | solution.py:480
  34.3 10.5 %all_to_all.44 = f32[8,16,512]{2,1,0:T(8,128)} all-to-all(f32[8,16,512]{2,1,0:T(8,128)} %bitcast.37), channel_id=1, replica_groups={{0,2,4,6,8,10,12,14},{16,18,20,22,24,26,28,30},{1,3,5,7,9,11,13,15},{17..., dimensions={0} | all-to-all | bytes 524288 | tf_op jit(solution)/shard_map/all_to_all | solution.py:601
  44.8 6.4 %shard_map.174 = (bf16[128,1024]{1,0:T(8,128)(2,1)}, f32[128,1024]{1,0:T(8,128)}, f32[128,1024]{1,0:T(8,128)}, f32[128,512]{1,0:T(8,128)}, f32[128,512]{1,0:T(8,128)}) custom-call(s32[1,1]{1,0:T(1,128)S(6)} %copy.20.length, bf16[128,1024]{1,0:T(8,128)(2,1)} %bitcast.25, bf16[128,1024]{1,0:T(8,128)(2,1)} %bitcast.32, bf16[128,1024]{1,0:T(8,128)(2,1)} %get-tuple-element.55.q, ...), custom_call_target="tpu_custom_call" | custom-call | tf_op jit(solution)/shard_map/pallas_call | solution.py:480
  51.1 3.4 %all-to-all-start.2 = ((f32[8,16,512]{2,1,0:T(8,128)}), f32[8,16,512]{2,1,0:T(8,128)S(1)}, u32[]{:S(2)}, u32[]{:S(2)}) async-start(f32[8,16,512]{2,1,0:T(8,128)} %bitcast.36), calls=%async_computation.2 | async-start | bytes 524288 | tf_op jit(solution)/shard_map/all_to_all | solution.py:601
  55.1 5.5 %all-to-all-done.2 = f32[8,16,512]{2,1,0:T(8,128)S(1)} async-done(((f32[8,16,512]{2,1,0:T(8,128)}), f32[8,16,512]{2,1,0:T(8,128)S(1)}, u32[]{:S(2)}, u32[]{:S(2)}) %all-to-all-start.2) | async-done | bytes 262176 | tf_op jit(solution)/shard_map/all_to_all | solution.py:601
  61.3 4.8 %shard_map.175 = (f32[128,1024]{1,0:T(8,128)}, f32[128,1024]{1,0:T(8,128)}, f32[2,128,128]{2,1,0:T(8,128)}, f32[16,1152]{1,0:T(8,128)}, f32[128,1024]{1,0:T(8,128)}, /*index=5*/f32[1,1024]{1,0:T(1,128)}) custom-call(s32[1,1]{1,0:T(1,128)} %bitcast.12.place, f32[128,512]{1,0:T(8,128)} %bitcast.27, f32[128,1024]{1,0:T(8,128)} %get-tuple-element.66.mem, ...), custom_call_target="tpu_custom_call" | custom-call | tf_op jit(solution)/shard_map/pallas_call | solution.py:480
  66.1 1.3 collective-permute-start.1
  68.4 2.6 %shard_map.178.refs_0_ = bf16[512,256]{1,0:T(8,128)(2,1)} custom-call(s32[1,1]{1,0:T(1,128)} %bitcast.11.me, f32[256,1024]{1,0:T(8,128)} %get-tuple-element.80.refs_0_.refs_3_, f32[256,1024]{1,0:T(8,128)} %copy-done.2), custom_call_target="tpu_custom_call" | custom-call | tf_op jit(solution)/shard_map/pallas_call | solution.py:480
  71.5 2.8 %shard_map.179 = (f32[128,1024]{1,0:T(8,128)}, f32[128,1024]{1,0:T(8,128)}, f32[128,1024]{1,0:T(8,128)}, f32[128,1024]{1,0:T(8,128)}) custom-call(s32[1,1]{1,0:T(1,128)} %bitcast.11.me, bf16[512,256]{1,0:T(8,128)(2,1)} %shard_map.178.refs_0_, f32[128,1024]{1,0:T(8,128)} %get-tuple-element.74.dq.refs_1_, f32[128,1024]{1,0:T(8,128)} %collective-permute-done.13.refs_2_), custom_call_target="tpu_custom_call" | custom-call | tf_op jit(solution)/shard_map/pallas_call | solution.py:480
  74.3 1.4 collective-permute-start.14
  75.8 1.5 collective-permute-start.15
  77.8 3.8 %shard_map.176 = (f32[128,1024]{1,0:T(8,128)}, f32[3,1024]{1,0:T(4,128)}) custom-call(f32[128,1024]{1,0:T(8,128)} %get-tuple-element.68.later, f32[2,128,128]{2,1,0:T(8,128)} %get-tuple-element.69.stat_b, f32[16,1152]{1,0:T(8,128)} %copy-done.18, f32[256,1024]{1,0:T(8,128)} %get-tuple-element.71.both.refs_0_, f32[128,1024]{1,0:T(8,128)} %bitcast.22, ...), custom_call_target="tpu_custom_call" | custom-call | tf_op jit(solution)/shard_map/pallas_call | solution.py:480
  81.6 3.7 %all-to-all-start.3 = ((f32[8,16,1024]{2,1,0:T(8,128)}), f32[8,16,1024]{2,1,0:T(8,128)S(1)}, u32[]{:S(2)}, u32[]{:S(2)}) async-start(f32[8,16,1024]{2,1,0:T(8,128)} %bitcast.34), calls=%async_computation.3 | async-start | bytes 1048576 | tf_op jit(solution)/shard_map/all_to_all | solution.py:601
  85.3 3.0 %shard_map.180.refs_2_.refs_1_ = bf16[512,512]{1,0:T(8,128)(2,1)} custom-call(s32[1,1]{1,0:T(1,128)} %bitcast.11.me, f32[256,1024]{1,0:T(8,128)} %get-tuple-element.71.both.refs_0_, f32[256,1024]{1,0:T(8,128)} %copy-done.7), custom_call_target="tpu_custom_call" | custom-call | tf_op jit(solution)/shard_map/pallas_call | solution.py:480
  88.3 5.0 %shard_map.181 = (f32[256,512]{1,0:T(8,128)}, f32[256,512]{1,0:T(8,128)}, f32[256,640]{1,0:T(8,128)}, f32[256,640]{1,0:T(8,128)}) custom-call(s32[1,1]{1,0:T(1,128)} %bitcast.11.me, f32[128,1024]{1,0:T(8,128)} %get-tuple-element.85.refs_0_, f32[128,1024]{1,0:T(8,128)} %copy-done.10, bf16[512,512]{1,0:T(8,128)(2,1)} %shard_map.180.refs_2_.refs_1_, ...), custom_call_target="tpu_custom_call" | custom-call | tf_op jit(solution)/shard_map/pallas_call | solution.py:480
  93.4 1.5 collective-permute-start.23
  94.9 9.6 %collective-permute-done.16 = f32[128,1024]{1,0:T(8,128)} collective-permute-done((f32[128,1024]{1,0:T(8,128)}, f32[128,1024]{1,0:T(8,128)}, u32[]{:S(2)}, u32[]{:S(2)}) %collective-permute-start.16) | collective-permute-done | bytes 524320 | tf_op jit(solution)/shard_map/ppermute | solution.py:575
  104.5 2.2 %slice_add_fusion.7 = (f32[64,1024]{1,0:T(8,128)S(1)}, f32[64,1024]{1,0:T(8,128)}) fusion(f32[128,1024]{1,0:T(8,128)} %collective-permute-done.16, f32[128,1024]{1,0:T(8,128)} %collective-permute-done.15, f32[128,1024]{1,0:T(8,128)} %collective-permute-done.14, f32[128,1024]{1,0:T(8,128)S(1)} %copy-done.11), kind=kLoop, calls=%fused_computation.11 | loop fusion | flops 393216 | bytes 2621440 | tf_op jit(solution)/shard_map/add | solution.py:583
  106.7 1.4 collective-permute-start.17
  109.5 6.8 %shard_map.177 = (f32[128,512]{1,0:T(8,128)}, f32[96,1024]{1,0:T(8,128)}, f32[96,1024]{1,0:T(8,128)}) custom-call(s32[1,1]{1,0:T(1,128)} %bitcast.10.key, s32[1,1]{1,0:T(1,128)S(6)} %copy.20.length, bf16[128,1024]{1,0:T(8,128)(2,1)} %bitcast.26, bf16[128,1024]{1,0:T(8,128)(2,1)} %get-tuple-element.64.s, bf16[128,512]{1,0:T(8,128)(2,1)} %get-tuple-element.56.kv, ...), custom_call_target="tpu_custom_call" | custom-call | tf_op jit(solution)/shard_map/pallas_call | solution.py:480
  116.7 1.7 slice_add_fusion.21
  119.4 1.4 collective-permute-start.24
  122.2 3.8 %collective-permute-done.25 = f32[256,640]{1,0:T(8,128)S(1)} collective-permute-done((f32[256,640]{1,0:T(8,128)}, f32[256,640]{1,0:T(8,128)S(1)}, u32[]{:S(2)}, u32[]{:S(2)}) %collective-permute-start.25) | collective-permute-done | bytes 655392 | tf_op jit(solution)/shard_map/ppermute | solution.py:562
  126.7 2.6 %shard_map.183 = (f32[128,512]{1,0:T(8,128)}, f32[128,512]{1,0:T(8,128)}, f32[128,512]{1,0:T(8,128)}, f32[128,512]{1,0:T(8,128)}) custom-call(s32[1,1]{1,0:T(1,128)} %bitcast.11.me, bf16[512,256]{1,0:T(8,128)(2,1)} %shard_map.178.refs_0_, bf16[512,512]{1,0:T(8,128)(2,1)} %shard_map.180.refs_2_.refs_1_, f32[128,512]{1,0:T(8,128)} %get-tuple-element.93.refs_2_, ...), custom_call_target="tpu_custom_call" | custom-call | tf_op jit(solution)/shard_map/pallas_call | solution.py:480
  130.4 2.4 %collective-permute-start.33 = (f32[128,512]{1,0:T(8,128)}, f32[128,512]{1,0:T(8,128)S(1)}, u32[]{:S(2)}, u32[]{:S(2)}) collective-permute-start(f32[128,512]{1,0:T(8,128)} %get-tuple-element.97), channel_id=1, source_target_pairs={{0,5},{1,4},{2,7},{3,6},{4,1},{5,0},{6,3},{7,2},{8,13},{9,12},{10,... | collective-permute-start | bytes 786440 | tf_op jit(solution)/shard_map/ppermute | solution.py:575
  133.6 1.2 collective-permute-start.5
  134.9 12.2 %collective-permute-done.4 = f32[24,1024]{1,0:T(8,128)S(1)} collective-permute-done((f32[24,1024]{1,0:T(8,128)}, f32[24,1024]{1,0:T(8,128)S(1)}, u32[]{:S(2)}, u32[]{:S(2)}) %collective-permute-start.4) | collective-permute-done | bytes 98336 | tf_op jit(solution)/shard_map/ppermute | solution.py:575
  147.1 3.5 %collective-permute-start.18 = (f32[32,1024]{1,0:T(8,128)S(1)}, f32[32,1024]{1,0:T(8,128)S(1)}, u32[]{:S(2)}, u32[]{:S(2)}) collective-permute-start(f32[32,1024]{1,0:T(8,128)S(1)} %copy-done.17), channel_id=1, source_target_pairs={{0,16},{1,17},{2,18},{3,19},{4,20},{5,21},{6,22},{7,23},{8,24},{9,... | collective-permute-start | bytes 393224 | tf_op jit(solution)/shard_map/ppermute | solution.py:562
  150.7 2.1 %collective-permute-start.6 = (f32[24,1024]{1,0:T(8,128)S(1)}, f32[24,1024]{1,0:T(8,128)S(1)}, u32[]{:S(2)}, u32[]{:S(2)}) collective-permute-start(f32[24,1024]{1,0:T(8,128)S(1)} %fusion.4), channel_id=1, source_target_pairs={{0,8},{1,9},{2,10},{3,11},{4,12},{5,13},{6,14},{7,15},{8,0},{9,1},... | collective-permute-start | bytes 294920 | tf_op jit(solution)/shard_map/ppermute | solution.py:562
  152.7 1.1 slice_add_fusion.16
  153.9 3.8 %collective-permute-done.26 = f32[128,640]{1,0:T(8,128)S(1)} collective-permute-done((f32[128,640]{1,0:T(8,128)S(1)}, f32[128,640]{1,0:T(8,128)S(1)}, u32[]{:S(2)}, u32[]{:S(2)}) %collective-permute-start.26) | collective-permute-done | bytes 327712 | tf_op jit(solution)/shard_map/ppermute | solution.py:562
  157.8 1.7 collective-permute-start.7
  159.5 1.6 collective-permute-start.35
  161.1 1.8 collective-permute-start.27
  163.6 2.8 %collective-permute-start.10 = (f32[24,1024]{1,0:T(8,128)S(1)}, f32[24,1024]{1,0:T(8,128)S(1)}, u32[]{:S(2)}, u32[]{:S(2)}) collective-permute-start(f32[24,1024]{1,0:T(8,128)S(1)} %add.138), channel_id=1, source_target_pairs={{0,5},{1,4},{2,7},{3,6},{4,1},{5,0},{6,3},{7,2},{8,13},{9,12},{10,... | collective-permute-start | bytes 294920 | tf_op jit(solution)/shard_map/ppermute | solution.py:575
  166.4 1.5 collective-permute-start.8
  167.9 1.4 collective-permute-done.10
  169.3 2.3 %collective-permute-done.8 = f32[24,1024]{1,0:T(8,128)S(1)} collective-permute-done((f32[24,1024]{1,0:T(8,128)S(1)}, f32[24,1024]{1,0:T(8,128)S(1)}, u32[]{:S(2)}, u32[]{:S(2)}) %collective-permute-start.8) | collective-permute-done | bytes 98336 | tf_op jit(solution)/shard_map/ppermute | solution.py:575
  173.4 1.2 collective-permute-start.28
  175.2 8.2 %collective-permute-done.28.got_out = f32[32,1152]{1,0:T(8,128)S(1)} collective-permute-done((f32[32,1152]{1,0:T(8,128)S(1)}, f32[32,1152]{1,0:T(8,128)S(1)}, u32[]{:S(2)}, u32[]{:S(2)}) %collective-permute-start.28) | collective-permute-done | bytes 147488 | tf_op jit(solution)/shard_map/ppermute | solution.py:562
  184.1 4.2 %shard_map.182 = (f32[32,1024]{1,0:T(8,128)}, f32[32,1024]{1,0:T(8,128)}, f32[1,32]{1,0:T(1,128)}, f32[1,32]{1,0:T(1,128)}, f32[32,128]{1,0:T(8,128)}) custom-call(s32[1,1]{1,0:T(1,128)} %bitcast.10.key, s32[1,1]{1,0:T(1,128)} %bitcast.11.me, f32[96,1024]{1,0:T(8,128)} %copy-done.6, f32[96,1024]{1,0:T(8,128)} %copy-done.13, ...), custom_call_target="tpu_custom_call" | custom-call | tf_op jit(solution)/shard_map/pallas_call | solution.py:480
  (105 shorter events, 17.9 us)
Async XLA Ops:
  0.6 14.5 %copy-start = (f32[128]{0:T(128)S(1)}, f32[128]{0:T(128)}, u32[]{:S(2)}) copy-start(f32[128]{0:T(128)} %param.19) | copy-start | bytes 1540
  5.9 14.1 %all-to-all-start = ((f32[8,16,1024]{2,1,0:T(8,128)}), f32[8,16,1024]{2,1,0:T(8,128)S(1)}, u32[]{:S(2)}, u32[]{:S(2)}) async-start(f32[8,16,1024]{2,1,0:T(8,128)} %bitcast.35), calls=%async_computation | async-start | bytes 1048576 | tf_op jit(solution)/shard_map/all_to_all | solution.py:601
  14.6 52.8 %collective-permute-start.12 = (f32[256,1024]{1,0:T(8,128)}, f32[256,1024]{1,0:T(8,128)S(1)}, u32[]{:S(2)}, u32[]{:S(2)}) collective-permute-start(f32[256,1024]{1,0:T(8,128)} %get-tuple-element.80.refs_0_.refs_3_), channel_id=1, source_target_pairs={{0,2},{1,3},{2,0},{3,1},{4,6},{5,7},{6,4},{7,5},{8,10},{9,11},{10,... | collective-permute-start | bytes 3145736 | tf_op jit(solution)/shard_map/ppermute | solution.py:562
  23.0 6.8 %collective-permute-start = (f32[16,1152]{1,0:T(8,128)}, f32[16,1152]{1,0:T(8,128)S(1)}, u32[]{:S(2)}, u32[]{:S(2)}) collective-permute-start(f32[16,1152]{1,0:T(8,128)} %get-tuple-element.61), channel_id=1, source_target_pairs={{0,16},{2,18},{4,20},{6,22},{8,24},{10,26},{12,28},{14,30},{1,17},... | collective-permute-start | bytes 221192 | tf_op jit(solution)/shard_map/ppermute | solution.py:607
  34.3 43.0 %collective-permute-start.20 = (f32[256,1024]{1,0:T(8,128)}, f32[256,1024]{1,0:T(8,128)S(1)}, u32[]{:S(2)}, u32[]{:S(2)}) collective-permute-start(f32[256,1024]{1,0:T(8,128)} %get-tuple-element.71.both.refs_0_), channel_id=1, source_target_pairs={{0,2},{1,3},{2,0},{3,1},{4,6},{5,7},{6,4},{7,5},{8,10},{9,11},{10,... | collective-permute-start | bytes 3145736 | tf_op jit(solution)/shard_map/ppermute | solution.py:562
  51.1 9.5 %all-to-all-start.2 = ((f32[8,16,512]{2,1,0:T(8,128)}), f32[8,16,512]{2,1,0:T(8,128)S(1)}, u32[]{:S(2)}, u32[]{:S(2)}) async-start(f32[8,16,512]{2,1,0:T(8,128)} %bitcast.36), calls=%async_computation.2 | async-start | bytes 524288 | tf_op jit(solution)/shard_map/all_to_all | solution.py:601
  54.5 16.4 %collective-permute-start.13 = (f32[128,1024]{1,0:T(8,128)}, f32[128,1024]{1,0:T(8,128)}, u32[]{:S(2)}, u32[]{:S(2)}) collective-permute-start(f32[128,1024]{1,0:T(8,128)} %get-tuple-element.74.dq.refs_1_), channel_id=1, source_target_pairs={{0,2},{1,3},{2,0},{3,1},{4,6},{5,7},{6,4},{7,5},{8,10},{9,11},{10,... | collective-permute-start | bytes 1572872 | tf_op jit(solution)/shard_map/ppermute | solution.py:562
  54.9 19.4 %collective-permute-start.19 = (f32[128,1024]{1,0:T(8,128)}, f32[128,1024]{1,0:T(8,128)S(1)}, u32[]{:S(2)}, u32[]{:S(2)}) collective-permute-start(f32[128,1024]{1,0:T(8,128)} %get-tuple-element.85.refs_0_), channel_id=1, source_target_pairs={{0,2},{1,3},{2,0},{3,1},{4,6},{5,7},{6,4},{7,5},{8,10},{9,11},{10,... | collective-permute-start | bytes 1572872 | tf_op jit(solution)/shard_map/ppermute | solution.py:562
  66.1 9.7 %collective-permute-start.1 = (f32[16,1152]{1,0:T(8,128)}, f32[16,1152]{1,0:T(8,128)S(1)}, u32[]{:S(2)}, u32[]{:S(2)}) collective-permute-start(f32[16,1152]{1,0:T(8,128)} %get-tuple-element.70), channel_id=1, source_target_pairs={{16,0},{18,2},{20,4},{22,6},{24,8},{26,10},{28,12},{30,14},{17,1},... | collective-permute-start | bytes 221192 | tf_op jit(solution)/shard_map/ppermute | solution.py:607
  71.0 17.4 %collective-permute-start.21 = (f32[128,1024]{1,0:T(8,128)}, f32[128,1024]{1,0:T(8,128)}, u32[]{:S(2)}, u32[]{:S(2)}) collective-permute-start(f32[128,1024]{1,0:T(8,128)} %get-tuple-element.86.refs_5_), channel_id=1, source_target_pairs={{0,2},{1,3},{2,0},{3,1},{4,6},{5,7},{6,4},{7,5},{8,10},{9,11},{10,... | collective-permute-start | bytes 1572872 | tf_op jit(solution)/shard_map/ppermute | solution.py:562
  71.0 17.4 %collective-permute-start.22 = (f32[128,1024]{1,0:T(8,128)}, f32[128,1024]{1,0:T(8,128)}, u32[]{:S(2)}, u32[]{:S(2)}) collective-permute-start(f32[128,1024]{1,0:T(8,128)} %get-tuple-element.87.refs_7_), channel_id=1, source_target_pairs={{0,2},{1,3},{2,0},{3,1},{4,6},{5,7},{6,4},{7,5},{8,10},{9,11},{10,... | collective-permute-start | bytes 1572872 | tf_op jit(solution)/shard_map/ppermute | solution.py:562
  74.3 7.3 %copy-start.10 = (f32[128,1024]{1,0:T(8,128)}, f32[128,1024]{1,0:T(8,128)S(1)}, u32[]{:S(2)}) copy-start(f32[128,1024]{1,0:T(8,128)S(1)} %collective-permute-done.19.refs_1_) | copy-start | bytes 1572868
  74.3 20.6 %collective-permute-start.14 = (f32[128,1024]{1,0:T(8,128)}, f32[128,1024]{1,0:T(8,128)}, u32[]{:S(2)}, u32[]{:S(2)}) collective-permute-start(f32[128,1024]{1,0:T(8,128)} %get-tuple-element.82), channel_id=1, source_target_pairs={{0,4},{1,5},{2,6},{3,7},{4,0},{5,1},{6,2},{7,3},{8,12},{9,13},{10,... | collective-permute-start | bytes 1572872 | tf_op jit(solution)/shard_map/ppermute | solution.py:575
  75.8 19.1 %collective-permute-start.15 = (f32[128,1024]{1,0:T(8,128)}, f32[128,1024]{1,0:T(8,128)}, u32[]{:S(2)}, u32[]{:S(2)}) collective-permute-start(f32[128,1024]{1,0:T(8,128)} %get-tuple-element.83), channel_id=1, source_target_pairs={{0,1},{1,0},{2,3},{3,2},{4,5},{5,4},{6,7},{7,6},{8,9},{9,8},{10,11... | collective-permute-start | bytes 1572872 | tf_op jit(solution)/shard_map/ppermute | solution.py:575
  77.3 27.2 %collective-permute-start.16 = (f32[128,1024]{1,0:T(8,128)}, f32[128,1024]{1,0:T(8,128)}, u32[]{:S(2)}, u32[]{:S(2)}) collective-permute-start(f32[128,1024]{1,0:T(8,128)} %get-tuple-element.84), channel_id=1, source_target_pairs={{0,5},{1,4},{2,7},{3,6},{4,1},{5,0},{6,3},{7,2},{8,13},{9,12},{10,... | collective-permute-start | bytes 1572872 | tf_op jit(solution)/shard_map/ppermute | solution.py:575
  81.6 27.1 %all-to-all-start.3 = ((f32[8,16,1024]{2,1,0:T(8,128)}), f32[8,16,1024]{2,1,0:T(8,128)S(1)}, u32[]{:S(2)}, u32[]{:S(2)}) async-start(f32[8,16,1024]{2,1,0:T(8,128)} %bitcast.34), calls=%async_computation.3 | async-start | bytes 1048576 | tf_op jit(solution)/shard_map/all_to_all | solution.py:601
  88.3 16.2 %copy-start.11 = (f32[128,1024]{1,0:T(8,128)S(1)}, f32[128,1024]{1,0:T(8,128)}, u32[]{:S(2)}) copy-start(f32[128,1024]{1,0:T(8,128)} %get-tuple-element.81) | copy-start | bytes 1572868
  93.4 14.7 %copy-start.4 = (f32[8,16,512]{2,1,0:T(8,128)S(1)}, f32[8,16,512]{2,1,0:T(8,128)}, u32[]{:S(2)}) copy-start(f32[8,16,512]{2,1,0:T(8,128)} %copy-done.3) | copy-start | bytes 786436
  93.4 25.3 %collective-permute-start.23 = (f32[256,512]{1,0:T(8,128)}, f32[256,512]{1,0:T(8,128)S(1)}, u32[]{:S(2)}, u32[]{:S(2)}) collective-permute-start(f32[256,512]{1,0:T(8,128)} %get-tuple-element.89), channel_id=1, source_target_pairs={{0,1},{1,0},{2,3},{3,2},{4,5},{5,4},{6,7},{7,6},{8,9},{9,8},{10,11... | collective-permute-start | bytes 1572872 | tf_op jit(solution)/shard_map/ppermute | solution.py:562
  106.7 9.9 %collective-permute-start.17 = (f32[64,1024]{1,0:T(8,128)}, f32[64,1024]{1,0:T(8,128)}, u32[]{:S(2)}, u32[]{:S(2)}) collective-permute-start(f32[64,1024]{1,0:T(8,128)} %get-tuple-element.103), channel_id=1, source_target_pairs={{0,8},{1,9},{2,10},{3,11},{4,12},{5,13},{6,14},{7,15},{8,0},{9,1},... | collective-permute-start | bytes 786440 | tf_op jit(solution)/shard_map/ppermute | solution.py:562
  108.1 17.9 %collective-permute-start.30 = (f32[128,512]{1,0:T(8,128)S(1)}, f32[128,512]{1,0:T(8,128)S(1)}, u32[]{:S(2)}, u32[]{:S(2)}) collective-permute-start(f32[128,512]{1,0:T(8,128)S(1)} %bitcast.29), channel_id=1, source_target_pairs={{0,2},{1,3},{2,0},{3,1},{4,6},{5,7},{6,4},{7,5},{8,10},{9,11},{10,... | collective-permute-start | bytes 786440 | tf_op jit(solution)/shard_map/ppermute | solution.py:562
  108.1 17.8 %collective-permute-start.25 = (f32[256,640]{1,0:T(8,128)}, f32[256,640]{1,0:T(8,128)S(1)}, u32[]{:S(2)}, u32[]{:S(2)}) collective-permute-start(f32[256,640]{1,0:T(8,128)} %get-tuple-element.91), channel_id=1, source_target_pairs={{0,4},{1,5},{2,6},{3,7},{4,0},{5,1},{6,2},{7,3},{8,12},{9,13},{10,... | collective-permute-start | bytes 1966088 | tf_op jit(solution)/shard_map/ppermute | solution.py:562
  109.5 9.1 %copy-start.9 = (f32[256,512]{1,0:T(8,128)S(1)}, f32[256,512]{1,0:T(8,128)}, u32[]{:S(2)}) copy-start(f32[256,512]{1,0:T(8,128)} %get-tuple-element.88) | copy-start | bytes 1572868
  116.3 9.6 %copy-start.8 = (f32[256,640]{1,0:T(8,128)S(1)}, f32[256,640]{1,0:T(8,128)}, u32[]{:S(2)}) copy-start(f32[256,640]{1,0:T(8,128)} %get-tuple-element.90) | copy-start | bytes 1966084
  116.3 4.5 %collective-permute-start.2 = (f32[96,1024]{1,0:T(8,128)}, f32[96,1024]{1,0:T(8,128)S(1)}, u32[]{:S(2)}, u32[]{:S(2)}) collective-permute-start(f32[96,1024]{1,0:T(8,128)} %get-tuple-element.78), channel_id=1, source_target_pairs={{0,2},{1,3},{2,0},{3,1},{4,6},{5,7},{6,4},{7,5},{8,10},{9,11},{10,... | collective-permute-start | bytes 1179656 | tf_op jit(solution)/shard_map/ppermute | solution.py:562
  118.4 7.6 %collective-permute-start.29 = (f32[128,512]{1,0:T(8,128)}, f32[128,512]{1,0:T(8,128)}, u32[]{:S(2)}, u32[]{:S(2)}) collective-permute-start(f32[128,512]{1,0:T(8,128)} %get-tuple-element.93.refs_2_), channel_id=1, source_target_pairs={{0,2},{1,3},{2,0},{3,1},{4,6},{5,7},{6,4},{7,5},{8,10},{9,11},{10,... | collective-permute-start | bytes 786440 | tf_op jit(solution)/shard_map/ppermute | solution.py:562
  119.4 13.4 %collective-permute-start.24 = (f32[128,512]{1,0:T(8,128)}, f32[128,512]{1,0:T(8,128)S(1)}, u32[]{:S(2)}, u32[]{:S(2)}) collective-permute-start(f32[128,512]{1,0:T(8,128)} %get-tuple-element.109), channel_id=1, source_target_pairs={{0,4},{1,5},{2,6},{3,7},{4,0},{5,1},{6,2},{7,3},{8,12},{9,13},{10,... | collective-permute-start | bytes 786440 | tf_op jit(solution)/shard_map/ppermute | solution.py:562
  121.6 12.1 %collective-permute-start.3 = (f32[24,1024]{1,0:T(8,128)}, f32[24,1024]{1,0:T(8,128)S(1)}, u32[]{:S(2)}, u32[]{:S(2)}) collective-permute-start(f32[24,1024]{1,0:T(8,128)} %get-tuple-element.110), channel_id=1, source_target_pairs={{0,4},{1,5},{2,6},{3,7},{4,0},{5,1},{6,2},{7,3},{8,12},{9,13},{10,... | collective-permute-start | bytes 294920 | tf_op jit(solution)/shard_map/ppermute | solution.py:575
  125.9 21.2 %copy-start.17 = (f32[32,1024]{1,0:T(8,128)S(1)}, f32[32,1024]{1,0:T(8,128)}, u32[]{:S(2)}) copy-start(f32[32,1024]{1,0:T(8,128)} %get-tuple-element.119) | copy-start | bytes 393220
  129.3 21.3 %collective-permute-start.31 = (f32[128,512]{1,0:T(8,128)}, f32[128,512]{1,0:T(8,128)S(1)}, u32[]{:S(2)}, u32[]{:S(2)}) collective-permute-start(f32[128,512]{1,0:T(8,128)} %get-tuple-element.95), channel_id=1, source_target_pairs={{0,4},{1,5},{2,6},{3,7},{4,0},{5,1},{6,2},{7,3},{8,12},{9,13},{10,... | collective-permute-start | bytes 786440 | tf_op jit(solution)/shard_map/ppermute | solution.py:575
  129.9 22.8 %collective-permute-start.32 = (f32[128,512]{1,0:T(8,128)}, f32[128,512]{1,0:T(8,128)S(1)}, u32[]{:S(2)}, u32[]{:S(2)}) collective-permute-start(f32[128,512]{1,0:T(8,128)} %get-tuple-element.96), channel_id=1, source_target_pairs={{0,1},{1,0},{2,3},{3,2},{4,5},{5,4},{6,7},{7,6},{8,9},{9,8},{10,11... | collective-permute-start | bytes 786440 | tf_op jit(solution)/shard_map/ppermute | solution.py:575
  130.4 22.3 %collective-permute-start.33 = (f32[128,512]{1,0:T(8,128)}, f32[128,512]{1,0:T(8,128)S(1)}, u32[]{:S(2)}, u32[]{:S(2)}) collective-permute-start(f32[128,512]{1,0:T(8,128)} %get-tuple-element.97), channel_id=1, source_target_pairs={{0,5},{1,4},{2,7},{3,6},{4,1},{5,0},{6,3},{7,2},{8,13},{9,12},{10,... | collective-permute-start | bytes 786440 | tf_op jit(solution)/shard_map/ppermute | solution.py:575
  132.8 14.2 %collective-permute-start.4 = (f32[24,1024]{1,0:T(8,128)}, f32[24,1024]{1,0:T(8,128)S(1)}, u32[]{:S(2)}, u32[]{:S(2)}) collective-permute-start(f32[24,1024]{1,0:T(8,128)} %get-tuple-element.112), channel_id=1, source_target_pairs={{0,1},{1,0},{2,3},{3,2},{4,5},{5,4},{6,7},{7,6},{8,9},{9,8},{10,11... | collective-permute-start | bytes 294920 | tf_op jit(solution)/shard_map/ppermute | solution.py:575
  133.6 17.0 %collective-permute-start.5 = (f32[24,1024]{1,0:T(8,128)S(1)}, f32[24,1024]{1,0:T(8,128)S(1)}, u32[]{:S(2)}, u32[]{:S(2)}) collective-permute-start(f32[24,1024]{1,0:T(8,128)S(1)} %get-tuple-element.111), channel_id=1, source_target_pairs={{0,5},{1,4},{2,7},{3,6},{4,1},{5,0},{6,3},{7,2},{8,13},{9,12},{10,... | collective-permute-start | bytes 294920 | tf_op jit(solution)/shard_map/ppermute | solution.py:575
  147.1 28.1 %collective-permute-start.18 = (f32[32,1024]{1,0:T(8,128)S(1)}, f32[32,1024]{1,0:T(8,128)S(1)}, u32[]{:S(2)}, u32[]{:S(2)}) collective-permute-start(f32[32,1024]{1,0:T(8,128)S(1)} %copy-done.17), channel_id=1, source_target_pairs={{0,16},{1,17},{2,18},{3,19},{4,20},{5,21},{6,22},{7,23},{8,24},{9,... | collective-permute-start | bytes 393224 | tf_op jit(solution)/shard_map/ppermute | solution.py:562
  150.6 7.1 %collective-permute-start.26 = (f32[128,640]{1,0:T(8,128)S(1)}, f32[128,640]{1,0:T(8,128)S(1)}, u32[]{:S(2)}, u32[]{:S(2)}) collective-permute-start(f32[128,640]{1,0:T(8,128)S(1)} %get-tuple-element.105), channel_id=1, source_target_pairs={{0,1},{1,0},{2,3},{3,2},{4,5},{5,4},{6,7},{7,6},{8,9},{9,8},{10,11... | collective-permute-start | bytes 983048 | tf_op jit(solution)/shard_map/ppermute | solution.py:562
  150.7 7.1 %collective-permute-start.6 = (f32[24,1024]{1,0:T(8,128)S(1)}, f32[24,1024]{1,0:T(8,128)S(1)}, u32[]{:S(2)}, u32[]{:S(2)}) collective-permute-start(f32[24,1024]{1,0:T(8,128)S(1)} %fusion.4), channel_id=1, source_target_pairs={{0,8},{1,9},{2,10},{3,11},{4,12},{5,13},{6,14},{7,15},{8,0},{9,1},... | collective-permute-start | bytes 294920 | tf_op jit(solution)/shard_map/ppermute | solution.py:562
  153.8 5.7 %collective-permute-start.34 = (f32[64,512]{1,0:T(8,128)S(1)}, f32[64,512]{1,0:T(8,128)S(1)}, u32[]{:S(2)}, u32[]{:S(2)}) collective-permute-start(f32[64,512]{1,0:T(8,128)S(1)} %get-tuple-element.107), channel_id=1, source_target_pairs={{0,8},{1,9},{2,10},{3,11},{4,12},{5,13},{6,14},{7,15},{8,0},{9,1},... | collective-permute-start | bytes 393224 | tf_op jit(solution)/shard_map/ppermute | solution.py:562
  157.8 5.8 %collective-permute-start.7 = (f32[24,1024]{1,0:T(8,128)S(1)}, f32[24,1024]{1,0:T(8,128)S(1)}, u32[]{:S(2)}, u32[]{:S(2)}) collective-permute-start(f32[24,1024]{1,0:T(8,128)S(1)} %add.137), channel_id=1, source_target_pairs={{0,16},{1,17},{2,18},{3,19},{4,20},{5,21},{6,22},{7,23},{8,24},{9,... | collective-permute-start | bytes 294920 | tf_op jit(solution)/shard_map/ppermute | solution.py:562
  159.5 8.4 %collective-permute-start.35 = (f32[32,512]{1,0:T(8,128)S(1)}, f32[32,512]{1,0:T(8,128)S(1)}, u32[]{:S(2)}, u32[]{:S(2)}) collective-permute-start(f32[32,512]{1,0:T(8,128)S(1)} %slice_add_fusion.27), channel_id=1, source_target_pairs={{0,16},{1,17},{2,18},{3,19},{4,20},{5,21},{6,22},{7,23},{8,24},{9,... | collective-permute-start | bytes 196616 | tf_op jit(solution)/shard_map/ppermute | solution.py:562
  161.1 11.6 %collective-permute-start.27 = (f32[64,1152]{1,0:T(8,128)S(1)}, f32[64,1152]{1,0:T(8,128)S(1)}, u32[]{:S(2)}, u32[]{:S(2)}) collective-permute-start(f32[64,1152]{1,0:T(8,128)S(1)} %pad_maximum_fusion.1), channel_id=1, source_target_pairs={{0,8},{1,9},{2,10},{3,11},{4,12},{5,13},{6,14},{7,15},{8,0},{9,1},... | collective-permute-start | bytes 884744 | tf_op jit(solution)/shard_map/ppermute | solution.py:562
  163.6 5.7 %collective-permute-start.10 = (f32[24,1024]{1,0:T(8,128)S(1)}, f32[24,1024]{1,0:T(8,128)S(1)}, u32[]{:S(2)}, u32[]{:S(2)}) collective-permute-start(f32[24,1024]{1,0:T(8,128)S(1)} %add.138), channel_id=1, source_target_pairs={{0,5},{1,4},{2,7},{3,6},{4,1},{5,0},{6,3},{7,2},{8,13},{9,12},{10,... | collective-permute-start | bytes 294920 | tf_op jit(solution)/shard_map/ppermute | solution.py:575
  166.4 5.1 %collective-permute-start.8 = (f32[24,1024]{1,0:T(8,128)S(1)}, f32[24,1024]{1,0:T(8,128)S(1)}, u32[]{:S(2)}, u32[]{:S(2)}) collective-permute-start(f32[24,1024]{1,0:T(8,128)S(1)} %add.138), channel_id=1, source_target_pairs={{0,4},{1,5},{2,6},{3,7},{4,0},{5,1},{6,2},{7,3},{8,12},{9,13},{10,... | collective-permute-start | bytes 294920 | tf_op jit(solution)/shard_map/ppermute | solution.py:575
  167.9 4.6 %collective-permute-start.9 = (f32[24,1024]{1,0:T(8,128)S(1)}, f32[24,1024]{1,0:T(8,128)S(1)}, u32[]{:S(2)}, u32[]{:S(2)}) collective-permute-start(f32[24,1024]{1,0:T(8,128)S(1)} %add.138), channel_id=1, source_target_pairs={{0,1},{1,0},{2,3},{3,2},{4,5},{5,4},{6,7},{7,6},{8,9},{9,8},{10,11... | collective-permute-start | bytes 294920 | tf_op jit(solution)/shard_map/ppermute | solution.py:575
  172.6 10.8 %copy-start.6 = (f32[96,1024]{1,0:T(8,128)}, f32[96,1024]{1,0:T(8,128)S(1)}, u32[]{:S(2)}) copy-start(f32[96,1024]{1,0:T(8,128)S(1)} %pad_maximum_fusion.near) | copy-start | bytes 1179652
  172.6 10.8 %collective-permute-start.11 = (f32[96,1024]{1,0:T(8,128)S(1)}, f32[96,1024]{1,0:T(8,128)S(1)}, u32[]{:S(2)}, u32[]{:S(2)}) collective-permute-start(f32[96,1024]{1,0:T(8,128)S(1)} %pad_maximum_fusion.near), channel_id=1, source_target_pairs={{0,2},{1,3},{2,0},{3,1},{4,6},{5,7},{6,4},{7,5},{8,10},{9,11},{10,... | collective-permute-start | bytes 1179656 | tf_op jit(solution)/shard_map/ppermute | solution.py:562
  173.4 9.9 %collective-permute-start.28 = (f32[32,1152]{1,0:T(8,128)S(1)}, f32[32,1152]{1,0:T(8,128)S(1)}, u32[]{:S(2)}, u32[]{:S(2)}) collective-permute-start(f32[32,1152]{1,0:T(8,128)S(1)} %get-tuple-element.115), channel_id=1, source_target_pairs={{0,16},{1,17},{2,18},{3,19},{4,20},{5,21},{6,22},{7,23},{8,24},{9,... | collective-permute-start | bytes 442376 | tf_op jit(solution)/shard_map/ppermute | solution.py:562
  175.2 8.2 %copy-start.16 = (f32[32,1024]{1,0:T(8,128)}, f32[32,1024]{1,0:T(8,128)S(1)}, u32[]{:S(2)}) copy-start(f32[32,1024]{1,0:T(8,128)S(1)} %collective-permute-done.18.got) | copy-start | bytes 393220
  (11 other events, 17.1 us)

commit v3 on v2

--- a/solution.py
+++ b/solution.py
@@ -225,7 +225,7 @@
 
 def back_scan_kernel(
     place, dmkv, mem, ret, stat, mem_own, wo, wk, wv, gain,
-    r_o, later_o, stat_o, end_o, g0_o, gain_o, *, count,
+    r_o, later_o, stat_o, end_o, g0_o, *, count,
 ):
     rows, width = mem.shape
     own = rows // count
@@ -235,7 +235,6 @@
     inverse = stat[1][:, :1]
     keep = stat[0][:, :1]
     memory = mem[...]
-    gain_o[...] = jnp.sum(dmn * memory * inverse, axis=0, keepdims=True)
     scaled = dmn * gain[...]
     inner = jnp.sum(scaled * memory, axis=1, keepdims=True) * (1.0 / width)
     r = inverse * scaled - memory * (inverse * inverse * inverse * inner)
@@ -267,7 +266,7 @@
     end_o[:, width:] = later_q
 
 
-def back_kernel(later, stat_b, handed, both, call, ret, stat, u, wo, gain_g, dc_o, vec_o, *, count):
+def back_kernel(later, stat_b, handed, both, call, ret, stat, u, wo, dc_o, vec_o, *, count):
     rows, width = later.shape
     passed = stat_b[1][:, :1]
     ahead = later[...] + passed * tiled(handed[:, :width], count)
@@ -280,19 +279,18 @@
     dz = d_retain * retain * (1.0 - retain)
     dc_o[...] = (1.0 - retain) * ahead + dz * u[...]
     v = jnp.sum(dz * context, axis=0, keepdims=True)
-    vec_o[0:1, :] = gain_g[...]
-    vec_o[1:2, :] = v
-    vec_o[2:3, :] = row_times(v, wo[...], False)
+    vec_o[0:1, :] = v
+    vec_o[1:2, :] = row_times(v, wo[...], False)
 
 
 def finish_kernel(
-    key, length, seg, s, kv, dc, dq, dkv_r, wq, wk, wv, vec,
-    dkv_o, keep_o, send_o, dqs_s, dkv_s,
+    key, length, s, kv, dc, dkv_r, vec,
+    dkv_o, keep_o, send_o, dqs_s,
 ):
-    count, width = seg.shape
+    count, width = kv.shape[0], s.shape[1]
     slots = s.shape[0]
     pieces, piece, _ = dqs_s.shape
-    kv_width = wk.shape[1]
+    kv_width = kv.shape[1] // 2
     pairs = width // LANES
     groups = kv_width // HEAD
     allowed = lax.broadcasted_iota(jnp.int32, (count, slots), 0) < length[0, 0]
@@ -326,15 +324,10 @@
             lanes = slice(side + tile * LANES, side + (tile + 1) * LANES)
             total = (parts[2 * tile] + parts[2 * tile + 1]).astype(BF16).astype(F32)
             total = (total + dkv_r[:, lanes]).astype(BF16)
-            dkv_s[:, lanes] = total
             dkv_o[:, lanes] = total.astype(F32)
-    dxn = mm_nt(dq[...].astype(BF16), wq[...])
-    dxn = dxn + mm_nt(dkv_s[:, :kv_width], wk[...]) + mm_nt(dkv_s[:, kv_width:], wv[...])
-    rows = seg[...].astype(F32)
-    gain_here = jnp.sum(dxn * (rows * inverse_rms(rows)), axis=0, keepdims=True)
     step = piece + 8
     sums = jnp.concatenate(
-        [vec[0:1, :] + gain_here, vec[1:3, :], jnp.zeros((5, width), F32)], axis=0
+        [vec[...], jnp.zeros((6, width), F32)], axis=0
     )
     for t in range(pieces // 2):
         at = slice(t * step, t * step + piece)
@@ -345,8 +338,9 @@
 
 
 def last_kernel(
-    key, me, near, far, sn, wq, mem0, gain, vector, kept, got, kept_out, got_out,
-    query_o, out_o, gain_o, gate_o, mem_o, dqs_s, turn_s,
+    key, me, near, far, sn, wq, mem0, gain, vector, kept, got, kept_out, got_out, kept_kv, got_kv,
+    wq_rows, wk_rows, wv_rows,
+    query_o, out_o, key_o, value_o, gain_o, gate_o, mem_o, dqs_s, turn_s,
 ):
     slots, width = sn.shape
     pieces, piece, _ = dqs_s.shape
@@ -360,17 +354,26 @@
     for b in range(width // height):
         turn_s[b, :, :slots] = turned[b * height : (b + 1) * height]
     rows = turn_s[me[0, 0], :, :slots].astype(BF16)
-    query_o[...] = kept[...] + got[...] + mm(rows, d_slots)
+    d_query = kept[...] + got[...] + mm(rows, d_slots)
+    query_o[...] = d_query
+    kv_width = key_o.shape[1]
+    d_kv = kept_kv[...] + got_kv[...]
+    key_o[...] = d_kv[:, :kv_width]
+    value_o[...] = d_kv[:, kv_width:]
+    scaled_gain = (
+        jnp.sum(d_query * wq_rows[...].astype(F32), axis=1, keepdims=True)
+        + jnp.sum(d_kv[:, :kv_width] * wk_rows[...].astype(F32), axis=1, keepdims=True)
+        + jnp.sum(d_kv[:, kv_width:] * wv_rows[...].astype(F32), axis=1, keepdims=True)
+    )
     dsn = mm_nt(d_slots, wq[...])
     start = mem0[...].astype(F32)
     inverse = inverse_rms(start)
-    gain_row = jnp.sum(dsn * (start * inverse), axis=0, keepdims=True)
     scaled = dsn * gain[...]
     inner = jnp.sum(scaled * start, axis=1, keepdims=True) * (1.0 / width)
     d_start = inverse * scaled - start * (inverse * inverse * inverse * inner)
     sums = near[piece : piece + 8]
     small = jnp.concatenate(
-        [sums, sums[0:1] + gain_row, jnp.zeros((slots - 9, width), F32)], axis=0
+        [sums, gain[...], jnp.zeros((slots - 9, width), F32)], axis=0
     )
     columns = jnp.concatenate([d_start, small], axis=0).T
     for b in range(width // height):
@@ -378,13 +381,14 @@
     mine = turn_s[me[0, 0]]
     held = kept_out[:, width:] + got_out[:, width:]
     mem_o[...] = mine[:, :slots] + held
-    across = mine[:, slots:].T
-    gain_o[...] = across[8:9]
-    gate_o[...] = across[2:3]
+    lane = lax.broadcasted_iota(jnp.int32, (height, slots), 1)
+    across = jnp.where(lane == 0, scaled_gain / mine[:, slots + 8 : slots + 9], mine[:, slots:]).T
+    gain_o[...] = across[0:1]
+    gate_o[...] = across[1:2]
     out_o[...] = (
         kept_out[:, :width]
         + got_out[:, :width]
-        + mine[:, slots + 1 : slots + 2] * vector[...]
+        + mine[:, slots : slots + 1] * vector[...]
     )
 
 
@@ -693,7 +697,7 @@
     early, *sent = products([lined0, dq, dq_far], [(order_a, spread, [(*early_items, (0, width))])])
     early_far = direct(sent)
     early = split_sum([early, *early_far])
-    r, later, stat_b, end, g0, gain_g = call(
+    r, later, stat_b, end, g0 = call(
         functools.partial(back_scan_kernel, count=count_half),
         [mine.reshape(1, 1)],
         [dmkv_all, mem, ret, stat, mem_own, out_weight, key_weight, value_weight, gain],
@@ -703,7 +707,6 @@
             ((2, slots, LANES), F32),
             ((own, width + LANES), F32),
             ((slots, width), F32),
-            ((1, width), F32),
         ],
     )
     r_far = swap(r, low)
@@ -730,8 +733,8 @@
     dc, vec = call(
         functools.partial(back_kernel, count=count_half),
         [],
-        [later, stat_b, entering, pack1, c_all, ret, stat, u, out_weight, gain_g],
-        [((slots, width), F32), ((3, width), F32)],
+        [later, stat_b, entering, pack1, c_all, ret, stat, u, out_weight],
+        [((slots, width), F32), ((2, width), F32)],
     )
     dc_here = trade(dc)
     slot_bits = [low] + order_a[:meet]
@@ -744,9 +747,9 @@
     dkv, kept_s, sent_s = call(
         finish_kernel,
         [key, lengths],
-        [segment, s, kv, dc_here, dq, dkv_r, query_weight, key_weight, value_weight, vec],
+        [s, kv, dc_here, dkv_r, vec],
         [((count, kv2), F32)] + [((spread * step, width), F32)] * 2,
-        [((parts, slots // parts, width), F32), ((count, kv2), BF16)],
+        [((parts, slots // parts, width), F32)],
     )
     got_s = swap(sent_s, low)
     dkv_far = swap(dkv, low)
@@ -768,22 +771,28 @@
     near = jnp.concatenate([total, *direct([total] * (spread - 1))], axis=0)
     far = swap(near, low)
     late, got = halved(*split_sum([late, *direct(sent)]), order_a[meet:])
-    g_kv = late + got
-    g_query, g_out, g_gain, g_gate, g_mem = call(
+    first = me[0, 0] * height
+    own_rows = [
+        lax.dynamic_slice(weight, (first, 0), (height, weight.shape[1]))
+        for weight in (query_weight, key_weight, value_weight)
+    ]
+    g_query, g_out, g_key, g_value, g_gain, g_gate, g_mem = call(
         last_kernel,
         [key, me],
         [
             near, far, sn, query_weight, memory_init, gain, vector,
-            early_kept, early_got, out_kept, out_got,
+            early_kept, early_got, out_kept, out_got, late, got, *own_rows,
         ],
-        [((height, width), F32)] * 2 + [((1, height), F32)] * 2 + [((height, slots), F32)],
+        [((height, width), F32)] * 2
+        + [((height, kv2 // 2), F32)] * 2
+        + [((1, height), F32)] * 2 + [((height, slots), F32)],
         [((parts, slots // parts, width), F32), ((devices, height, 2 * slots), F32)],
     )
     return (
         out[None, None],
         g_query,
-        g_kv[:, : kv2 // 2],
-        g_kv[:, kv2 // 2 :],
+        g_key,
+        g_value,
         g_out,
         g_gain[0],
         g_gate[0],

time: 189 us -> 184 us (0.974)
  waiting for transfers between devices: 53.6 us -> 51.2 us
  Pallas kernels: 56.1 us -> 53.9 us
  starting transfers between devices: 50.7 us -> 48.5 us
    ppermute x12, waiting for transfers between devices: 26.7 us -> 17.1 us  [direct(): lax.ppermute(part, ('chain', 'dp'), [(i, i ^ mask) for i in range(devices)])]
    ppermute x22, waiting for transfers between devices: 16.5 us -> 23.5 us  [swap(): lax.ppermute(rows, ('chain', 'dp'), [(i, i ^ 1 << pos) for i in range(dev...]
    dynamic_slice x0 -> x2, local copies, waits for them, and re-layouts: none -> 2.8 us  [per_device(): lax.dynamic_slice(weight, (first, 0), (height, weight.shape[1]))]
    pallas_call x14, Pallas kernels: 56.1 us -> 53.9 us  [call(): pl.pallas_call(kernel, out_shape=tuple((jax.ShapeDtypeStruct(shape, kind)...]
    unnamed x40 -> x38, local copies, waits for them, and re-layouts: 5.43 us -> 4.8 us
  transfers between devices with their start and end apart: 39 -> 39, of which waited for: 13 -> 15; matrix products, arithmetic and copies ran while one was open for 5% -> 7% of each run, Pallas kernels for 25% -> 25%
where the time goes in v3:
time: 184 us; the launch traced here: 183 us
  Pallas kernels  53.9 us (29%)
  waiting for transfers between devices  51.2 us (28%)
  starting transfers between devices  48.5 us (26%)
  blocking collectives  10.5 us (6%)
  other arithmetic  8.62 us (5%)
  local copies, waits for them, and re-layouts  8.36 us (5%)
    pallas_call x14, Pallas kernels, call(): pl.pallas_call(kernel, out_shape=tuple((jax.ShapeDtypeStruct(shape, kind)...  53.9 us
    ppermute x22, waiting for transfers between devices, swap(): lax.ppermute(rows, ('chain', 'dp'), [(i, i ^ 1 << pos) for i in range(dev...  23.5 us
    ppermute x22, starting transfers between devices, swap(): lax.ppermute(rows, ('chain', 'dp'), [(i, i ^ 1 << pos) for i in range(dev...  17.2 us
    ppermute x12, waiting for transfers between devices, direct(): lax.ppermute(part, ('chain', 'dp'), [(i, i ^ mask) for i in range(devices)])  17.1 us
    ppermute x12, starting transfers between devices, direct(): lax.ppermute(part, ('chain', 'dp'), [(i, i ^ mask) for i in range(devices)])  13.2 us
    all_to_all x3, starting transfers between devices, trade(): lax.all_to_all(blocks, 'chain', 0, 0, axis_index_groups=halves, tiled=True)  12.4 us
    all_to_all x1, blocking collectives, trade(): lax.all_to_all(blocks, 'chain', 0, 0, axis_index_groups=halves, tiled=True)  10.5 us
    all_to_all x3, waiting for transfers between devices, trade(): lax.all_to_all(blocks, 'chain', 0, 0, axis_index_groups=halves, tiled=True)  9.61 us
  transfers between devices with their start and end apart: 39, of which 15 were waited for; matrix products, arithmetic and copies ran while one was open for 7% of the time, Pallas kernels for 25%

profile of v3, /device:TPU:0, one launch (start us, length us, event | category | flops | bytes accessed | tf_op | source)
XLA Modules:
  0.0 182.8 jit_solution(3530877329666817411)
XLA Ops:
  1.3 4.6 %shard_map.170 = (bf16[128,1024]{1,0:T(8,128)(2,1)}, bf16[128,512]{1,0:T(8,128)(2,1)}, bf16[128,1024]{1,0:T(8,128)(2,1)}, bf16[128,1024]{1,0:T(8,128)(2,1)}, f32[128,1024]{1,0:T(8,128)}) custom-call(s32[1,1]{1,0:T(1,128)S(6)} %copy.20.length, bf16[128,1024]{1,0:T(8,128)(2,1)} %bitcast.23, bf16[1024,1024]{1,0:T(8,128)(2,1)} %wq.3, bf16[1024,256]{1,0:T(8,128)(2,1)} %wk.5, ...), custom_call_target="tpu_custom_call" | custom-call | tf_op jit(solution)/shard_map/pallas_call | solution.py:484
  5.9 5.3 %all-to-all-start = ((f32[8,16,1024]{2,1,0:T(8,128)}), f32[8,16,1024]{2,1,0:T(8,128)S(1)}, u32[]{:S(2)}, u32[]{:S(2)}) async-start(f32[8,16,1024]{2,1,0:T(8,128)} %bitcast.34), calls=%async_computation | async-start | bytes 1048576 | tf_op jit(solution)/shard_map/all_to_all | solution.py:605
  11.1 3.5 %shard_map.171 = (f32[256,1024]{1,0:T(8,128)}, f32[1,1024]{1,0:T(1,128)}) custom-call(s32[1,1]{1,0:T(1,128)S(6)} %copy.20.length, bf16[128,1024]{1,0:T(8,128)(2,1)} %bitcast.24, bf16[128,1024]{1,0:T(8,128)(2,1)} %bitcast.30, bf16[1024,1024]{1,0:T(8,128)(2,1)} %wo.9, f32[1,1024]{1,0:T(1,128)} %bitcast.38, f32[1,1024]{1,0:T(1,128)} %bitcast.42), custom_call_target="tpu_custom_call" | custom-call | tf_op jit(solution)/shard_map/pallas_call | solution.py:484
  15.8 4.1 %all-to-all-done = f32[8,16,1024]{2,1,0:T(8,128)S(1)} async-done(((f32[8,16,1024]{2,1,0:T(8,128)}), f32[8,16,1024]{2,1,0:T(8,128)S(1)}, u32[]{:S(2)}, u32[]{:S(2)}) %all-to-all-start) | async-done | bytes 524320 | tf_op jit(solution)/shard_map/all_to_all | solution.py:605
  20.8 2.2 %shard_map.172 = (f32[128,1024]{1,0:T(8,128)}, f32[2,128,128]{2,1,0:T(8,128)}, f32[16,1152]{1,0:T(8,128)}) custom-call(f32[128,1024]{1,0:T(8,128)} %bitcast.21, f32[16,1]{1,0:T(8,128)} %copy.19.bias, f32[1,1024]{1,0:T(1,128)} %get-tuple-element.59.u), custom_call_target="tpu_custom_call" | custom-call | tf_op jit(solution)/shard_map/pallas_call | solution.py:484
  23.0 4.5 %collective-permute-start = (f32[16,1152]{1,0:T(8,128)}, f32[16,1152]{1,0:T(8,128)S(1)}, u32[]{:S(2)}, u32[]{:S(2)}) collective-permute-start(f32[16,1152]{1,0:T(8,128)} %get-tuple-element.62), channel_id=1, source_target_pairs={{0,16},{2,18},{4,20},{6,22},{8,24},{10,26},{12,28},{14,30},{1,17},... | collective-permute-start | bytes 221192 | tf_op jit(solution)/shard_map/ppermute | solution.py:611
  27.5 1.4 dynamic-slice_convert_fusion.mem_own
  30.4 3.9 %shard_map.173 = (f32[256,1024]{1,0:T(8,128)}, f32[128,1024]{1,0:T(8,128)}, f32[2,128,128]{2,1,0:T(8,128)}, f32[128,512]{1,0:T(8,128)}) custom-call(f32[128,1024]{1,0:T(8,128)} %get-tuple-element.60.p_in, f32[2,128,128]{2,1,0:T(8,128)} %get-tuple-element.61.stat.ret, f32[16,1152]{1,0:T(8,128)} %copy-done.17, f32[16,1024]{1,0:T(8,128)} %dynamic-slice_convert_fusion.mem_own, ...), custom_call_target="tpu_custom_call" | custom-call | tf_op jit(solution)/shard_map/pallas_call | solution.py:484
  34.3 10.5 %all_to_all.44 = f32[8,16,512]{2,1,0:T(8,128)} all-to-all(f32[8,16,512]{2,1,0:T(8,128)} %bitcast.36), channel_id=1, replica_groups={{0,2,4,6,8,10,12,14},{16,18,20,22,24,26,28,30},{1,3,5,7,9,11,13,15},{17..., dimensions={0} | all-to-all | bytes 524288 | tf_op jit(solution)/shard_map/all_to_all | solution.py:605
  44.8 6.4 %shard_map.174 = (bf16[128,1024]{1,0:T(8,128)(2,1)}, f32[128,1024]{1,0:T(8,128)}, f32[128,1024]{1,0:T(8,128)}, f32[128,512]{1,0:T(8,128)}, f32[128,512]{1,0:T(8,128)}) custom-call(s32[1,1]{1,0:T(1,128)S(6)} %copy.20.length, bf16[128,1024]{1,0:T(8,128)(2,1)} %bitcast.25, bf16[128,1024]{1,0:T(8,128)(2,1)} %bitcast.31, bf16[128,1024]{1,0:T(8,128)(2,1)} %get-tuple-element.56.q, ...), custom_call_target="tpu_custom_call" | custom-call | tf_op jit(solution)/shard_map/pallas_call | solution.py:484
  51.2 3.4 %all-to-all-start.2 = ((f32[8,16,512]{2,1,0:T(8,128)}), f32[8,16,512]{2,1,0:T(8,128)S(1)}, u32[]{:S(2)}, u32[]{:S(2)}) async-start(f32[8,16,512]{2,1,0:T(8,128)} %bitcast.35), calls=%async_computation.2 | async-start | bytes 524288 | tf_op jit(solution)/shard_map/all_to_all | solution.py:605
  55.2 5.5 %all-to-all-done.2 = f32[8,16,512]{2,1,0:T(8,128)S(1)} async-done(((f32[8,16,512]{2,1,0:T(8,128)}), f32[8,16,512]{2,1,0:T(8,128)S(1)}, u32[]{:S(2)}, u32[]{:S(2)}) %all-to-all-start.2) | async-done | bytes 262176 | tf_op jit(solution)/shard_map/all_to_all | solution.py:605
  61.3 4.7 %shard_map.175 = (f32[128,1024]{1,0:T(8,128)}, f32[128,1024]{1,0:T(8,128)}, f32[2,128,128]{2,1,0:T(8,128)}, f32[16,1152]{1,0:T(8,128)}, f32[128,1024]{1,0:T(8,128)}) custom-call(s32[1,1]{1,0:T(1,128)} %bitcast.12.place, f32[128,512]{1,0:T(8,128)} %bitcast.26, f32[128,1024]{1,0:T(8,128)} %get-tuple-element.67.mem, f32[2,128,128]{2,1,0:T(8,128)} %get-tuple-element.61.stat.ret, ...), custom_call_target="tpu_custom_call" | custom-call | tf_op jit(solution)/shard_map/pallas_call | solution.py:484
  66.0 1.3 collective-permute-start.1
  68.3 2.6 %shard_map.178.refs_0_ = bf16[512,256]{1,0:T(8,128)(2,1)} custom-call(s32[1,1]{1,0:T(1,128)} %bitcast.11.me, f32[256,1024]{1,0:T(8,128)} %get-tuple-element.79.refs_0_.refs_3_, f32[256,1024]{1,0:T(8,128)} %copy-done.2), custom_call_target="tpu_custom_call" | custom-call | tf_op jit(solution)/shard_map/pallas_call | solution.py:484
  71.5 2.8 %shard_map.179 = (f32[128,1024]{1,0:T(8,128)}, f32[128,1024]{1,0:T(8,128)}, f32[128,1024]{1,0:T(8,128)}, f32[128,1024]{1,0:T(8,128)}) custom-call(s32[1,1]{1,0:T(1,128)} %bitcast.11.me, bf16[512,256]{1,0:T(8,128)(2,1)} %shard_map.178.refs_0_, f32[128,1024]{1,0:T(8,128)} %get-tuple-element.80.refs_1_, f32[128,1024]{1,0:T(8,128)} %collective-permute-done.13.refs_2_), custom_call_target="tpu_custom_call" | custom-call | tf_op jit(solution)/shard_map/pallas_call | solution.py:484
  74.3 1.4 collective-permute-start.14
  75.7 1.5 collective-permute-start.15
  77.8 3.8 %shard_map.176 = (f32[128,1024]{1,0:T(8,128)}, f32[2,1024]{1,0:T(2,128)}) custom-call(f32[128,1024]{1,0:T(8,128)} %get-tuple-element.69.later, f32[2,128,128]{2,1,0:T(8,128)} %get-tuple-element.70.stat_b, f32[16,1152]{1,0:T(8,128)} %copy-done.16, f32[256,1024]{1,0:T(8,128)} %get-tuple-element.72.both.refs_0_, f32[128,1024]{1,0:T(8,128)} %bitcast.22, ...), custom_call_target="tpu_custom_call" | custom-call | tf_op jit(solution)/shard_map/pallas_call | solution.py:484
  81.6 3.7 %all-to-all-start.3 = ((f32[8,16,1024]{2,1,0:T(8,128)}), f32[8,16,1024]{2,1,0:T(8,128)S(1)}, u32[]{:S(2)}, u32[]{:S(2)}) async-start(f32[8,16,1024]{2,1,0:T(8,128)} %bitcast.33), calls=%async_computation.3 | async-start | bytes 1048576 | tf_op jit(solution)/shard_map/all_to_all | solution.py:605
  85.3 3.0 %shard_map.180.refs_2_.refs_1_ = bf16[512,512]{1,0:T(8,128)(2,1)} custom-call(s32[1,1]{1,0:T(1,128)} %bitcast.11.me, f32[256,1024]{1,0:T(8,128)} %get-tuple-element.72.both.refs_0_, f32[256,1024]{1,0:T(8,128)} %copy-done.7), custom_call_target="tpu_custom_call" | custom-call | tf_op jit(solution)/shard_map/pallas_call | solution.py:484
  88.3 5.0 %shard_map.181 = (f32[256,512]{1,0:T(8,128)}, f32[256,512]{1,0:T(8,128)}, f32[256,640]{1,0:T(8,128)}, f32[256,640]{1,0:T(8,128)}) custom-call(s32[1,1]{1,0:T(1,128)} %bitcast.11.me, f32[128,1024]{1,0:T(8,128)} %get-tuple-element.85.refs_0_, f32[128,1024]{1,0:T(8,128)} %copy-done.10, bf16[512,512]{1,0:T(8,128)(2,1)} %shard_map.180.refs_2_.refs_1_, ...), custom_call_target="tpu_custom_call" | custom-call | tf_op jit(solution)/shard_map/pallas_call | solution.py:484
  93.4 1.5 collective-permute-start.23
  94.9 9.6 %collective-permute-done.16 = f32[128,1024]{1,0:T(8,128)} collective-permute-done((f32[128,1024]{1,0:T(8,128)}, f32[128,1024]{1,0:T(8,128)}, u32[]{:S(2)}, u32[]{:S(2)}) %collective-permute-start.16) | collective-permute-done | bytes 524320 | tf_op jit(solution)/shard_map/ppermute | solution.py:579
  104.5 2.3 %slice_add_fusion.7 = (f32[64,1024]{1,0:T(8,128)S(1)}, f32[64,1024]{1,0:T(8,128)}) fusion(f32[128,1024]{1,0:T(8,128)} %collective-permute-done.16, f32[128,1024]{1,0:T(8,128)} %collective-permute-done.15, f32[128,1024]{1,0:T(8,128)} %collective-permute-done.14, f32[128,1024]{1,0:T(8,128)S(1)} %copy-done.11), kind=kLoop, calls=%fused_computation.11 | loop fusion | flops 393216 | bytes 2621440 | tf_op jit(solution)/shard_map/add | solution.py:587
  106.8 1.4 collective-permute-start.17
  108.7 1.5 constant_dynamic-slice_fusion.2.wq_rows
  110.2 3.3 %collective-permute-done.17 = f32[64,1024]{1,0:T(8,128)} collective-permute-done((f32[64,1024]{1,0:T(8,128)}, f32[64,1024]{1,0:T(8,128)}, u32[]{:S(2)}, u32[]{:S(2)}) %collective-permute-start.17) | collective-permute-done | bytes 262176 | tf_op jit(solution)/shard_map/ppermute | solution.py:566
  113.5 1.7 slice_add_fusion.21
  115.2 3.5 %collective-permute-start.18 = (f32[32,1024]{1,0:T(8,128)}, f32[32,1024]{1,0:T(8,128)}, u32[]{:S(2)}, u32[]{:S(2)}) collective-permute-start(f32[32,1024]{1,0:T(8,128)} %get-tuple-element.121), channel_id=1, source_target_pairs={{0,16},{1,17},{2,18},{3,19},{4,20},{5,21},{6,22},{7,23},{8,24},{9,... | collective-permute-start | bytes 393224 | tf_op jit(solution)/shard_map/ppermute | solution.py:566
  119.6 4.7 %shard_map.177 = (f32[128,512]{1,0:T(8,128)}, f32[96,1024]{1,0:T(8,128)}, f32[96,1024]{1,0:T(8,128)}) custom-call(s32[1,1]{1,0:T(1,128)} %bitcast.10.key, s32[1,1]{1,0:T(1,128)S(6)} %copy.20.length, bf16[128,1024]{1,0:T(8,128)(2,1)} %get-tuple-element.65.s, bf16[128,512]{1,0:T(8,128)(2,1)} %get-tuple-element.57.kv, f32[128,1024]{1,0:T(8,128)} %bitcast.29, ...), custom_call_target="tpu_custom_call" | custom-call | tf_op jit(solution)/shard_map/pallas_call | solution.py:484
  125.5 1.4 collective-permute-start.24
  128.3 2.6 %shard_map.182 = (f32[128,512]{1,0:T(8,128)}, f32[128,512]{1,0:T(8,128)}, f32[128,512]{1,0:T(8,128)}, f32[128,512]{1,0:T(8,128)}) custom-call(s32[1,1]{1,0:T(1,128)} %bitcast.11.me, bf16[512,256]{1,0:T(8,128)(2,1)} %shard_map.178.refs_0_, bf16[512,512]{1,0:T(8,128)(2,1)} %shard_map.180.refs_2_.refs_1_, f32[128,512]{1,0:T(8,128)} %get-tuple-element.92.refs_2_, ...), custom_call_target="tpu_custom_call" | custom-call | tf_op jit(solution)/shard_map/pallas_call | solution.py:484
  131.6 1.5 collective-permute-start.4
  133.2 1.7 collective-permute-done.24
  136.5 1.4 collective-permute-start.31
  137.9 3.7 %collective-permute-done.4 = f32[24,1024]{1,0:T(8,128)S(1)} collective-permute-done((f32[24,1024]{1,0:T(8,128)S(1)}, f32[24,1024]{1,0:T(8,128)S(1)}, u32[]{:S(2)}, u32[]{:S(2)}) %collective-permute-start.4) | collective-permute-done | bytes 98336 | tf_op jit(solution)/shard_map/ppermute | solution.py:579
  143.0 2.1 %collective-permute-start.6 = (f32[24,1024]{1,0:T(8,128)S(1)}, f32[24,1024]{1,0:T(8,128)S(1)}, u32[]{:S(2)}, u32[]{:S(2)}) collective-permute-start(f32[24,1024]{1,0:T(8,128)S(1)} %fusion.4), channel_id=1, source_target_pairs={{0,8},{1,9},{2,10},{3,11},{4,12},{5,13},{6,14},{7,15},{8,0},{9,1},... | collective-permute-start | bytes 294920 | tf_op jit(solution)/shard_map/ppermute | solution.py:566
  145.2 2.6 %collective-permute-done.6 = f32[24,1024]{1,0:T(8,128)S(1)} collective-permute-done((f32[24,1024]{1,0:T(8,128)S(1)}, f32[24,1024]{1,0:T(8,128)S(1)}, u32[]{:S(2)}, u32[]{:S(2)}) %collective-permute-start.6) | collective-permute-done | bytes 98336 | tf_op jit(solution)/shard_map/ppermute | solution.py:566
  148.2 5.1 %collective-permute-done.7 = f32[24,1024]{1,0:T(8,128)S(1)} collective-permute-done((f32[24,1024]{1,0:T(8,128)S(1)}, f32[24,1024]{1,0:T(8,128)S(1)}, u32[]{:S(2)}, u32[]{:S(2)}) %collective-permute-start.7) | collective-permute-done | bytes 98336 | tf_op jit(solution)/shard_map/ppermute | solution.py:566
  153.3 3.2 %collective-permute-start.27 = (f32[64,1152]{1,0:T(8,128)S(1)}, f32[64,1152]{1,0:T(8,128)S(1)}, u32[]{:S(2)}, u32[]{:S(2)}) collective-permute-start(f32[64,1152]{1,0:T(8,128)S(1)} %pad_maximum_fusion.1), channel_id=1, source_target_pairs={{0,8},{1,9},{2,10},{3,11},{4,12},{5,13},{6,14},{7,15},{8,0},{9,1},... | collective-permute-start | bytes 884744 | tf_op jit(solution)/shard_map/ppermute | solution.py:566
  156.6 1.2 collective-permute-start.10
  157.8 1.3 collective-permute-start.8
  160.2 1.9 %collective-permute-done.10 = f32[24,1024]{1,0:T(8,128)S(1)} collective-permute-done((f32[24,1024]{1,0:T(8,128)S(1)}, f32[24,1024]{1,0:T(8,128)S(1)}, u32[]{:S(2)}, u32[]{:S(2)}) %collective-permute-start.10) | collective-permute-done | bytes 98336 | tf_op jit(solution)/shard_map/ppermute | solution.py:579
  164.5 2.6 %collective-permute-done.34 = f32[64,512]{1,0:T(8,128)S(1)} collective-permute-done((f32[64,512]{1,0:T(8,128)S(1)}, f32[64,512]{1,0:T(8,128)S(1)}, u32[]{:S(2)}, u32[]{:S(2)}) %collective-permute-start.34) | collective-permute-done | bytes 131104 | tf_op jit(solution)/shard_map/ppermute | solution.py:566
  168.1 1.3 constant_dynamic-slice_fusion
  169.4 8.1 %collective-permute-done.35.got_kv = f32[32,512]{1,0:T(8,128)S(1)} collective-permute-done((f32[32,512]{1,0:T(8,128)S(1)}, f32[32,512]{1,0:T(8,128)S(1)}, u32[]{:S(2)}, u32[]{:S(2)}) %collective-permute-start.35) | collective-permute-done | bytes 65568 | tf_op jit(solution)/shard_map/ppermute | solution.py:566
  178.4 4.2 %shard_map.183 = (f32[32,1024]{1,0:T(8,128)}, f32[32,1024]{1,0:T(8,128)}, f32[32,256]{1,0:T(8,128)}, f32[32,256]{1,0:T(8,128)}, f32[1,32]{1,0:T(1,128)}, /*index=5*/f32[1,32]{1,0:T(1,128)}, f32[32,128]{1,0:T(8,128)}) custom-call(s32[1,1]{1,0:T(1,128)} %bitcast.10.key, s32[1,1]{1,0:T(1,128)} %bitcast.11.me, f32[96,1024]{1,0:T(8,128)} %copy-done.6, ...), custom_call_target="tpu_custom_call" | custom-call | tf_op jit(solution)/shard_map/pallas_call | solution.py:484
  (103 shorter events, 20.5 us)
Async XLA Ops:
  0.6 14.5 %copy-start = (f32[128]{0:T(128)S(1)}, f32[128]{0:T(128)}, u32[]{:S(2)}) copy-start(f32[128]{0:T(128)} %param.19) | copy-start | bytes 1540
  5.9 14.1 %all-to-all-start = ((f32[8,16,1024]{2,1,0:T(8,128)}), f32[8,16,1024]{2,1,0:T(8,128)S(1)}, u32[]{:S(2)}, u32[]{:S(2)}) async-start(f32[8,16,1024]{2,1,0:T(8,128)} %bitcast.34), calls=%async_computation | async-start | bytes 1048576 | tf_op jit(solution)/shard_map/all_to_all | solution.py:605
  14.6 52.8 %collective-permute-start.12 = (f32[256,1024]{1,0:T(8,128)}, f32[256,1024]{1,0:T(8,128)S(1)}, u32[]{:S(2)}, u32[]{:S(2)}) collective-permute-start(f32[256,1024]{1,0:T(8,128)} %get-tuple-element.79.refs_0_.refs_3_), channel_id=1, source_target_pairs={{0,2},{1,3},{2,0},{3,1},{4,6},{5,7},{6,4},{7,5},{8,10},{9,11},{10,... | collective-permute-start | bytes 3145736 | tf_op jit(solution)/shard_map/ppermute | solution.py:566
  23.0 6.8 %collective-permute-start = (f32[16,1152]{1,0:T(8,128)}, f32[16,1152]{1,0:T(8,128)S(1)}, u32[]{:S(2)}, u32[]{:S(2)}) collective-permute-start(f32[16,1152]{1,0:T(8,128)} %get-tuple-element.62), channel_id=1, source_target_pairs={{0,16},{2,18},{4,20},{6,22},{8,24},{10,26},{12,28},{14,30},{1,17},... | collective-permute-start | bytes 221192 | tf_op jit(solution)/shard_map/ppermute | solution.py:611
  34.3 42.9 %collective-permute-start.20 = (f32[256,1024]{1,0:T(8,128)}, f32[256,1024]{1,0:T(8,128)S(1)}, u32[]{:S(2)}, u32[]{:S(2)}) collective-permute-start(f32[256,1024]{1,0:T(8,128)} %get-tuple-element.72.both.refs_0_), channel_id=1, source_target_pairs={{0,2},{1,3},{2,0},{3,1},{4,6},{5,7},{6,4},{7,5},{8,10},{9,11},{10,... | collective-permute-start | bytes 3145736 | tf_op jit(solution)/shard_map/ppermute | solution.py:566
  51.2 9.5 %all-to-all-start.2 = ((f32[8,16,512]{2,1,0:T(8,128)}), f32[8,16,512]{2,1,0:T(8,128)S(1)}, u32[]{:S(2)}, u32[]{:S(2)}) async-start(f32[8,16,512]{2,1,0:T(8,128)} %bitcast.35), calls=%async_computation.2 | async-start | bytes 524288 | tf_op jit(solution)/shard_map/all_to_all | solution.py:605
  54.6 16.4 %collective-permute-start.13 = (f32[128,1024]{1,0:T(8,128)}, f32[128,1024]{1,0:T(8,128)}, u32[]{:S(2)}, u32[]{:S(2)}) collective-permute-start(f32[128,1024]{1,0:T(8,128)} %get-tuple-element.80.refs_1_), channel_id=1, source_target_pairs={{0,2},{1,3},{2,0},{3,1},{4,6},{5,7},{6,4},{7,5},{8,10},{9,11},{10,... | collective-permute-start | bytes 1572872 | tf_op jit(solution)/shard_map/ppermute | solution.py:566
  55.0 19.3 %collective-permute-start.19 = (f32[128,1024]{1,0:T(8,128)}, f32[128,1024]{1,0:T(8,128)S(1)}, u32[]{:S(2)}, u32[]{:S(2)}) collective-permute-start(f32[128,1024]{1,0:T(8,128)} %get-tuple-element.85.refs_0_), channel_id=1, source_target_pairs={{0,2},{1,3},{2,0},{3,1},{4,6},{5,7},{6,4},{7,5},{8,10},{9,11},{10,... | collective-permute-start | bytes 1572872 | tf_op jit(solution)/shard_map/ppermute | solution.py:566
  66.0 9.7 %collective-permute-start.1 = (f32[16,1152]{1,0:T(8,128)}, f32[16,1152]{1,0:T(8,128)S(1)}, u32[]{:S(2)}, u32[]{:S(2)}) collective-permute-start(f32[16,1152]{1,0:T(8,128)} %get-tuple-element.71), channel_id=1, source_target_pairs={{16,0},{18,2},{20,4},{22,6},{24,8},{26,10},{28,12},{30,14},{17,1},... | collective-permute-start | bytes 221192 | tf_op jit(solution)/shard_map/ppermute | solution.py:611
  70.9 17.4 %collective-permute-start.21 = (f32[128,1024]{1,0:T(8,128)}, f32[128,1024]{1,0:T(8,128)}, u32[]{:S(2)}, u32[]{:S(2)}) collective-permute-start(f32[128,1024]{1,0:T(8,128)} %get-tuple-element.86.refs_5_), channel_id=1, source_target_pairs={{0,2},{1,3},{2,0},{3,1},{4,6},{5,7},{6,4},{7,5},{8,10},{9,11},{10,... | collective-permute-start | bytes 1572872 | tf_op jit(solution)/shard_map/ppermute | solution.py:566
  70.9 17.4 %collective-permute-start.22 = (f32[128,1024]{1,0:T(8,128)}, f32[128,1024]{1,0:T(8,128)}, u32[]{:S(2)}, u32[]{:S(2)}) collective-permute-start(f32[128,1024]{1,0:T(8,128)} %get-tuple-element.87.refs_7_), channel_id=1, source_target_pairs={{0,2},{1,3},{2,0},{3,1},{4,6},{5,7},{6,4},{7,5},{8,10},{9,11},{10,... | collective-permute-start | bytes 1572872 | tf_op jit(solution)/shard_map/ppermute | solution.py:566
  74.3 7.3 %copy-start.10 = (f32[128,1024]{1,0:T(8,128)}, f32[128,1024]{1,0:T(8,128)S(1)}, u32[]{:S(2)}) copy-start(f32[128,1024]{1,0:T(8,128)S(1)} %collective-permute-done.19.refs_1_) | copy-start | bytes 1572868
  74.3 20.6 %collective-permute-start.14 = (f32[128,1024]{1,0:T(8,128)}, f32[128,1024]{1,0:T(8,128)}, u32[]{:S(2)}, u32[]{:S(2)}) collective-permute-start(f32[128,1024]{1,0:T(8,128)} %get-tuple-element.82), channel_id=1, source_target_pairs={{0,4},{1,5},{2,6},{3,7},{4,0},{5,1},{6,2},{7,3},{8,12},{9,13},{10,... | collective-permute-start | bytes 1572872 | tf_op jit(solution)/shard_map/ppermute | solution.py:579
  75.7 19.2 %collective-permute-start.15 = (f32[128,1024]{1,0:T(8,128)}, f32[128,1024]{1,0:T(8,128)}, u32[]{:S(2)}, u32[]{:S(2)}) collective-permute-start(f32[128,1024]{1,0:T(8,128)} %get-tuple-element.83), channel_id=1, source_target_pairs={{0,1},{1,0},{2,3},{3,2},{4,5},{5,4},{6,7},{7,6},{8,9},{9,8},{10,11... | collective-permute-start | bytes 1572872 | tf_op jit(solution)/shard_map/ppermute | solution.py:579
  77.3 27.2 %collective-permute-start.16 = (f32[128,1024]{1,0:T(8,128)}, f32[128,1024]{1,0:T(8,128)}, u32[]{:S(2)}, u32[]{:S(2)}) collective-permute-start(f32[128,1024]{1,0:T(8,128)} %get-tuple-element.84), channel_id=1, source_target_pairs={{0,5},{1,4},{2,7},{3,6},{4,1},{5,0},{6,3},{7,2},{8,13},{9,12},{10,... | collective-permute-start | bytes 1572872 | tf_op jit(solution)/shard_map/ppermute | solution.py:579
  81.6 37.2 %all-to-all-start.3 = ((f32[8,16,1024]{2,1,0:T(8,128)}), f32[8,16,1024]{2,1,0:T(8,128)S(1)}, u32[]{:S(2)}, u32[]{:S(2)}) async-start(f32[8,16,1024]{2,1,0:T(8,128)} %bitcast.33), calls=%async_computation.3 | async-start | bytes 1048576 | tf_op jit(solution)/shard_map/all_to_all | solution.py:605
  88.3 16.2 %copy-start.11 = (f32[128,1024]{1,0:T(8,128)S(1)}, f32[128,1024]{1,0:T(8,128)}, u32[]{:S(2)}) copy-start(f32[128,1024]{1,0:T(8,128)} %get-tuple-element.81) | copy-start | bytes 1572868
  93.4 16.8 %copy-start.4 = (f32[8,16,512]{2,1,0:T(8,128)S(1)}, f32[8,16,512]{2,1,0:T(8,128)}, u32[]{:S(2)}) copy-start(f32[8,16,512]{2,1,0:T(8,128)} %copy-done.3) | copy-start | bytes 786436
  93.4 30.9 %collective-permute-start.23 = (f32[256,512]{1,0:T(8,128)}, f32[256,512]{1,0:T(8,128)S(1)}, u32[]{:S(2)}, u32[]{:S(2)}) collective-permute-start(f32[256,512]{1,0:T(8,128)} %get-tuple-element.89), channel_id=1, source_target_pairs={{0,1},{1,0},{2,3},{3,2},{4,5},{5,4},{6,7},{7,6},{8,9},{9,8},{10,11... | collective-permute-start | bytes 1572872 | tf_op jit(solution)/shard_map/ppermute | solution.py:566
  104.5 20.3 %copy-start.9 = (f32[256,512]{1,0:T(8,128)S(1)}, f32[256,512]{1,0:T(8,128)}, u32[]{:S(2)}) copy-start(f32[256,512]{1,0:T(8,128)} %get-tuple-element.88) | copy-start | bytes 1572868
  106.8 20.2 %copy-start.8 = (f32[256,640]{1,0:T(8,128)S(1)}, f32[256,640]{1,0:T(8,128)}, u32[]{:S(2)}) copy-start(f32[256,640]{1,0:T(8,128)} %get-tuple-element.90) | copy-start | bytes 1966084
  106.8 6.7 %collective-permute-start.17 = (f32[64,1024]{1,0:T(8,128)}, f32[64,1024]{1,0:T(8,128)}, u32[]{:S(2)}, u32[]{:S(2)}) collective-permute-start(f32[64,1024]{1,0:T(8,128)} %get-tuple-element.105), channel_id=1, source_target_pairs={{0,8},{1,9},{2,10},{3,11},{4,12},{5,13},{6,14},{7,15},{8,0},{9,1},... | collective-permute-start | bytes 786440 | tf_op jit(solution)/shard_map/ppermute | solution.py:566
  108.1 17.4 %collective-permute-start.25 = (f32[256,640]{1,0:T(8,128)}, f32[256,640]{1,0:T(8,128)S(1)}, u32[]{:S(2)}, u32[]{:S(2)}) collective-permute-start(f32[256,640]{1,0:T(8,128)} %get-tuple-element.91), channel_id=1, source_target_pairs={{0,4},{1,5},{2,6},{3,7},{4,0},{5,1},{6,2},{7,3},{8,12},{9,13},{10,... | collective-permute-start | bytes 1966088 | tf_op jit(solution)/shard_map/ppermute | solution.py:566
  110.2 17.6 %collective-permute-start.30 = (f32[128,512]{1,0:T(8,128)S(1)}, f32[128,512]{1,0:T(8,128)}, u32[]{:S(2)}, u32[]{:S(2)}) collective-permute-start(f32[128,512]{1,0:T(8,128)S(1)} %bitcast.28), channel_id=1, source_target_pairs={{0,2},{1,3},{2,0},{3,1},{4,6},{5,7},{6,4},{7,5},{8,10},{9,11},{10,... | collective-permute-start | bytes 786440 | tf_op jit(solution)/shard_map/ppermute | solution.py:566
  115.2 54.2 %collective-permute-start.18 = (f32[32,1024]{1,0:T(8,128)}, f32[32,1024]{1,0:T(8,128)}, u32[]{:S(2)}, u32[]{:S(2)}) collective-permute-start(f32[32,1024]{1,0:T(8,128)} %get-tuple-element.121), channel_id=1, source_target_pairs={{0,16},{1,17},{2,18},{3,19},{4,20},{5,21},{6,22},{7,23},{8,24},{9,... | collective-permute-start | bytes 393224 | tf_op jit(solution)/shard_map/ppermute | solution.py:566
  124.2 4.0 %collective-permute-start.29 = (f32[128,512]{1,0:T(8,128)}, f32[128,512]{1,0:T(8,128)}, u32[]{:S(2)}, u32[]{:S(2)}) collective-permute-start(f32[128,512]{1,0:T(8,128)} %get-tuple-element.92.refs_2_), channel_id=1, source_target_pairs={{0,2},{1,3},{2,0},{3,1},{4,6},{5,7},{6,4},{7,5},{8,10},{9,11},{10,... | collective-permute-start | bytes 786440 | tf_op jit(solution)/shard_map/ppermute | solution.py:566
  124.2 6.7 %collective-permute-start.2 = (f32[96,1024]{1,0:T(8,128)}, f32[96,1024]{1,0:T(8,128)S(1)}, u32[]{:S(2)}, u32[]{:S(2)}) collective-permute-start(f32[96,1024]{1,0:T(8,128)} %get-tuple-element.77), channel_id=1, source_target_pairs={{0,2},{1,3},{2,0},{3,1},{4,6},{5,7},{6,4},{7,5},{8,10},{9,11},{10,... | collective-permute-start | bytes 1179656 | tf_op jit(solution)/shard_map/ppermute | solution.py:566
  125.5 5.4 %copy-start.12 = (f32[96,1024]{1,0:T(8,128)S(1)}, f32[96,1024]{1,0:T(8,128)}, u32[]{:S(2)}) copy-start(f32[96,1024]{1,0:T(8,128)} %get-tuple-element.76) | copy-start | bytes 1179652
  125.5 9.4 %collective-permute-start.24 = (f32[128,512]{1,0:T(8,128)}, f32[128,512]{1,0:T(8,128)S(1)}, u32[]{:S(2)}, u32[]{:S(2)}) collective-permute-start(f32[128,512]{1,0:T(8,128)} %get-tuple-element.111), channel_id=1, source_target_pairs={{0,4},{1,5},{2,6},{3,7},{4,0},{5,1},{6,2},{7,3},{8,12},{9,13},{10,... | collective-permute-start | bytes 786440 | tf_op jit(solution)/shard_map/ppermute | solution.py:566
  127.7 15.3 %collective-permute-start.26 = (f32[128,640]{1,0:T(8,128)}, f32[128,640]{1,0:T(8,128)S(1)}, u32[]{:S(2)}, u32[]{:S(2)}) collective-permute-start(f32[128,640]{1,0:T(8,128)} %get-tuple-element.107), channel_id=1, source_target_pairs={{0,1},{1,0},{2,3},{3,2},{4,5},{5,4},{6,7},{7,6},{8,9},{9,8},{10,11... | collective-permute-start | bytes 983048 | tf_op jit(solution)/shard_map/ppermute | solution.py:566
  130.9 29.2 %copy-start.14 = (f32[128,512]{1,0:T(8,128)S(1)}, f32[128,512]{1,0:T(8,128)}, u32[]{:S(2)}) copy-start(f32[128,512]{1,0:T(8,128)} %get-tuple-element.93) | copy-start | bytes 786436
  131.0 5.5 %collective-permute-start.3 = (f32[24,1024]{1,0:T(8,128)S(1)}, f32[24,1024]{1,0:T(8,128)S(1)}, u32[]{:S(2)}, u32[]{:S(2)}) collective-permute-start(f32[24,1024]{1,0:T(8,128)S(1)} %get-tuple-element.112), channel_id=1, source_target_pairs={{0,4},{1,5},{2,6},{3,7},{4,0},{5,1},{6,2},{7,3},{8,12},{9,13},{10,... | collective-permute-start | bytes 294920 | tf_op jit(solution)/shard_map/ppermute | solution.py:579
  131.6 9.9 %collective-permute-start.4 = (f32[24,1024]{1,0:T(8,128)S(1)}, f32[24,1024]{1,0:T(8,128)S(1)}, u32[]{:S(2)}, u32[]{:S(2)}) collective-permute-start(f32[24,1024]{1,0:T(8,128)S(1)} %get-tuple-element.114), channel_id=1, source_target_pairs={{0,1},{1,0},{2,3},{3,2},{4,5},{5,4},{6,7},{7,6},{8,9},{9,8},{10,11... | collective-permute-start | bytes 294920 | tf_op jit(solution)/shard_map/ppermute | solution.py:579
  134.9 7.2 %collective-permute-start.5 = (f32[24,1024]{1,0:T(8,128)S(1)}, f32[24,1024]{1,0:T(8,128)S(1)}, u32[]{:S(2)}, u32[]{:S(2)}) collective-permute-start(f32[24,1024]{1,0:T(8,128)S(1)} %get-tuple-element.113), channel_id=1, source_target_pairs={{0,5},{1,4},{2,7},{3,6},{4,1},{5,0},{6,3},{7,2},{8,13},{9,12},{10,... | collective-permute-start | bytes 294920 | tf_op jit(solution)/shard_map/ppermute | solution.py:579
  136.5 20.1 %collective-permute-start.31 = (f32[128,512]{1,0:T(8,128)}, f32[128,512]{1,0:T(8,128)S(1)}, u32[]{:S(2)}, u32[]{:S(2)}) collective-permute-start(f32[128,512]{1,0:T(8,128)} %get-tuple-element.94), channel_id=1, source_target_pairs={{0,4},{1,5},{2,6},{3,7},{4,0},{5,1},{6,2},{7,3},{8,12},{9,13},{10,... | collective-permute-start | bytes 786440 | tf_op jit(solution)/shard_map/ppermute | solution.py:579
  141.6 16.2 %collective-permute-start.32 = (f32[128,512]{1,0:T(8,128)}, f32[128,512]{1,0:T(8,128)S(1)}, u32[]{:S(2)}, u32[]{:S(2)}) collective-permute-start(f32[128,512]{1,0:T(8,128)} %get-tuple-element.95), channel_id=1, source_target_pairs={{0,1},{1,0},{2,3},{3,2},{4,5},{5,4},{6,7},{7,6},{8,9},{9,8},{10,11... | collective-permute-start | bytes 786440 | tf_op jit(solution)/shard_map/ppermute | solution.py:579
  142.1 17.0 %collective-permute-start.33 = (f32[128,512]{1,0:T(8,128)}, f32[128,512]{1,0:T(8,128)S(1)}, u32[]{:S(2)}, u32[]{:S(2)}) collective-permute-start(f32[128,512]{1,0:T(8,128)} %get-tuple-element.96), channel_id=1, source_target_pairs={{0,5},{1,4},{2,7},{3,6},{4,1},{5,0},{6,3},{7,2},{8,13},{9,12},{10,... | collective-permute-start | bytes 786440 | tf_op jit(solution)/shard_map/ppermute | solution.py:579
  143.0 4.7 %collective-permute-start.6 = (f32[24,1024]{1,0:T(8,128)S(1)}, f32[24,1024]{1,0:T(8,128)S(1)}, u32[]{:S(2)}, u32[]{:S(2)}) collective-permute-start(f32[24,1024]{1,0:T(8,128)S(1)} %fusion.4), channel_id=1, source_target_pairs={{0,8},{1,9},{2,10},{3,11},{4,12},{5,13},{6,14},{7,15},{8,0},{9,1},... | collective-permute-start | bytes 294920 | tf_op jit(solution)/shard_map/ppermute | solution.py:566
  147.7 5.6 %collective-permute-start.7 = (f32[24,1024]{1,0:T(8,128)S(1)}, f32[24,1024]{1,0:T(8,128)S(1)}, u32[]{:S(2)}, u32[]{:S(2)}) collective-permute-start(f32[24,1024]{1,0:T(8,128)S(1)} %add.139), channel_id=1, source_target_pairs={{0,16},{1,17},{2,18},{3,19},{4,20},{5,21},{6,22},{7,23},{8,24},{9,... | collective-permute-start | bytes 294920 | tf_op jit(solution)/shard_map/ppermute | solution.py:566
  153.3 10.5 %collective-permute-start.27 = (f32[64,1152]{1,0:T(8,128)S(1)}, f32[64,1152]{1,0:T(8,128)S(1)}, u32[]{:S(2)}, u32[]{:S(2)}) collective-permute-start(f32[64,1152]{1,0:T(8,128)S(1)} %pad_maximum_fusion.1), channel_id=1, source_target_pairs={{0,8},{1,9},{2,10},{3,11},{4,12},{5,13},{6,14},{7,15},{8,0},{9,1},... | collective-permute-start | bytes 884744 | tf_op jit(solution)/shard_map/ppermute | solution.py:566
  156.6 5.6 %collective-permute-start.10 = (f32[24,1024]{1,0:T(8,128)S(1)}, f32[24,1024]{1,0:T(8,128)S(1)}, u32[]{:S(2)}, u32[]{:S(2)}) collective-permute-start(f32[24,1024]{1,0:T(8,128)S(1)} %add.140), channel_id=1, source_target_pairs={{0,5},{1,4},{2,7},{3,6},{4,1},{5,0},{6,3},{7,2},{8,13},{9,12},{10,... | collective-permute-start | bytes 294920 | tf_op jit(solution)/shard_map/ppermute | solution.py:579
  157.8 4.9 %collective-permute-start.8 = (f32[24,1024]{1,0:T(8,128)S(1)}, f32[24,1024]{1,0:T(8,128)S(1)}, u32[]{:S(2)}, u32[]{:S(2)}) collective-permute-start(f32[24,1024]{1,0:T(8,128)S(1)} %add.140), channel_id=1, source_target_pairs={{0,4},{1,5},{2,6},{3,7},{4,0},{5,1},{6,2},{7,3},{8,12},{9,13},{10,... | collective-permute-start | bytes 294920 | tf_op jit(solution)/shard_map/ppermute | solution.py:579
  159.1 4.6 %collective-permute-start.9 = (f32[24,1024]{1,0:T(8,128)S(1)}, f32[24,1024]{1,0:T(8,128)S(1)}, u32[]{:S(2)}, u32[]{:S(2)}) collective-permute-start(f32[24,1024]{1,0:T(8,128)S(1)} %add.140), channel_id=1, source_target_pairs={{0,1},{1,0},{2,3},{3,2},{4,5},{5,4},{6,7},{7,6},{8,9},{9,8},{10,11... | collective-permute-start | bytes 294920 | tf_op jit(solution)/shard_map/ppermute | solution.py:579
  162.2 5.0 %collective-permute-start.34 = (f32[64,512]{1,0:T(8,128)S(1)}, f32[64,512]{1,0:T(8,128)S(1)}, u32[]{:S(2)}, u32[]{:S(2)}) collective-permute-start(f32[64,512]{1,0:T(8,128)S(1)} %get-tuple-element.109), channel_id=1, source_target_pairs={{0,8},{1,9},{2,10},{3,11},{4,12},{5,13},{6,14},{7,15},{8,0},{9,1},... | collective-permute-start | bytes 393224 | tf_op jit(solution)/shard_map/ppermute | solution.py:566
  163.7 13.9 %copy-start.6 = (f32[96,1024]{1,0:T(8,128)}, f32[96,1024]{1,0:T(8,128)S(1)}, u32[]{:S(2)}) copy-start(f32[96,1024]{1,0:T(8,128)S(1)} %pad_maximum_fusion.near) | copy-start | bytes 1179652
  163.7 13.9 %collective-permute-start.11 = (f32[96,1024]{1,0:T(8,128)S(1)}, f32[96,1024]{1,0:T(8,128)S(1)}, u32[]{:S(2)}, u32[]{:S(2)}) collective-permute-start(f32[96,1024]{1,0:T(8,128)S(1)} %pad_maximum_fusion.near), channel_id=1, source_target_pairs={{0,2},{1,3},{2,0},{3,1},{4,6},{5,7},{6,4},{7,5},{8,10},{9,11},{10,... | collective-permute-start | bytes 1179656 | tf_op jit(solution)/shard_map/ppermute | solution.py:566
  164.5 13.1 %collective-permute-start.28 = (f32[32,1152]{1,0:T(8,128)S(1)}, f32[32,1152]{1,0:T(8,128)S(1)}, u32[]{:S(2)}, u32[]{:S(2)}) collective-permute-start(f32[32,1152]{1,0:T(8,128)S(1)} %get-tuple-element.117), channel_id=1, source_target_pairs={{0,16},{1,17},{2,18},{3,19},{4,20},{5,21},{6,22},{7,23},{8,24},{9,... | collective-permute-start | bytes 442376 | tf_op jit(solution)/shard_map/ppermute | solution.py:566
  167.8 9.8 %collective-permute-start.35 = (f32[32,512]{1,0:T(8,128)S(1)}, f32[32,512]{1,0:T(8,128)S(1)}, u32[]{:S(2)}, u32[]{:S(2)}) collective-permute-start(f32[32,512]{1,0:T(8,128)S(1)} %get-tuple-element.123), channel_id=1, source_target_pairs={{0,16},{1,17},{2,18},{3,19},{4,20},{5,21},{6,22},{7,23},{8,24},{9,... | collective-permute-start | bytes 196616 | tf_op jit(solution)/shard_map/ppermute | solution.py:566
  (10 other events, 12.5 us)
